TPU v7x, 8 devices: a whole 2x2x1 slice. The times are simulated.
8 devices in a mesh: col: 2 (over z, y), row: 4 (over x, core).
Axes of the slice: x: 2, y: 2, z: 1, core: 2. Of those that a mesh axis runs over, the one named last changes fastest.
Arguments:
- vel_x: float32 [20, 2, 512, 512], P(None, None, 'row', 'col')
- vel_y: float32 [20, 2, 512, 512], P(None, None, 'row', 'col')
- pot_temp: float32 [20, 2, 512, 512], P(None, None, 'row', 'col')
- salinity: float32 [20, 2, 512, 512], P(None, None, 'row', 'col')
- surf_eta: float32 [2, 512, 512], P(None, 'row', 'col')
- trans_x: float32 [2, 512, 512], P(None, 'row', 'col')
- trans_y: float32 [2, 512, 512], P(None, 'row', 'col')
- col_depth: float32 [512, 512], P('row', 'col')
- wet_levels: int32 [512, 512], P('row', 'col')
- avg_weights: float32 [20], replicated
Outputs:
- output 1: float32 [2, 512, 512], P(None, 'row', 'col')
- output 2: float32 [2, 512, 512], P(None, 'row', 'col')
- output 3: float32 [2, 512, 512], P(None, 'row', 'col')
- output 4: float32 [20, 2, 512, 512], P(None, None, 'row', 'col')
- output 5: float32 [20, 2, 512, 512], P(None, None, 'row', 'col')
- output 6: float32 [20, 2, 512, 512], P(None, None, 'row', 'col')
- output 7: float32 [20, 2, 512, 512], P(None, None, 'row', 'col')
All inputs are finite; a program needn't handle non-finite values.
Results may differ from a plain program's by a relative error of at most 0.001.
Values sent between devices are 32-bit elements.
A program may use at most 1 GiB of HBM per device.

v0:
```python
import functools
import jax
import jax.numpy as jnp
from jax import lax
from jax.sharding import PartitionSpec as P

WAVE_COURANT = 0.4
THERM_EXP = 0.2
HALINE_CON = 0.15
PRESS_SCALE = 0.5
VISC_NUMBER = 1.0
DIFF_NUMBER = 0.5


def take_east(field_in, col_count):
    edge_slab = field_in[..., :1]
    received = lax.ppermute(edge_slab, "col", [(source, (source - 1) % col_count) for source in range(col_count)])
    return jnp.concatenate([field_in[..., 1:], received], axis=-1)


def take_west(field_in, col_count):
    edge_slab = field_in[..., -1:]
    received = lax.ppermute(edge_slab, "col", [(source, (source + 1) % col_count) for source in range(col_count)])
    return jnp.concatenate([received, field_in[..., :-1]], axis=-1)


def take_north(field_in, row_count):
    edge_slab = field_in[..., :1, :]
    received = lax.ppermute(edge_slab, "row", [(source, source - 1) for source in range(1, row_count)])
    return jnp.concatenate([field_in[..., 1:, :], received], axis=-2)


def take_south(field_in, row_count):
    edge_slab = field_in[..., -1:, :]
    received = lax.ppermute(edge_slab, "row", [(source, source + 1) for source in range(row_count - 1)])
    return jnp.concatenate([received, field_in[..., :-1, :]], axis=-2)


def vertical_solve(right_side, face_mask, strength):
    mask_below = jnp.concatenate([face_mask[1:], jnp.zeros_like(face_mask[:1])], axis=0)
    face_up = face_mask * mask_below
    face_down = jnp.concatenate([jnp.zeros_like(face_up[:1]), face_up[:-1]], axis=0)
    lower_diag = -strength * face_down
    upper_diag = -strength * face_up
    main_diag = 1.0 + strength * (face_down + face_up)

    def forward(state_prev, level_row):
        upper_prev, side_prev = state_prev
        low_k, diag_k, up_k, side_k = level_row
        divisor = diag_k - low_k * upper_prev
        upper_new = up_k / divisor
        side_new = (side_k - low_k * side_prev) / divisor
        return (upper_new, side_new), (upper_new, side_new)

    zero_level = jnp.zeros_like(right_side[0])
    upper_all, side_all = lax.scan(forward, (zero_level, zero_level), (lower_diag, main_diag, upper_diag, right_side))[1]

    def backward(sol_next, level_row):
        up_k, side_k = level_row
        sol_k = side_k - up_k * sol_next
        return sol_k, sol_k

    return lax.scan(backward, zero_level, (upper_all, side_all), reverse=True)[1]


def three_d_step(vel_x, vel_y, pot_temp, salinity, col_depth, wet_levels, shift_east, shift_west, shift_north, shift_south):
    level_count = vel_x.shape[0]
    levels = jnp.arange(level_count).reshape(level_count, 1, 1, 1)
    cell_mask = (levels < wet_levels).astype(jnp.float32)
    xface_mask = cell_mask * (levels < shift_east(wet_levels)).astype(jnp.float32)
    yface_mask = cell_mask * (levels < shift_north(wet_levels)).astype(jnp.float32)
    density = HALINE_CON * salinity - THERM_EXP * pot_temp
    pressure = (PRESS_SCALE / level_count) * (jnp.cumsum(density, axis=0) - 0.5 * density)
    vy_south = shift_south(vel_y)
    vx_north = shift_north(vel_x)
    vy_at_x = 0.25 * (vel_y + vy_south + shift_east(vel_y) + shift_east(vy_south))
    vx_at_y = 0.25 * (vel_x + shift_west(vel_x) + vx_north + shift_west(vx_north))
    tend_x = xface_mask * (pressure - shift_east(pressure) - 0.5 * vel_x * (shift_east(vel_x) - shift_west(vel_x)) - 0.5 * vy_at_x * (vx_north - shift_south(vel_x)))
    tend_y = yface_mask * (pressure - shift_north(pressure) - 0.5 * vx_at_y * (shift_east(vel_y) - shift_west(vel_y)) - 0.5 * vel_y * (shift_north(vel_y) - vy_south))
    count_x = jnp.maximum(jnp.sum(xface_mask, axis=0), 1.0)
    count_y = jnp.maximum(jnp.sum(yface_mask, axis=0), 1.0)
    depth_x = 0.5 * (col_depth + shift_east(col_depth)) * xface_mask[0]
    depth_y = 0.5 * (col_depth + shift_north(col_depth)) * yface_mask[0]
    force_x = depth_x * jnp.sum(tend_x, axis=0) / count_x
    force_y = depth_y * jnp.sum(tend_y, axis=0) / count_y
    pred_x = vertical_solve(vel_x + tend_x, xface_mask, VISC_NUMBER)
    pred_y = vertical_solve(vel_y + tend_y, yface_mask, VISC_NUMBER)
    dev_x = pred_x - jnp.sum(pred_x, axis=0) / count_x
    dev_y = pred_y - jnp.sum(pred_y, axis=0) / count_y

    def tracer_step(tracer):
        flux_x = vel_x * 0.5 * (tracer + shift_east(tracer))
        flux_y = vel_y * 0.5 * (tracer + shift_north(tracer))
        advected = cell_mask * (tracer - (flux_x - shift_west(flux_x) + flux_y - shift_south(flux_y)))
        return vertical_solve(advected, cell_mask, DIFF_NUMBER)

    return cell_mask[0], xface_mask, yface_mask, depth_x, depth_y, force_x, force_y, dev_x, dev_y, tracer_step(pot_temp), tracer_step(salinity)


def barotropic(surf_eta, trans_x, trans_y, force_x, force_y, depth_x, depth_y, wet_top, xface_top, yface_top, avg_weights, shift_east, shift_west, shift_north, shift_south):
    sub_count = avg_weights.shape[0]
    step_x = force_x / sub_count
    step_y = force_y / sub_count

    def subcycle(sub_state, weight):
        eta_now, tx_now, ty_now, eta_avg, tx_avg, ty_avg = sub_state
        eta_now = wet_top * (eta_now - WAVE_COURANT * (tx_now - shift_west(tx_now) + ty_now - shift_south(ty_now)))
        tx_now = xface_top * (tx_now + step_x - WAVE_COURANT * depth_x * (shift_east(eta_now) - eta_now))
        ty_now = yface_top * (ty_now + step_y - WAVE_COURANT * depth_y * (shift_north(eta_now) - eta_now))
        return (eta_now, tx_now, ty_now, eta_avg + weight * eta_now, tx_avg + weight * tx_now, ty_avg + weight * ty_now), None

    zero_field = jnp.zeros_like(surf_eta)
    end_state = lax.scan(subcycle, (surf_eta, trans_x, trans_y, zero_field, zero_field, zero_field), avg_weights)[0]
    return end_state[3], end_state[4], end_state[5]


def solution(mesh):
    col_count = mesh.shape["col"]
    row_count = mesh.shape["row"]
    shift_east = functools.partial(take_east, col_count=col_count)
    shift_west = functools.partial(take_west, col_count=col_count)
    shift_north = functools.partial(take_north, row_count=row_count)
    shift_south = functools.partial(take_south, row_count=row_count)

    def local_step(vel_x, vel_y, pot_temp, salinity, surf_eta, trans_x, trans_y, col_depth, wet_levels, avg_weights):
        wet_top, xface_mask, yface_mask, depth_x, depth_y, force_x, force_y, dev_x, dev_y, temp_new, salt_new = three_d_step(vel_x, vel_y, pot_temp, salinity, col_depth, wet_levels, shift_east, shift_west, shift_north, shift_south)
        eta_new, trans_x_new, trans_y_new = barotropic(surf_eta, trans_x, trans_y, force_x, force_y, depth_x, depth_y, wet_top, xface_mask[0], yface_mask[0], avg_weights, shift_east, shift_west, shift_north, shift_south)
        vel_x_new = xface_mask * (dev_x + trans_x_new / (depth_x + 1.0 - xface_mask[0]))
        vel_y_new = yface_mask * (dev_y + trans_y_new / (depth_y + 1.0 - yface_mask[0]))
        return eta_new, trans_x_new, trans_y_new, vel_x_new, vel_y_new, temp_new, salt_new

    spec_3d = P(None, None, "row", "col")
    spec_2d = P(None, "row", "col")
    spec_map = P("row", "col")
    spec_weights = P()
    return jax.shard_map(local_step, mesh=mesh, in_specs=(spec_3d, spec_3d, spec_3d, spec_3d, spec_2d, spec_2d, spec_2d, spec_map, spec_map, spec_weights), out_specs=(spec_2d, spec_2d, spec_2d, spec_3d, spec_3d, spec_3d, spec_3d), check_vma=False)
```

profile of v0, /device:TPU:0, one launch (start us, length us, event | category | flops | bytes accessed | tf_op | source)
XLA Modules:
  0.0 1271.6 jit_solution(9829297922683298661)
XLA Ops:
  10.5 4.9 fusion.96
  16.8 9.9 fusion.97
  28.2 11.4 subtract_multiply_fusion
  39.6 5.4 slice.283
  46.7 9.1 fusion.92
  55.8 5.1 fusion.93
  72.3 6.3 slice.276
  123.8 6.1 multiply_add_fusion
  175.9 5.9 fusion.27
  192.9 8.2 collective-permute-start.13
  201.4 22.7 %fusion.47 = (f32[20,2,128,256]{3,2,1,0:T(8,128)}, f32[20,2,128,256]{3,2,1,0:T(8,128)}, f32[20,2,128,256]{3,2,1,0:T(8,128)}, f32[20,2,128,256]{3,2,1,0:T(8,128)}) fusion(f32[20,2,128,256]{3,2,1,0:T(8,128)} %param.31, f32[20,2,128,1]{3,2,1,0:T(8,128)} %copy.36, f32[20,2,128,255]{3,2,1,0:T(8,128)} %slice.254, f32[20,2,128,256]{3,2,1,0:T(8,128)} %param.28, ...), kind=kLoop, calls=%fused_computation.115 | loop fusion | flops 18350080 | bytes 62914560 | tf_op jit(solution)/shard_map/mul | solution.py:92
  246.2 26.5 %fusion.86 = (f32[20,2,128,256]{3,2,1,0:T(8,128)}, f32[20,2,128,256]{3,2,1,0:T(8,128)}) fusion(f32[20,2,128,256]{3,2,1,0:T(8,128)} %param.29, f32[20,2,127,256]{3,2,1,0:T(8,128)} %get-tuple-element.1160, f32[20,2,1,256]{3,2,1,0:T(1,128)S(1)} %collective-permute-done.9, f32[20,2,1,256]{3,2,1,0:T(1,128)S(1)} %collective-permute-done.19, ...), kind=kLoop, calls=%fused_computation.181 | loop fusion | flops 28835840 | bytes 70778880 | tf_op jit(solution)/shard_map/add | solution.py:87
  278.7 77.1 %while.160 = (s32[]{:T(128)}, f32[2,128,256]{2,1,0:T(8,128)S(1)}, f32[2,128,256]{2,1,0:T(8,128)S(1)}, f32[20,2,128,256]{3,2,1,0:T(8,128)}, f32[20,2,128,256]{3,2...) while((s32[]{:T(128)}, f32[2,128,256]{2,1,0:T(8,128)S(1)}, ...), condition=%wide.region_13.14_spmd.clone, body=%wide.region_12.13_spmd.clone.sunk | while | flops 524291 | bytes 3015295 | solution.py:56
  358.8 39.1 %while.161 = (s32[]{:T(128)}, f32[2,128,256]{2,1,0:T(8,128)S(1)}, f32[20,2,128,256]{3,2,1,0:T(8,128)}, f32[20,2,128,256]{3,2,1,0:T(8,128)}, f32[20,2,128,256]{3,...) while((s32[]{:T(128)}, f32[2,128,256]{2,1,0:T(8,128)S(1)}, f32[20,2,128,256]{3,2,1,0:T(8,128)}, ...), condition=%wide.region_15.16_spmd.clone, body=%wide.region_14.15_spmd.clone.sunk | while | flops 196612 | bytes 1310831 | solution.py:63
  403.7 27.5 %fusion.89 = (f32[20,2,128,256]{3,2,1,0:T(8,128)}, f32[20,2,128,256]{3,2,1,0:T(8,128)}) fusion(f32[20,2,128,256]{3,2,1,0:T(8,128)} %param.28, f32[20,2,127,256]{3,2,1,0:T(8,128)} %get-tuple-element.1168, f32[20,2,1,256]{3,2,1,0:T(1,128)} %collective-permute-done.13, f32[20,2,1,256]{3,2,1,0:T(1,128)} %collective-permute-done.12, ...), kind=kLoop, calls=%fused_computation.182 | loop fusion | flops 28835840 | bytes 70778880 | tf_op jit(solution)/shard_map/add | solution.py:86
  437.2 77.1 %while.158 = (s32[]{:T(128)}, f32[2,128,256]{2,1,0:T(8,128)S(1)}, f32[2,128,256]{2,1,0:T(8,128)S(1)}, f32[20,2,128,256]{3,2,1,0:T(8,128)}, f32[20,2,128,256]{3,2...) while((s32[]{:T(128)}, f32[2,128,256]{2,1,0:T(8,128)S(1)}, ...), condition=%wide.region_8.9_spmd.clone, body=%wide.region_7.8_spmd.clone.sunk | while | flops 524291 | bytes 3015295 | solution.py:56
  517.3 39.0 %while.159 = (s32[]{:T(128)}, f32[2,128,256]{2,1,0:T(8,128)S(1)}, f32[20,2,128,256]{3,2,1,0:T(8,128)}, f32[20,2,128,256]{3,2,1,0:T(8,128)}, f32[20,2,128,256]{3,...) while((s32[]{:T(128)}, f32[2,128,256]{2,1,0:T(8,128)S(1)}, f32[20,2,128,256]{3,2,1,0:T(8,128)}, ...), condition=%wide.region_10.11_spmd.clone, body=%wide.region_9.10_spmd.clone.sunk | while | flops 196612 | bytes 1310831 | solution.py:63
  569.7 404.2 %while.157 = (s32[]{:T(128)}, f32[2,128,256]{2,1,0:T(8,128)S(1)}, f32[2,128,256]{2,1,0:T(8,128)S(1)}, f32[2,128,256]{2,1,0:T(8,128)S(1)}, f32[2,128,256]{2,1,0:T...) while((s32[]{:T(128)}, f32[2,128,256]{2,1,0:T(8,128)S(1)}, ...), condition=%wide.region_6.7_spmd.clone, body=%wide.region_5.6_spmd.clone.sunk | while | flops 1966083 | bytes 7764316 | solution.py:113
  613.7 4.7 collective-permute-done.1
  653.7 4.7 collective-permute-done.1
  694.2 4.7 collective-permute-done.1
  734.9 4.7 collective-permute-done.1
  816.2 4.7 collective-permute-done.1
  856.9 4.7 collective-permute-done.1
  897.5 4.7 collective-permute-done.1
  978.1 6.0 add_multiply_fusion
  984.2 5.8 add_multiply_fusion.1
  996.3 24.5 %fusion.51 = (f32[20,2,128,256]{3,2,1,0:T(8,128)}, f32[20,2,128,256]{3,2,1,0:T(8,128)}) fusion(f32[20,2,128,256]{3,2,1,0:T(8,128)} %param.31, f32[20,2,128,256]{3,2,1,0:T(8,128)} %get-tuple-element.1154, f32[20,2,128,256]{3,2,1,0:T(8,128)} %get-tuple-element.1151, f32[20,2,128,255]{3,2,1,0:T(8,128)} %bitcast.192, f32[20,2,128,1]{3,2,1,0:T(8,128)} %copy.38, ...), kind=kLoop, calls=%fused_computation.120 | loop fusion | flops 18350080 | bytes 65536000 | tf_op jit(solution)/shard_map/mul | solution.py:94
  1026.7 77.2 %while.164 = (s32[]{:T(128)}, f32[2,128,256]{2,1,0:T(8,128)S(1)}, f32[2,128,256]{2,1,0:T(8,128)S(1)}, f32[20,2,128,256]{3,2,1,0:T(8,128)}, f32[20,2,128,256]{3,2...) while((s32[]{:T(128)}, f32[2,128,256]{2,1,0:T(8,128)S(1)}, ...), condition=%wide.region_22.23_spmd.clone, body=%wide.region_21.22_spmd.clone.sunk | while | flops 524291 | bytes 3015295 | solution.py:56
  1106.9 39.0 %while.165 = (s32[]{:T(128)}, f32[2,128,256]{2,1,0:T(8,128)S(1)}, f32[20,2,128,256]{3,2,1,0:T(8,128)}, f32[20,2,128,256]{3,2,1,0:T(8,128)}, f32[20,2,128,256]{3,...) while((s32[]{:T(128)}, f32[2,128,256]{2,1,0:T(8,128)S(1)}, f32[20,2,128,256]{3,2,1,0:T(8,128)}, ...), condition=%wide.region_24.25_spmd.clone, body=%wide.region_23.24_spmd.clone.sunk | while | flops 196612 | bytes 1310831 | solution.py:63
  1151.7 77.4 %while.162 = (s32[]{:T(128)}, f32[2,128,256]{2,1,0:T(8,128)S(1)}, f32[2,128,256]{2,1,0:T(8,128)S(1)}, f32[20,2,128,256]{3,2,1,0:T(8,128)}, f32[20,2,128,256]{3,2...) while((s32[]{:T(128)}, f32[2,128,256]{2,1,0:T(8,128)S(1)}, ...), condition=%wide.region_18.19_spmd.clone, body=%wide.region_17.18_spmd.clone.sunk | while | flops 524291 | bytes 3015295 | solution.py:56
  1232.1 39.0 %while.163 = (s32[]{:T(128)}, f32[2,128,256]{2,1,0:T(8,128)S(1)}, f32[20,2,128,256]{3,2,1,0:T(8,128)}, f32[20,2,128,256]{3,2,1,0:T(8,128)}, f32[20,2,128,256]{3,...) while((s32[]{:T(128)}, f32[2,128,256]{2,1,0:T(8,128)S(1)}, f32[20,2,128,256]{3,2,1,0:T(8,128)}, ...), condition=%wide.region_20.21_spmd.clone, body=%wide.region_19.20_spmd.clone.sunk | while | flops 196612 | bytes 1310831 | solution.py:63
  (959 shorter events, 1049.9 us)
Async XLA Ops:
  2.4 173.4 %collective-permute-start.12 = (f32[20,2,1,256]{3,2,1,0:T(1,128)}, f32[20,2,1,256]{3,2,1,0:T(1,128)}, u32[]{:S(2)}, u32[]{:S(2)}) collective-permute-start(f32[20,2,1,256]{3,2,1,0:T(1,128)} %get-tuple-element.1169), channel_id=1, source_target_pairs={{1,0},{2,1},{3,2},{5,4},{6,5},{7,6}} | collective-permute-start | bytes 122888 | tf_op jit(solution)/shard_map/ppermute | solution.py:29
  5.2 116.2 %collective-permute-start.4 = (s32[128,1]{1,0:T(8,128)}, s32[128,1]{1,0:T(8,128)}, u32[]{:S(2)}, u32[]{:S(2)}) collective-permute-start(s32[128,1]{1,0:T(8,128)} %slice.207), channel_id=1, source_target_pairs={{0,4},{4,0},{1,5},{5,1},{2,6},{6,2},{3,7},{7,3}} | collective-permute-start | bytes 1544 | tf_op jit(solution)/shard_map/ppermute | solution.py:17
  9.2 114.5 %collective-permute-start.14 = (s32[1,256]{1,0:T(1,128)S(1)}, s32[1,256]{1,0:T(1,128)S(1)}, u32[]{:S(2)}, u32[]{:S(2)}) collective-permute-start(s32[1,256]{1,0:T(1,128)S(1)} %slice.228), channel_id=1, source_target_pairs={{1,0},{2,1},{3,2},{5,4},{6,5},{7,6}} | collective-permute-start | bytes 3080 | tf_op jit(solution)/shard_map/ppermute | solution.py:29
  16.8 130.5 %collective-permute-start.8 = (f32[20,2,128,1]{2,1,3,0:T(2,128)}, f32[20,2,128,1]{2,1,3,0:T(2,128)}, u32[]{:S(2)}, u32[]{:S(2)}) collective-permute-start(f32[20,2,128,1]{2,1,3,0:T(2,128)} %copy.40), channel_id=1, source_target_pairs={{0,4},{4,0},{1,5},{5,1},{2,6},{6,2},{3,7},{7,3}} | collective-permute-start | bytes 61448 | tf_op jit(solution)/shard_map/ppermute | solution.py:23
  119.3 24.4 %collective-permute-start.5 = (f32[128,1]{1,0:T(8,128)S(1)}, f32[128,1]{1,0:T(8,128)S(1)}, u32[]{:S(2)}, u32[]{:S(2)}) collective-permute-start(f32[128,1]{1,0:T(8,128)S(1)} %copy-done.40), channel_id=1, source_target_pairs={{0,4},{4,0},{1,5},{5,1},{2,6},{6,2},{3,7},{7,3}} | collective-permute-start | bytes 1544 | tf_op jit(solution)/shard_map/ppermute | solution.py:17
  122.3 23.5 %collective-permute-start.15 = (f32[1,256]{1,0:T(1,128)S(1)}, f32[1,256]{1,0:T(1,128)S(1)}, u32[]{:S(2)}, u32[]{:S(2)}) collective-permute-start(f32[1,256]{1,0:T(1,128)S(1)} %slice.231), channel_id=1, source_target_pairs={{1,0},{2,1},{3,2},{5,4},{6,5},{7,6}} | collective-permute-start | bytes 3080 | tf_op jit(solution)/shard_map/ppermute | solution.py:29
  147.3 12.4 collective-permute-start.6
  147.3 15.9 %collective-permute-start.7 = (f32[20,2,128,1]{2,1,3,0:T(2,128)S(1)}, f32[20,2,128,1]{2,1,3,0:T(2,128)S(1)}, u32[]{:S(2)}, u32[]{:S(2)}) collective-permute-start(f32[20,2,128,1]{2,1,3,0:T(2,128)S(1)} %copy.39), channel_id=1, source_target_pairs={{0,4},{4,0},{1,5},{5,1},{2,6},{6,2},{3,7},{7,3}} | collective-permute-start | bytes 61448 | tf_op jit(solution)/shard_map/ppermute | solution.py:17
  149.3 19.2 %collective-permute-start.20 = (f32[20,2,128,1]{2,1,3,0:T(2,128)S(1)}, f32[20,2,128,1]{2,1,3,0:T(2,128)S(1)}, u32[]{:S(2)}, u32[]{:S(2)}) collective-permute-start(f32[20,2,128,1]{2,1,3,0:T(2,128)S(1)} %copy.43), channel_id=1, source_target_pairs={{0,4},{4,0},{1,5},{5,1},{2,6},{6,2},{3,7},{7,3}} | collective-permute-start | bytes 61448 | tf_op jit(solution)/shard_map/ppermute | solution.py:17
  149.4 22.9 %collective-permute-start.24 = (f32[20,2,128,1]{2,1,3,0:T(2,128)S(1)}, f32[20,2,128,1]{2,1,3,0:T(2,128)S(1)}, u32[]{:S(2)}, u32[]{:S(2)}) collective-permute-start(f32[20,2,128,1]{2,1,3,0:T(2,128)S(1)} %copy.44), channel_id=1, source_target_pairs={{0,4},{4,0},{1,5},{5,1},{2,6},{6,2},{3,7},{7,3}} | collective-permute-start | bytes 61448 | tf_op jit(solution)/shard_map/ppermute | solution.py:17
  161.9 82.5 %collective-permute-start.16 = (f32[20,2,1,256]{3,2,1,0:T(1,128)S(1)}, f32[20,2,1,256]{3,2,1,0:T(1,128)S(1)}, u32[]{:S(2)}, u32[]{:S(2)}) collective-permute-start(f32[20,2,1,256]{3,2,1,0:T(1,128)S(1)} %copy-done.43), channel_id=1, source_target_pairs={{1,0},{2,1},{3,2},{5,4},{6,5},{7,6}} | collective-permute-start | bytes 122888 | tf_op jit(solution)/shard_map/ppermute | solution.py:29
  165.5 17.7 %collective-permute-start.9 = (f32[20,2,1,256]{3,2,1,0:T(1,128)S(1)}, f32[20,2,1,256]{3,2,1,0:T(1,128)S(1)}, u32[]{:S(2)}, u32[]{:S(2)}) collective-permute-start(f32[20,2,1,256]{3,2,1,0:T(1,128)S(1)} %copy-done.42), channel_id=1, source_target_pairs={{0,1},{1,2},{2,3},{4,5},{5,6},{6,7}} | collective-permute-start | bytes 122888 | tf_op jit(solution)/shard_map/ppermute | solution.py:35
  170.9 75.3 %collective-permute-start.19 = (f32[20,2,1,256]{3,2,1,0:T(1,128)S(1)}, f32[20,2,1,256]{3,2,1,0:T(1,128)S(1)}, u32[]{:S(2)}, u32[]{:S(2)}) collective-permute-start(f32[20,2,1,256]{3,2,1,0:T(1,128)S(1)} %copy-done.41), channel_id=1, source_target_pairs={{1,0},{2,1},{3,2},{5,4},{6,5},{7,6}} | collective-permute-start | bytes 122888 | tf_op jit(solution)/shard_map/ppermute | solution.py:29
  174.5 26.6 %collective-permute-start.22 = (f32[20,2,1,256]{3,2,1,0:T(1,128)S(1)}, f32[20,2,1,256]{3,2,1,0:T(1,128)S(1)}, u32[]{:S(2)}, u32[]{:S(2)}) collective-permute-start(f32[20,2,1,256]{3,2,1,0:T(1,128)S(1)} %copy-done.45), channel_id=1, source_target_pairs={{1,0},{2,1},{3,2},{5,4},{6,5},{7,6}} | collective-permute-start | bytes 122888 | tf_op jit(solution)/shard_map/ppermute | solution.py:29
  181.8 19.6 %collective-permute-start.26 = (f32[20,2,1,256]{3,2,1,0:T(1,128)S(1)}, f32[20,2,1,256]{3,2,1,0:T(1,128)S(1)}, u32[]{:S(2)}, u32[]{:S(2)}) collective-permute-start(f32[20,2,1,256]{3,2,1,0:T(1,128)S(1)} %copy-done.44), channel_id=1, source_target_pairs={{1,0},{2,1},{3,2},{5,4},{6,5},{7,6}} | collective-permute-start | bytes 122888 | tf_op jit(solution)/shard_map/ppermute | solution.py:29
  192.9 210.8 %collective-permute-start.13 = (f32[20,2,1,256]{3,2,1,0:T(1,128)}, f32[20,2,1,256]{3,2,1,0:T(1,128)}, u32[]{:S(2)}, u32[]{:S(2)}) collective-permute-start(f32[20,2,1,256]{3,2,1,0:T(1,128)} %get-tuple-element.1170), channel_id=1, source_target_pairs={{0,1},{1,2},{2,3},{4,5},{5,6},{6,7}} | collective-permute-start | bytes 122888 | tf_op jit(solution)/shard_map/ppermute | solution.py:35
  201.1 40.8 %collective-permute-start.17 = (f32[20,2,128,1]{2,1,3,0:T(2,128)S(1)}, f32[20,2,128,1]{2,1,3,0:T(2,128)S(1)}, u32[]{:S(2)}, u32[]{:S(2)}) collective-permute-start(f32[20,2,128,1]{2,1,3,0:T(2,128)S(1)} %copy.27), channel_id=1, source_target_pairs={{0,4},{4,0},{1,5},{5,1},{2,6},{6,2},{3,7},{7,3}} | collective-permute-start | bytes 61448 | tf_op jit(solution)/shard_map/ppermute | solution.py:23
  240.2 160.5 %collective-permute-start.11 = (f32[20,2,128,1]{2,1,3,0:T(2,128)}, f32[20,2,128,1]{2,1,3,0:T(2,128)}, u32[]{:S(2)}, u32[]{:S(2)}) collective-permute-start(f32[20,2,128,1]{2,1,3,0:T(2,128)} %copy.25), channel_id=1, source_target_pairs={{0,4},{4,0},{1,5},{5,1},{2,6},{6,2},{3,7},{7,3}} | collective-permute-start | bytes 61448 | tf_op jit(solution)/shard_map/ppermute | solution.py:17
  244.2 745.9 %collective-permute-start.21 = (f32[20,2,128,1]{2,1,3,0:T(2,128)}, f32[20,2,128,1]{2,1,3,0:T(2,128)}, u32[]{:S(2)}, u32[]{:S(2)}) collective-permute-start(f32[20,2,128,1]{2,1,3,0:T(2,128)} %copy.33), channel_id=1, source_target_pairs={{0,4},{4,0},{1,5},{5,1},{2,6},{6,2},{3,7},{7,3}} | collective-permute-start | bytes 61448 | tf_op jit(solution)/shard_map/ppermute | solution.py:23
  244.5 748.8 %collective-permute-start.25 = (f32[20,2,128,1]{2,1,3,0:T(2,128)}, f32[20,2,128,1]{2,1,3,0:T(2,128)}, u32[]{:S(2)}, u32[]{:S(2)}) collective-permute-start(f32[20,2,128,1]{2,1,3,0:T(2,128)} %copy.37), channel_id=1, source_target_pairs={{0,4},{4,0},{1,5},{5,1},{2,6},{6,2},{3,7},{7,3}} | collective-permute-start | bytes 61448 | tf_op jit(solution)/shard_map/ppermute | solution.py:23
  397.9 598.4 %collective-permute-start.23 = (f32[20,2,1,256]{3,2,1,0:T(1,128)}, f32[20,2,1,256]{3,2,1,0:T(1,128)}, u32[]{:S(2)}, u32[]{:S(2)}) collective-permute-start(f32[20,2,1,256]{3,2,1,0:T(1,128)} %slice.297), channel_id=1, source_target_pairs={{0,1},{1,2},{2,3},{4,5},{5,6},{6,7}} | collective-permute-start | bytes 122888 | tf_op jit(solution)/shard_map/ppermute | solution.py:35
  569.7 9.3 collective-permute-start
  609.0 9.3 collective-permute-start
  648.9 9.5 collective-permute-start
  689.3 9.6 collective-permute-start
  729.9 9.6 collective-permute-start
  770.6 9.6 collective-permute-start
  811.3 9.6 collective-permute-start
  851.9 9.6 collective-permute-start
  892.6 9.6 collective-permute-start
  933.2 9.6 collective-permute-start
  973.9 22.4 %collective-permute-start.27 = (f32[20,2,1,256]{3,2,1,0:T(1,128)}, f32[20,2,1,256]{3,2,1,0:T(1,128)S(1)}, u32[]{:S(2)}, u32[]{:S(2)}) collective-permute-start(f32[20,2,1,256]{3,2,1,0:T(1,128)} %slice.301), channel_id=1, source_target_pairs={{0,1},{1,2},{2,3},{4,5},{5,6},{6,7}} | collective-permute-start | bytes 122888 | tf_op jit(solution)/shard_map/ppermute | solution.py:35
  (136 other events, 1444.2 us)
where the time goes:
time: 1290 us; the launch traced here: 1270 us
  other arithmetic  635 us (49%)
  local copies, waits for them, and re-layouts  378 us (29%)
  starting transfers between devices  154 us (12%)
  waiting for transfers between devices  102 us (8%)
    dynamic_update_slice x160, other arithmetic, vertical_solve(): lax.scan(forward, (zero_level, zero_level), (lower_diag, main_diag, upper...  312 us
    ppermute x25, waiting for transfers between devices, take_west(): lax.ppermute(edge_slab, 'col', [(source, (source + 1) % col_count) for so...  81.7 us
    mul x80, local copies, waits for them, and re-layouts, forward(): divisor = diag_k - low_k * upper_prev  78.9 us
    div x80, local copies, waits for them, and re-layouts, forward(): upper_new = up_k / divisor  73.6 us
    ppermute x24, starting transfers between devices, take_south(): lax.ppermute(edge_slab, 'row', [(source, source + 1) for source in range(...  63.3 us
    add x20, other arithmetic, subcycle(): ty_avg + weight * ty_now  61.4 us
    add x20, other arithmetic, subcycle(): eta_avg + weight * eta_now  50.9 us
    another operation x12, local copies, waits for them, and re-layouts  35.5 us
  transfers between devices with their start and end apart: 104, of which 40 were waited for; matrix products, arithmetic and copies ran while one was open for 58% of the time, Pallas kernels for 0%

commit v1 on v0

v1 whole, which is shorter than its diff:
```python
import functools
import numpy as np
import jax
import jax.numpy as jnp
from jax import lax
from jax.experimental import pallas as pl
from jax.experimental.pallas import tpu as pltpu
from jax.sharding import PartitionSpec as P

WAVE_COURANT = 0.4
THERM_EXP = 0.2
HALINE_CON = 0.15
PRESS_SCALE = 0.5
VISC_NUMBER = 1.0
DIFF_NUMBER = 0.5

LEVELS = 20
SUBS = 20
CHUNK = 4
NCH = LEVELS // CHUNK
PAIRS = 2 * CHUNK
ROWS = 128
LN = 128
PR = 144
EXT = 192
F32 = jnp.float32
PK = 32
UP = 32
MESH_ID = pl.DeviceIdType.MESH


def solve_table(strength):
    inner = np.zeros(LEVELS)
    last = np.zeros(LEVELS)
    inner[0] = 1.0 + strength
    last[0] = 1.0
    for k in range(1, LEVELS):
        inner[k] = 1.0 + 2.0 * strength - strength**2 / inner[k - 1]
        last[k] = 1.0 + strength - strength**2 / inner[k - 1]
    ratio = strength / inner
    before = np.concatenate([[0.0], ratio[:-1]])
    return np.stack([before, ratio, 1.0 / inner, 1.0 / last]).astype(np.float32)


def lanes(rows):
    return lax.broadcasted_iota(jnp.int32, (rows, LN), 1)


def east(tile, following):
    return pltpu.roll(jnp.where(lanes(tile.shape[0]) == 0, following, tile), LN - 1, 1)


def west(tile, previous):
    return pltpu.roll(jnp.where(lanes(tile.shape[0]) == LN - 1, previous, tile), 1, 1)


NEXT = (1, 2, 0)
PREV = (2, 0, 1)


def unpack_columns(packed, buf, chunk, fields, index_of):
    def block(i, carry):
        r = pl.multiple_of(i * 16, 16)
        tile = packed[pl.ds(r, 16), :]
        for f in fields:
            for kk in range(CHUNK):
                for m in range(2):
                    j = f * PAIRS + kk * 2 + m
                    buf[index_of[f], chunk * CHUNK + kk, m, 2, pl.ds(8 + r, 16), :] = pltpu.roll(tile, LN - 1 - 2 * j, 1)
        return carry
    lax.fori_loop(0, ROWS // 16, block, 0)


def momentum_kernel(u_hbm, v_hbm, t_hbm, s_hbm, eta_hbm, tx_hbm, ty_hbm, h_hbm, kmt_ref, weights, table,
                    us_hbm, vs_hbm, eta_out, tx_out, ty_out, corr_out, kmask_out, col_out, rows_out,
                    buf, tu, tv, pbuf, pacc, gsum, xsum, ku, kv,
                    send_col, recv_col, send_row, recv_row, send_dia, recv_dia,
                    xb, sp, rp, xf, sf, rf, hux, huy, ae, aw, an, as_, cc, ebuf, dbuf, gbuf, eacc, bacc,
                    ld_sem, xl_sem, cs_sem, cr_sem, xs_sem, xr_sem, fs_sem, fr_sem, st_sem, ot_sem):
    me_c = lax.axis_index("col")
    me_r = lax.axis_index("row")
    peer = 1 - me_c
    has_n = me_r < 3
    has_s = me_r > 0
    hbm = (u_hbm, v_hbm, t_hbm, s_hbm)

    def loads(c):
        out = []
        for f in range(4):
            for t in range(2):
                out.append(pltpu.make_async_copy(
                    hbm[f].at[pl.ds(c * CHUNK, CHUNK), :, :, pl.ds(t * LN, LN)],
                    buf.at[f, pl.ds(c * CHUNK, CHUNK), :, t, pl.ds(8, ROWS), :], ld_sem.at[c, f * 2 + t]))
        return out

    def ext_loads():
        out = []
        for t in range(2):
            lane = pl.ds(t * LN, LN)
            out.append(pltpu.make_async_copy(h_hbm.at[:, lane], xb.at[1, t, pl.ds(32, ROWS), :], xl_sem.at[t]))
            for i, ref in enumerate((eta_hbm, tx_hbm, ty_hbm)):
                out.append(pltpu.make_async_copy(ref.at[:, :, lane], xb.at[pl.ds(2 + 2 * i, 2), t, pl.ds(32, ROWS), :], xl_sem.at[2 + 2 * i + t]))
        return out

    for copy in ext_loads() + loads(0) + loads(1):
        copy.start()

    barrier = pltpu.get_barrier_semaphore()

    def greet(col, row):
        pl.semaphore_signal(barrier, inc=1, device_id={"col": col, "row": row}, device_id_type=MESH_ID)

    greet(peer, me_r)

    @pl.when(has_n)
    def _():
        greet(me_c, me_r + 1)
        greet(peer, me_r + 1)

    @pl.when(has_s)
    def _():
        greet(me_c, me_r - 1)
        greet(peer, me_r - 1)

    zrow = jnp.zeros((8, LN), F32)
    for ref, count in ((xb, 8), (xf, 4)):
        for f in range(count):
            for t in range(3):
                ref[f, t, 0:8, :] = zrow
                ref[f, t, EXT - 8:EXT, :] = zrow
    for ref, count in ((rp, 4), (rf, 2)):
        for f in range(count):
            ref[f, 0:8, :] = zrow
            ref[f, EXT - 8:EXT, :] = zrow

    def zero_side(side, lo):
        z24 = jnp.zeros((24, LN), F32)
        for f in range(8):
            for t in range(2):
                xb[f, t, lo:lo + 24, :] = z24
        for f in range(4):
            rp[f, lo:lo + 24, :] = z24
            for t in range(2):
                xf[f, t, lo:lo + 24, :] = z24
        for f in range(2):
            rf[f, lo:lo + 24, :] = z24
        for c in range(NCH):
            recv_dia[side, c, :, :] = zrow
            for f in range(4):
                for t in range(2):
                    recv_row[side, c, t, f, :, :] = zrow

    @pl.when(me_r == 0)
    def _():
        zero_side(0, 8)

    @pl.when(me_r == 3)
    def _():
        zero_side(1, 160)

    def zero_planes(i, carry):
        r = pl.multiple_of(i * 16, 16)
        z = jnp.zeros((16, LN), F32)
        for m in range(2):
            for t in range(3):
                pacc[m, t, pl.ds(r, 16), :] = z
        return carry
    lax.fori_loop(0, PR // 16, zero_planes, 0)

    def zero_planes2(i, carry):
        r = pl.multiple_of(i * 16, 16)
        z = jnp.zeros((16, LN), F32)
        for m in range(2):
            for t in range(2):
                for f in range(2):
                    gsum[f, m, t, pl.ds(r, 16), :] = z
                    xsum[f, m, t, pl.ds(r, 16), :] = z
                for ref in (tu, tv):
                    ref[0, m, t, pl.ds(r, 16), :] = z
                    ref[LEVELS + 1, m, t, pl.ds(r, 16), :] = z
        return carry
    lax.fori_loop(0, ROWS // 16, zero_planes2, 0)

    for t in range(2):
        for r in range(0, ROWS, 32):
            xb[0, t, 32 + r:64 + r, :] = kmt_ref[r:r + 32, t * LN:(t + 1) * LN].astype(F32)
    for copy in ext_loads():
        copy.wait()

    def pack_pair(first, second, send, slot, rows):
        lane = lanes(rows)

        def block(i, carry):
            r = pl.multiple_of(i * rows, rows)
            a = jnp.where(lane < 64, first(0, r), first(1, r))
            b = jnp.where(lane < 64, second(0, r), second(1, r))
            outer = (lane < 32) | (lane >= 96)
            send[slot, pl.ds(r, rows), :] = jnp.where(outer, a, pltpu.roll(b, 64, 1))
            return carry
        lax.fori_loop(0, ROWS // rows, block, 0)

    for pair in range(4):
        pack_pair(lambda t, r, p=pair: xb[2 * p, t, pl.ds(32 + r, 64), :],
                  lambda t, r, p=pair: xb[2 * p + 1, t, pl.ds(32 + r, 64), :], sp, pair, 64)

    @pl.when((me_r == 0) | (me_r == 3))
    def _():
        pl.semaphore_wait(barrier, 3)

    @pl.when((me_r != 0) & (me_r != 3))
    def _():
        pl.semaphore_wait(barrier, 5)

    def remote(src, dst, ssem, rsem, col, row):
        return pltpu.make_async_remote_copy(src_ref=src, dst_ref=dst, send_sem=ssem, recv_sem=rsem,
                                            device_id={"col": col, "row": row}, device_id_type=MESH_ID)

    def wide_copies(own, packed, landing, ssem, rsem):
        north, south = me_r + 1, me_r - 1
        side = remote(packed, landing.at[:, pl.ds(32, ROWS), :], ssem.at[0], rsem.at[0], peer, me_r)
        up = (remote(own.at[:, pl.ds(0, 2), pl.ds(136, 24), :], own.at[:, pl.ds(0, 2), pl.ds(8, 24), :], ssem.at[1], rsem.at[1], me_c, north),
              remote(packed.at[:, pl.ds(104, 24), :], landing.at[:, pl.ds(8, 24), :], ssem.at[2], rsem.at[2], peer, north))
        down = (remote(own.at[:, pl.ds(0, 2), pl.ds(32, 24), :], own.at[:, pl.ds(0, 2), pl.ds(160, 24), :], ssem.at[3], rsem.at[3], me_c, south),
                remote(packed.at[:, pl.ds(0, 24), :], landing.at[:, pl.ds(160, 24), :], ssem.at[4], rsem.at[4], peer, south))
        return side, up, down

    def edge_copies(c):
        north, south = me_r + 1, me_r - 1
        side = remote(send_col.at[c], recv_col.at[c], cs_sem.at[c, 0], cr_sem.at[c, 0], peer, me_r)
        up = (remote(send_row.at[0, c], recv_row.at[0, c], cs_sem.at[c, 1], cr_sem.at[c, 1], me_c, north),
              remote(send_dia.at[0, c], recv_dia.at[0, c], cs_sem.at[c, 2], cr_sem.at[c, 2], peer, north))
        down = (remote(send_row.at[1, c], recv_row.at[1, c], cs_sem.at[c, 3], cr_sem.at[c, 3], me_c, south),
                remote(send_dia.at[1, c], recv_dia.at[1, c], cs_sem.at[c, 4], cr_sem.at[c, 4], peer, south))
        return side, up, down

    def start_all(copies):
        side, up, down = copies
        side.start()

        @pl.when(has_n)
        def _():
            for copy in up:
                copy.start()

        @pl.when(has_s)
        def _():
            for copy in down:
                copy.start()

    def wait_recv_all(copies):
        side, up, down = copies
        side.wait_recv()

        @pl.when(has_s)
        def _():
            for copy in up:
                copy.wait_recv()

        @pl.when(has_n)
        def _():
            for copy in down:
                copy.wait_recv()

    def wait_send_all(copies):
        side, up, down = copies
        side.wait_send()

        @pl.when(has_n)
        def _():
            for copy in up:
                copy.wait_send()

        @pl.when(has_s)
        def _():
            for copy in down:
                copy.wait_send()

    start_all(wide_copies(xb, sp, rp, xs_sem, xr_sem))

    def pack_and_send(c):
        for copy in loads(c):
            copy.wait()
        lane = lanes(PK)

        def block(i, carry):
            r = pl.multiple_of(i * PK, PK)
            packed = jnp.zeros((PK, LN), F32)
            for f in range(4):
                for kk in range(CHUNK):
                    for m in range(2):
                        j = f * PAIRS + kk * 2 + m
                        k = c * CHUNK + kk
                        edge = jnp.where(lane == 0, buf[f, k, m, 0, pl.ds(8 + r, PK), :], buf[f, k, m, 1, pl.ds(8 + r, PK), :])
                        packed = jnp.where(lane >= 2 * j, pltpu.roll(edge, 2 * j + 1, 1), packed)
            send_col[c, pl.ds(r, PK), :] = packed
            return carry
        lane1 = lanes(1)
        for kk in range(CHUNK):
            for m in range(2):
                jj = kk * 2 + m
                k = c * CHUNK + kk
                for side, row, dia in ((0, 8 + ROWS - 1, 1), (1, 8, 0)):
                    for f in range(4):
                        a = buf[f, k, m, 0, row:row + 1, :]
                        b = buf[f, k, m, 1, row:row + 1, :]
                        send_row[side, c, 0, f, jj:jj + 1, :] = a
                        send_row[side, c, 1, f, jj:jj + 1, :] = b
                        if f == dia:
                            send_dia[side, c, jj:jj + 1, :] = jnp.where(lane1 == 0, a, b)
        lax.fori_loop(0, ROWS // PK, block, 0)
        start_all(edge_copies(c))

    pack_and_send(0)
    for copy in loads(2):
        copy.start()
    pack_and_send(1)

    wait_recv_all(wide_copies(xb, sp, rp, xs_sem, xr_sem))

    def unpack_wide(i, carry):
        r = pl.multiple_of(i * 32, 32)
        for pair in range(4):
            tile = rp[pair, pl.ds(r, 32), :]
            xb[2 * pair, 2, pl.ds(r, 32), :] = tile
            xb[2 * pair + 1, 2, pl.ds(r, 32), :] = pltpu.roll(tile, 64, 1)
        return carry
    lax.fori_loop(0, EXT // 32, unpack_wide, 0)

    XR = 88

    def depths(i, carry):
        r = pl.multiple_of(8 + i * XR, 8)
        kt = [xb[0, t, pl.ds(r, XR), :] for t in range(3)]
        ht = [xb[1, t, pl.ds(r, XR), :] for t in range(3)]
        for t in range(3):
            kx = jnp.minimum(kt[t], east(kt[t], kt[NEXT[t]]))
            ky = jnp.minimum(kt[t], xb[0, t, pl.ds(r + 1, XR), :])
            hux[t, pl.ds(r, XR), :] = jnp.where(kx > 0.0, 0.5 * (ht[t] + east(ht[t], ht[NEXT[t]])), 0.0)
            huy[t, pl.ds(r, XR), :] = jnp.where(ky > 0.0, 0.5 * (ht[t] + xb[1, t, pl.ds(r + 1, XR), :]), 0.0)
            cc[t, pl.ds(r, XR), :] = jnp.where(kt[t] > 0.0, WAVE_COURANT, 0.0)
        return carry
    for t in range(3):
        for ref in (hux, huy):
            ref[t, 0:8, :] = zrow
        for p in range(2):
            for m in range(2):
                ebuf[p, m, t, 0:8, :] = zrow
                ebuf[p, m, t, EXT - 8:EXT, :] = zrow
    lax.fori_loop(0, 2, depths, 0)

    def face_levels(i, carry):
        r = pl.multiple_of(i * 64, 64)
        kt = [xb[0, t, pl.ds(32 + r, 64), :] for t in range(3)]
        for t in range(2):
            ku[t, pl.ds(r, 64), :] = jnp.minimum(kt[t], east(kt[t], kt[NEXT[t]]))
            kv[t, pl.ds(r, 64), :] = jnp.minimum(kt[t], xb[0, t, pl.ds(33 + r, 64), :])
            kmask_out[0, t, pl.ds(r, 64), :] = kt[t]
        return carry
    lax.fori_loop(0, 2, face_levels, 0)

    def coefficients(i, carry):
        r = pl.multiple_of(8 + i * XR, 8)
        hx = [hux[t, pl.ds(r, XR), :] for t in range(3)]
        for t in range(3):
            c0 = cc[t, pl.ds(r, XR), :]
            cw = WAVE_COURANT * c0
            ae[t, pl.ds(r, XR), :] = cw * hx[t]
            aw[t, pl.ds(r, XR), :] = cw * west(hx[t], hx[PREV[t]])
            an[t, pl.ds(r, XR), :] = cw * huy[t, pl.ds(r, XR), :]
            as_[t, pl.ds(r, XR), :] = cw * huy[t, pl.ds(r - 1, XR), :]
        return carry
    lax.fori_loop(0, 2, coefficients, 0)

    def first_subcycle(m, base, rows):
        tx = [xb[4 + m, t, pl.ds(base, rows), :] for t in range(3)]
        for t in range(3):
            c0 = cc[t, pl.ds(base, rows), :]
            ty = xb[6 + m, t, pl.ds(base, rows), :]
            div = tx[t] - west(tx[t], tx[PREV[t]]) + ty - xb[6 + m, t, pl.ds(base - 1, rows), :]
            change = -c0 * div
            dbuf[m, t, pl.ds(base, rows), :] = change
            eta = jnp.where(c0 > 0.0, xb[2 + m, t, pl.ds(base, rows), :], 0.0) + change
            ebuf[1, m, t, pl.ds(base, rows), :] = eta

    def first_block(i, carry):
        for m in range(2):
            first_subcycle(m, pl.multiple_of(8 + i * XR, 8), XR)
        return carry
    lax.fori_loop(0, 2, first_block, 0)

    RHO_T = np.float32(-THERM_EXP * PRESS_SCALE / LEVELS / 2)
    RHO_S = np.float32(HALINE_CON * PRESS_SCALE / LEVELS / 2)
    BR = 64

    def pressure_rows(k, base, rows, tiles):
        for m in range(2):
            for t in tiles:
                half = RHO_T * buf[2, k, m, t, pl.ds(base, rows), :] + RHO_S * buf[3, k, m, t, pl.ds(base, rows), :]
                p = pacc[m, t, pl.ds(base, rows), :] + half
                pbuf[m, t, pl.ds(base, rows), :] = p
                pacc[m, t, pl.ds(base, rows), :] = p + half

    def level(k):
        def pressure_block(i, carry):
            pressure_rows(k, pl.multiple_of(8 + i * 64, 8), 64, range(3))
            return carry
        lax.fori_loop(0, 2, pressure_block, 0)
        pressure_rows(k, 8 + ROWS, 8, range(2))
        level_no = k.astype(F32)
        before = table[0, k]

        def block(i, carry):
            r = pl.multiple_of(i * BR, BR)
            b = pl.multiple_of(8 + i * BR, 8)
            wet_x = [ku[t, pl.ds(r, BR), :] > level_no for t in range(2)]
            wet_y = [kv[t, pl.ds(r, BR), :] > level_no for t in range(2)]
            for m in range(2):
                u = [buf[0, k, m, t, pl.ds(b, BR), :] for t in range(3)]
                v = [buf[1, k, m, t, pl.ds(b, BR), :] for t in range(3)]
                un = [buf[0, k, m, t, pl.ds(b + 1, BR), :] for t in range(3)]
                vs = [buf[1, k, m, t, pl.ds(b - 1, BR), :] for t in range(3)]
                p = [pbuf[m, t, pl.ds(b, BR), :] for t in range(3)]
                w = [v[t] + vs[t] for t in range(3)]
                z = [u[t] + un[t] for t in range(3)]
                for t in range(2):
                    nx, pv = NEXT[t], PREV[t]
                    us = buf[0, k, m, t, pl.ds(b - 1, BR), :]
                    gu = (p[t] - east(p[t], p[nx])) - (0.5 * u[t]) * (east(u[t], u[nx]) - west(u[t], u[pv])) \
                        - (0.125 * (w[t] + east(w[t], w[nx]))) * (un[t] - us)
                    gu = jnp.where(wet_x[t], gu, 0.0)
                    gsum[0, m, t, pl.ds(r, BR), :] += gu
                    tu[k + 1, m, t, pl.ds(r, BR), :] = u[t] + gu + before * tu[k, m, t, pl.ds(r, BR), :]
                    vn = buf[1, k, m, t, pl.ds(b + 1, BR), :]
                    pn = pbuf[m, t, pl.ds(b + 1, BR), :]
                    gv = (p[t] - pn) - (0.125 * (z[t] + west(z[t], z[pv]))) * (east(v[t], v[nx]) - west(v[t], v[pv])) \
                        - (0.5 * v[t]) * (vn - vs[t])
                    gv = jnp.where(wet_y[t], gv, 0.0)
                    gsum[1, m, t, pl.ds(r, BR), :] += gv
                    tv[k + 1, m, t, pl.ds(r, BR), :] = v[t] + gv + before * tv[k, m, t, pl.ds(r, BR), :]
            return carry
        lax.fori_loop(0, ROWS // BR, block, 0)

    def chunk_step(c, carry):
        @pl.when(c + 3 < NCH)
        def _():
            for copy in loads(c + 3):
                copy.start()

        @pl.when(c + 2 < NCH)
        def _():
            pack_and_send(c + 2)

        wait_recv_all(edge_copies(c))
        unpack_columns(recv_col.at[c], buf, c, range(4), range(4))
        for kk in range(CHUNK):
            k = c * CHUNK + kk
            for m in range(2):
                jj = kk * 2 + m
                for side, row, dia in ((0, 7, 1), (1, 8 + ROWS, 0)):
                    for f in range(4):
                        for t in range(2):
                            buf[f, k, m, t, row:row + 1, :] = recv_row[side, c, t, f, jj:jj + 1, :]
                    buf[dia, k, m, 2, row:row + 1, :] = recv_dia[side, c, jj:jj + 1, :]

        def one_level(kk, carry2):
            level(c * CHUNK + kk)
            return carry2
        lax.fori_loop(0, CHUNK, one_level, 0)
        return carry
    lax.fori_loop(0, NCH, chunk_step, 0)

    packet_copies = [pltpu.make_async_copy(recv_col, col_out, ot_sem.at[0]),
                     pltpu.make_async_copy(recv_row, rows_out, ot_sem.at[1])]
    for copy in packet_copies:
        copy.start()

    def forcing(i, carry):
        r = pl.multiple_of(i * 32, 32)
        for t in range(2):
            nx = jnp.maximum(ku[t, pl.ds(r, 32), :], 1.0)
            ny = jnp.maximum(kv[t, pl.ds(r, 32), :], 1.0)
            fx = hux[t, pl.ds(32 + r, 32), :] / nx / SUBS
            fy = huy[t, pl.ds(32 + r, 32), :] / ny / SUBS
            for m in range(2):
                xf[m, t, pl.ds(32 + r, 32), :] = fx * gsum[0, m, t, pl.ds(r, 32), :]
                xf[2 + m, t, pl.ds(32 + r, 32), :] = fy * gsum[1, m, t, pl.ds(r, 32), :]
        return carry
    lax.fori_loop(0, ROWS // 32, forcing, 0)
    for m in range(2):
        pack_pair(lambda t, r, m=m: xf[m, t, pl.ds(32 + r, 64), :],
                  lambda t, r, m=m: xf[2 + m, t, pl.ds(32 + r, 64), :], sf, m, 64)
    start_all(wide_copies(xf, sf, rf, fs_sem, fr_sem))

    def stores(c):
        out = []
        for f, (ref, dst) in enumerate(((tu, us_hbm), (tv, vs_hbm))):
            for t in range(2):
                out.append(pltpu.make_async_copy(ref.at[pl.ds(c * CHUNK + 1, CHUNK), :, t, :, :],
                                                 dst.at[pl.ds(c * CHUNK, CHUNK), :, :, pl.ds(t * LN, LN)], st_sem.at[c, f * 2 + t]))
        return out

    def upward(step, carry):
        c = NCH - 1 - step

        def block(i, carry2):
            r = pl.multiple_of(i * UP, UP)
            for f, (ref, kp) in enumerate(((tu, ku), (tv, kv))):
                for t in range(2):
                    depth = kp[t, pl.ds(r, UP), :]
                    below = [ref[c * CHUNK + CHUNK + 1, m, t, pl.ds(r, UP), :] for m in range(2)]
                    total = [xsum[f, m, t, pl.ds(r, UP), :] for m in range(2)]
                    for kk in range(CHUNK - 1, -1, -1):
                        k = c * CHUNK + kk
                        level_no = k.astype(F32)
                        inv = jnp.where(depth > level_no + 1.0, table[2, k], jnp.where(depth > level_no, table[3, k], 0.0))
                        for m in range(2):
                            below[m] = ref[k + 1, m, t, pl.ds(r, UP), :] * inv + table[1, k] * below[m]
                            ref[k + 1, m, t, pl.ds(r, UP), :] = below[m]
                            total[m] = total[m] + below[m]
                    for m in range(2):
                        xsum[f, m, t, pl.ds(r, UP), :] = total[m]
            return carry2
        lax.fori_loop(0, ROWS // UP, block, 0)
        for copy in stores(c):
            copy.start()
        return carry
    lax.fori_loop(0, NCH, upward, 0)

    wait_recv_all(wide_copies(xf, sf, rf, fs_sem, fr_sem))

    def unpack_force(i, carry):
        r = pl.multiple_of(i * 32, 32)
        for m in range(2):
            tile = rf[m, pl.ds(r, 32), :]
            xf[m, 2, pl.ds(r, 32), :] = tile
            xf[2 + m, 2, pl.ds(r, 32), :] = pltpu.roll(tile, 64, 1)
        return carry
    lax.fori_loop(0, EXT // 32, unpack_force, 0)

    def forcing_divergence(i, carry):
        r = pl.multiple_of(8 + i * XR, 8)
        for m in range(2):
            fx = [xf[m, t, pl.ds(r, XR), :] for t in range(3)]
            for t in range(3):
                div = fx[t] - west(fx[t], fx[PREV[t]]) + xf[2 + m, t, pl.ds(r, XR), :] - xf[2 + m, t, pl.ds(r - 1, XR), :]
                gbuf[m, t, pl.ds(r, XR), :] = cc[t, pl.ds(r, XR), :] * div
        return carry
    lax.fori_loop(0, 2, forcing_divergence, 0)

    whole = weights[SUBS - 1]
    moment = weights[SUBS - 1]
    for n in range(SUBS - 2, -1, -1):
        whole = whole + weights[n]
        moment = moment + whole

    def first_sums(i, carry):
        r = pl.multiple_of(i * 8, 8)
        for m in range(2):
            for t in range(3):
                eta = ebuf[1, m, t, pl.ds(32 + r, 8), :]
                bacc[m, t, pl.ds(r, 8), :] = whole * eta
                if t < 2:
                    eacc[m, t, pl.ds(r, 8), :] = weights[0] * eta
        return carry
    lax.fori_loop(0, 17, first_sums, 0)

    def subcycle(n, tail, lo, hi):
        old, new = lax.rem(n - 1, 2), lax.rem(n, 2)
        weight = weights[n - 1]
        for r, end in ((lo, 96), (96, hi)):
            first = max(r, 32)
            for t in range(3):
                c_e, c_w = ae[t, r:end, :], aw[t, r:end, :]
                c_n, c_s = an[t, r:end, :], as_[t, r:end, :]
                for m in range(2):
                    e = ebuf[old, m, t, r:end, :]
                    to_e = east(e, ebuf[old, m, NEXT[t], r:end, :])
                    to_w = west(e, ebuf[old, m, PREV[t], r:end, :])
                    to_n = ebuf[old, m, t, r + 1:end + 1, :]
                    to_s = ebuf[old, m, t, r - 1:end - 1, :]
                    d = dbuf[m, t, r:end, :] - gbuf[m, t, r:end, :]
                    d = d + (c_e * (to_e - e) + c_w * (to_w - e)) + (c_n * (to_n - e) + c_s * (to_s - e))
                    dbuf[m, t, r:end, :] = d
                    e = e + d
                    ebuf[new, m, t, r:end, :] = e
                    last = min(end, 168)
                    bacc[m, t, first - 32:last - 32, :] += tail * e[first - r:last - r]
                    if t < 2:
                        last = min(end, 160)
                        eacc[m, t, first - 32:last - 32, :] += weight * e[first - r:last - r]

    tail = whole
    for first_n, last_n, lo, hi in ((2, 5, 8, 184), (5, 13, 16, 176), (13, 21, 24, 168)):
        def body(n, carry, lo=lo, hi=hi):
            carry = carry - weights[n - 2]
            subcycle(n, carry, lo, hi)
            return carry
        tail = lax.fori_loop(first_n, last_n, body, tail)

    def averages(i, carry):
        r = pl.multiple_of(i * 16, 16)
        g = pl.multiple_of(32 + i * 16, 16)
        for t in range(2):
            depth_x = hux[t, pl.ds(g, 16), :]
            depth_y = huy[t, pl.ds(g, 16), :]
            kx = ku[t, pl.ds(r, 16), :]
            ky = kv[t, pl.ds(r, 16), :]
            inv_x = 1.0 / (depth_x + jnp.where(kx > 0.0, 0.0, 1.0))
            inv_y = 1.0 / (depth_y + jnp.where(ky > 0.0, 0.0, 1.0))
            mean_x = 1.0 / jnp.maximum(kx, 1.0)
            mean_y = 1.0 / jnp.maximum(ky, 1.0)
            kmask_out[1, t, pl.ds(r, 16), :] = kx
            kmask_out[2, t, pl.ds(r, 16), :] = ky
            for m in range(2):
                lane = slice(t * LN, (t + 1) * LN)
                acc = bacc[m, t, pl.ds(r, 16), :]
                eta_out[m, pl.ds(r, 16), lane] = eacc[m, t, pl.ds(r, 16), :]
                tx = whole * xb[4 + m, t, pl.ds(g, 16), :] + moment * xf[m, t, pl.ds(g, 16), :] \
                    - WAVE_COURANT * depth_x * (east(acc, bacc[m, NEXT[t], pl.ds(r, 16), :]) - acc)
                ty = whole * xb[6 + m, t, pl.ds(g, 16), :] + moment * xf[2 + m, t, pl.ds(g, 16), :] \
                    - WAVE_COURANT * depth_y * (bacc[m, t, pl.ds(r + 1, 16), :] - acc)
                tx = jnp.where(kx > 0.0, tx, 0.0)
                ty = jnp.where(ky > 0.0, ty, 0.0)
                tx_out[m, pl.ds(r, 16), lane] = tx
                ty_out[m, pl.ds(r, 16), lane] = ty
                corr_out[0, m, t, pl.ds(r, 16), :] = tx * inv_x - xsum[0, m, t, pl.ds(r, 16), :] * mean_x
                corr_out[1, m, t, pl.ds(r, 16), :] = ty * inv_y - xsum[1, m, t, pl.ds(r, 16), :] * mean_y
        return carry
    lax.fori_loop(0, ROWS // 16, averages, 0)

    wait_send_all(wide_copies(xb, sp, rp, xs_sem, xr_sem))
    wait_send_all(wide_copies(xf, sf, rf, fs_sem, fr_sem))
    for copy in packet_copies:
        copy.wait()

    def drain(c, carry):
        wait_send_all(edge_copies(c))
        for copy in stores(c):
            copy.wait()
        return carry
    lax.fori_loop(0, NCH, drain, 0)


def tracer_kernel(u_hbm, v_hbm, t_hbm, s_hbm, us_hbm, vs_hbm, eta_in, tx_in, ty_in, corr, kmask, col_in, rows_in, table,
                  eta_hbm, tx_hbm, ty_hbm, un_hbm, vn_hbm, tn_hbm, sn_hbm,
                  buf, tt, ts, su, sv, small, cols, rows, ld_sem, ed_sem, st_sem, in_sem, out_sem):
    hbm = (u_hbm, v_hbm, t_hbm, s_hbm)
    sources = (eta_in, tx_in, ty_in)
    sinks = (eta_hbm, tx_hbm, ty_hbm)

    def loads(c):
        out = []
        for f in range(4):
            for t in range(2):
                out.append(pltpu.make_async_copy(
                    hbm[f].at[pl.ds(c * CHUNK, CHUNK), :, :, pl.ds(t * LN, LN)],
                    buf.at[f, pl.ds(c * CHUNK, CHUNK), :, t, pl.ds(8, ROWS), :], ld_sem.at[c, f * 2 + t]))
        for f, (src, dst) in enumerate(((us_hbm, su), (vs_hbm, sv))):
            out.append(pltpu.make_async_copy(src.at[pl.ds(c * CHUNK, CHUNK)], dst.at[pl.ds(c * CHUNK, CHUNK)], ld_sem.at[c, 8 + f]))
        return out

    def stores_v(c):
        return [pltpu.make_async_copy(src.at[pl.ds(c * CHUNK, CHUNK)], dst.at[pl.ds(c * CHUNK, CHUNK)], st_sem.at[c, f])
                for f, (src, dst) in enumerate(((su, un_hbm), (sv, vn_hbm)))]

    def stores_t(c):
        return [pltpu.make_async_copy(src.at[pl.ds(c * CHUNK + 1, CHUNK)], dst.at[pl.ds(c * CHUNK, CHUNK)], st_sem.at[c, 2 + f])
                for f, (src, dst) in enumerate(((tt, tn_hbm), (ts, sn_hbm)))]

    edges = [pltpu.make_async_copy(col_in, cols, ed_sem.at[0]), pltpu.make_async_copy(rows_in, rows, ed_sem.at[1])]
    for copy in edges:
        copy.start()
    for c in range(NCH):
        for copy in loads(c):
            copy.start()
    small_in = [pltpu.make_async_copy(sources[i], small.at[i], in_sem.at[i]) for i in range(3)]
    small_out = [pltpu.make_async_copy(small.at[i], sinks[i], out_sem.at[i]) for i in range(3)]
    for copy in small_in:
        copy.start()

    def zero_planes(i, carry):
        r = pl.multiple_of(i * 16, 16)
        z = jnp.zeros((16, 2 * LN), F32)
        for m in range(2):
            for ref in (tt, ts):
                ref[0, m, pl.ds(r, 16), :] = z
                ref[LEVELS + 1, m, pl.ds(r, 16), :] = z
        return carry
    lax.fori_loop(0, ROWS // 16, zero_planes, 0)
    for copy in edges:
        copy.wait()

    BR = 32

    def level(k):
        level_no = k.astype(F32)
        before = table[0, k]

        def block(i, carry):
            r = pl.multiple_of(i * BR, BR)
            b = pl.multiple_of(8 + i * BR, 8)
            for t in range(2):
                lane = slice(t * LN, (t + 1) * LN)
                wet_x = kmask[1, t, pl.ds(r, BR), :] > level_no
                wet_y = kmask[2, t, pl.ds(r, BR), :] > level_no
                for m in range(2):
                    su[k, m, pl.ds(r, BR), lane] = jnp.where(wet_x, su[k, m, pl.ds(r, BR), lane] + corr[0, m, t, pl.ds(r, BR), :], 0.0)
                    sv[k, m, pl.ds(r, BR), lane] = jnp.where(wet_y, sv[k, m, pl.ds(r, BR), lane] + corr[1, m, t, pl.ds(r, BR), :], 0.0)
            wet = [kmask[0, t, pl.ds(r, BR), :] > level_no for t in range(2)]
            for m in range(2):
                hu = [0.5 * buf[0, k, m, t, pl.ds(b, BR), :] for t in range(3)]
                hv = [0.5 * buf[1, k, m, t, pl.ds(b, BR), :] for t in range(2)]
                hs = [0.5 * buf[1, k, m, t, pl.ds(b - 1, BR), :] for t in range(2)]
                for f, ref in ((2, tt), (3, ts)):
                    q = [buf[f, k, m, t, pl.ds(b, BR), :] for t in range(3)]
                    fx = [hu[t] * (q[t] + east(q[t], q[NEXT[t]])) for t in range(3)]
                    for t in range(2):
                        lane = slice(t * LN, (t + 1) * LN)
                        fy = hv[t] * (q[t] + buf[f, k, m, t, pl.ds(b + 1, BR), :])
                        fs = hs[t] * (q[t] + buf[f, k, m, t, pl.ds(b - 1, BR), :])
                        adv = q[t] - ((fx[t] - west(fx[t], fx[PREV[t]])) + (fy - fs))
                        adv = jnp.where(wet[t], adv, 0.0)
                        ref[k + 1, m, pl.ds(r, BR), lane] = adv + before * ref[k, m, pl.ds(r, BR), lane]
            return carry
        lax.fori_loop(0, ROWS // BR, block, 0)

    def chunk_step(c, carry):
        for copy in loads(c):
            copy.wait()
        unpack_columns(cols.at[c], buf, c, (0, 2, 3), range(4))
        for kk in range(CHUNK):
            k = c * CHUNK + kk
            for m in range(2):
                jj = kk * 2 + m
                for f in (1, 2, 3):
                    for t in range(2):
                        buf[f, k, m, t, 7:8, :] = rows[0, c, t, f, jj:jj + 1, :]
                for f in (2, 3):
                    for t in range(2):
                        buf[f, k, m, t, 8 + ROWS:9 + ROWS, :] = rows[1, c, t, f, jj:jj + 1, :]

        def one_level(kk, carry2):
            level(c * CHUNK + kk)
            return carry2
        lax.fori_loop(0, CHUNK, one_level, 0)
        for copy in stores_v(c):
            copy.start()
        return carry
    lax.fori_loop(0, NCH, chunk_step, 0)

    for copy in small_in:
        copy.wait()
    for copy in small_out:
        copy.start()

    def upward(step, carry):
        c = NCH - 1 - step

        def block(i, carry2):
            r = pl.multiple_of(i * 16, 16)
            for t in range(2):
                lane = slice(t * LN, (t + 1) * LN)
                depth = kmask[0, t, pl.ds(r, 16), :]
                below = [[ref[c * CHUNK + CHUNK + 1, m, pl.ds(r, 16), lane] for m in range(2)] for ref in (tt, ts)]
                for kk in range(CHUNK - 1, -1, -1):
                    k = c * CHUNK + kk
                    level_no = k.astype(F32)
                    inv = jnp.where(depth > level_no + 1.0, table[2, k], jnp.where(depth > level_no, table[3, k], 0.0))
                    for f, ref in enumerate((tt, ts)):
                        for m in range(2):
                            below[f][m] = ref[k + 1, m, pl.ds(r, 16), lane] * inv + table[1, k] * below[f][m]
                            ref[k + 1, m, pl.ds(r, 16), lane] = below[f][m]
            return carry2
        lax.fori_loop(0, ROWS // 16, block, 0)
        for copy in stores_t(c):
            copy.start()
        return carry
    lax.fori_loop(0, NCH, upward, 0)

    for copy in small_out:
        copy.wait()

    def drain(c, carry):
        for copy in stores_v(c) + stores_t(c):
            copy.wait()
        return carry
    lax.fori_loop(0, NCH, drain, 0)


def solution(mesh):
    assert mesh.shape["col"] == 2 and mesh.shape["row"] == 4
    any_spec = pl.BlockSpec(memory_space=pl.ANY)
    vmem_spec = pl.BlockSpec(memory_space=pltpu.VMEM)
    smem_spec = pl.BlockSpec(memory_space=pltpu.SMEM)
    shape = lambda *dims: jax.ShapeDtypeStruct(dims, F32)
    dma = lambda *dims: pltpu.SemaphoreType.DMA(dims)
    vm = lambda *dims: pltpu.VMEM(dims, F32)
    visc = solve_table(VISC_NUMBER)
    diff = solve_table(DIFF_NUMBER)
    full = (LEVELS, 2, ROWS, 2 * LN)
    flat = (2, ROWS, 2 * LN)

    momentum = pl.pallas_call(
        momentum_kernel,
        name="momentum",
        out_shape=(shape(*full), shape(*full), shape(*flat), shape(*flat), shape(*flat), shape(2, 2, 2, ROWS, LN),
                   shape(3, 2, ROWS, LN), shape(NCH, ROWS, LN), shape(2, NCH, 2, 4, PAIRS, LN)),
        in_specs=[any_spec] * 8 + [vmem_spec, smem_spec, smem_spec],
        out_specs=(any_spec, any_spec, vmem_spec, vmem_spec, vmem_spec, vmem_spec, vmem_spec, any_spec, any_spec),
        scratch_shapes=[
            vm(4, LEVELS, 2, 3, PR, LN), vm(LEVELS + 2, 2, 2, ROWS, LN), vm(LEVELS + 2, 2, 2, ROWS, LN),
            vm(2, 3, PR, LN), vm(2, 3, PR, LN), vm(2, 2, 2, ROWS, LN), vm(2, 2, 2, ROWS, LN), vm(2, ROWS, LN), vm(2, ROWS, LN),
            vm(NCH, ROWS, LN), vm(NCH, ROWS, LN), vm(2, NCH, 2, 4, PAIRS, LN), vm(2, NCH, 2, 4, PAIRS, LN),
            vm(2, NCH, PAIRS, LN), vm(2, NCH, PAIRS, LN),
            vm(8, 3, EXT, LN), vm(4, ROWS, LN), vm(4, EXT, LN), vm(4, 3, EXT, LN), vm(2, ROWS, LN), vm(2, EXT, LN),
            vm(3, EXT, LN), vm(3, EXT, LN), vm(3, EXT, LN), vm(3, EXT, LN), vm(3, EXT, LN), vm(3, EXT, LN), vm(3, EXT, LN),
            vm(2, 2, 3, EXT, LN), vm(2, 3, EXT, LN), vm(2, 3, EXT, LN), vm(2, 2, ROWS + 8, LN), vm(2, 3, ROWS + 8, LN),
            dma(NCH, 8), dma(8), dma(NCH, 5), dma(NCH, 5), dma(5), dma(5), dma(5), dma(5), dma(NCH, 4), dma(2),
        ],
        compiler_params=pltpu.CompilerParams(collective_id=0, has_side_effects=True, vmem_limit_bytes=67043328),
    )

    tracers = pl.pallas_call(
        tracer_kernel,
        name="tracers",
        out_shape=(shape(*flat), shape(*flat), shape(*flat), shape(*full), shape(*full), shape(*full), shape(*full)),
        in_specs=[any_spec] * 9 + [vmem_spec, vmem_spec, any_spec, any_spec, smem_spec],
        out_specs=(any_spec,) * 7,
        scratch_shapes=[
            vm(4, LEVELS, 2, 3, PR, LN), vm(LEVELS + 2, 2, ROWS, 2 * LN), vm(LEVELS + 2, 2, ROWS, 2 * LN),
            vm(*full), vm(*full), vm(3, 2, ROWS, 2 * LN), vm(NCH, ROWS, LN), vm(2, NCH, 2, 4, PAIRS, LN),
            dma(NCH, 10), dma(2), dma(NCH, 4), dma(3), dma(3),
        ],
        compiler_params=pltpu.CompilerParams(vmem_limit_bytes=67043328),
    )

    def local_step(vel_x, vel_y, pot_temp, salinity, surf_eta, trans_x, trans_y, col_depth, wet_levels, avg_weights):
        star_x, star_y, eta, tx, ty, corr, kmask, cols, rows = momentum(
            vel_x, vel_y, pot_temp, salinity, surf_eta, trans_x, trans_y, col_depth, wet_levels, avg_weights, jnp.asarray(visc))
        return tracers(vel_x, vel_y, pot_temp, salinity, star_x, star_y, eta, tx, ty, corr, kmask, cols, rows, jnp.asarray(diff))

    spec_3d = P(None, None, "row", "col")
    spec_2d = P(None, "row", "col")
    spec_map = P("row", "col")
    return jax.shard_map(local_step, mesh=mesh, in_specs=(spec_3d, spec_3d, spec_3d, spec_3d, spec_2d, spec_2d, spec_2d, spec_map, spec_map, P()),
                         out_specs=(spec_2d, spec_2d, spec_2d, spec_3d, spec_3d, spec_3d, spec_3d), check_vma=False)
```

time: 1290 us -> 92.8 us (0.07); the launches traced: 1270 us -> 92.6 us
  other arithmetic: 635 us -> 0 us
  local copies, waits for them, and re-layouts: 378 us -> 0 us
  starting transfers between devices: 154 us -> 0 us
  waiting for transfers between devices: 102 us -> 0 us
  Pallas kernels: 0 us -> 92 us
    dynamic_update_slice x160 -> x0, other arithmetic: 312 us -> none  [vertical_solve(): lax.scan(forward, (zero_level, zero_level), (lower_diag, main_diag, upper...]
    add x43 -> x0, other arithmetic: 172 us -> none  [the longest x20 61.4 us: subcycle(): ty_avg + weight * ty_now]
    ppermute x104 -> x0, starting transfers between devices: 154 us -> none  [the longest x24 63.3 us: take_south(): lax.ppermute(edge_slab, 'row', [(source, source + 1) for source in range(...]
    slice x163 -> x0, local copies, waits for them, and re-layouts: 133 us -> none  [the longest x26 32 us: take_west(): edge_slab = field_in[..., -1:]]
    mul x30 -> x0, other arithmetic: 105 us -> none  [the longest x20 33 us: subcycle(): WAVE_COURANT * depth_y * (shift_north(eta_now) - eta_now)]
    ppermute x104 -> x0, waiting for transfers between devices: 102 us -> none  [the longest x25 81.7 us: take_west(): lax.ppermute(edge_slab, 'col', [(source, (source + 1) % col_count) for so...]
    pallas_call x0 -> x2, Pallas kernels: none -> 92 us  [the longest x1 60.8 us: local_step(): momentum(vel_x, vel_y, pot_temp, salinity, surf_eta, trans_x, trans_y, co...]
    mul x80 -> x0, local copies, waits for them, and re-layouts: 78.9 us -> none  [forward(): divisor = diag_k - low_k * upper_prev]
  transfers between devices with their start and end apart: 104 -> 0, of which waited for: 40 -> 0; matrix products, arithmetic and copies ran while one was open for 58% -> 0% of each run, Pallas kernels for 0% -> 0%
where the time goes in v1:
time: 92.8 us; the launch traced here: 92.6 us
  Pallas kernels  92 us (99%)
    pallas_call x1, Pallas kernels, local_step(): momentum(vel_x, vel_y, pot_temp, salinity, surf_eta, trans_x, trans_y, co...  60.8 us
    pallas_call x1, Pallas kernels, local_step(): tracers(vel_x, vel_y, pot_temp, salinity, star_x, star_y, eta, tx, ty, co...  31.2 us

profile of v1, /device:TPU:0, one launch (start us, length us, event | category | flops | bytes accessed | tf_op | source)
XLA Modules:
  0.0 92.6 jit_solution(2803882660330521151)
XLA Ops:
  0.6 60.8 %momentum.1 = (f32[20,2,128,256]{3,2,1,0:T(8,128)}, f32[20,2,128,256]{3,2,1,0:T(8,128)}, f32[2,128,256]{2,1,0:T(8,128)}, f32[2,128,256]{2,1,0:T(8,128)}, f32[2,1...) custom-call(f32[20,2,128,256]{3,2,1,0:T(8,128)} %u_hbm.3, ...), custom_call_target="tpu_custom_call" | custom-call | tf_op jit(solution)/shard_map/momentum/pallas_call | solution.py:838
  61.4 31.2 %tracers.1 = (f32[2,128,256]{2,1,0:T(8,128)}, f32[2,128,256]{2,1,0:T(8,128)}, f32[2,128,256]{2,1,0:T(8,128)}, f32[20,2,128,256]{3,2,1,0:T(8,128)}, f32[20,2,128,...) custom-call(f32[20,2,128,256]{3,2,1,0:T(8,128)} %u_hbm.3, f32[20,2,128,256]{3,2,1,0:T(8,128)} %v_hbm.3, ...), custom_call_target="tpu_custom_call" | custom-call | tf_op jit(solution)/shard_map/tracers/pallas_call | solution.py:840

commit v2 on v1

v2 whole, which is shorter than its diff:
```python
import functools
import numpy as np
import jax
import jax.numpy as jnp
from jax import lax
from jax.experimental import pallas as pl
from jax.experimental.pallas import tpu as pltpu
from jax.sharding import PartitionSpec as P

WAVE_COURANT = 0.4
THERM_EXP = 0.2
HALINE_CON = 0.15
PRESS_SCALE = 0.5
VISC_NUMBER = 1.0
DIFF_NUMBER = 0.5

LEVELS = 20
SUBS = 20
CHUNK = 4
NCH = LEVELS // CHUNK
PAIRS = 2 * CHUNK
ROWS = 128
LN = 128
PR = 144
EXT = 192
F32 = jnp.float32
PK = 64
UP = 32
MESH_ID = pl.DeviceIdType.MESH


def solve_table(strength):
    inner = np.zeros(LEVELS)
    last = np.zeros(LEVELS)
    inner[0] = 1.0 + strength
    last[0] = 1.0
    for k in range(1, LEVELS):
        inner[k] = 1.0 + 2.0 * strength - strength**2 / inner[k - 1]
        last[k] = 1.0 + strength - strength**2 / inner[k - 1]
    ratio = strength / inner
    before = np.concatenate([[0.0], ratio[:-1]])
    return np.stack([before, ratio, 1.0 / inner, 1.0 / last]).astype(np.float32)


def lanes(rows):
    return lax.broadcasted_iota(jnp.int32, (rows, LN), 1)


def east(tile, following):
    return pltpu.roll(jnp.where(lanes(tile.shape[0]) == 0, following, tile), LN - 1, 1)


def west(tile, previous):
    return pltpu.roll(jnp.where(lanes(tile.shape[0]) == LN - 1, previous, tile), 1, 1)


NEXT = (1, 2, 0)
PREV = (2, 0, 1)


def halo(packed, j):
    return pltpu.roll(packed, LN - 1 - 2 * j, 1)


def east_pair(first, second, edge):
    last = lanes(first.shape[0]) == LN - 1
    a, b = pltpu.roll(first, LN - 1, 1), pltpu.roll(second, LN - 1, 1)
    return jnp.where(last, b, a), jnp.where(last, edge, b)


def west_pair(first, second, edge):
    origin = lanes(first.shape[0]) == 0
    a, b = pltpu.roll(first, 1, 1), pltpu.roll(second, 1, 1)
    return jnp.where(origin, edge, a), jnp.where(origin, a, b)


def momentum_kernel(u_hbm, v_hbm, t_hbm, s_hbm, eta_hbm, tx_hbm, ty_hbm, h_hbm, kmt_ref, weights, table,
                    us_hbm, vs_hbm, eta_out, tx_out, ty_out, corr_out, kmask_out, col_out, rows_out,
                    buf, tu, tv, cu, cv, pbuf, pacc, phal, rhoc, gsum, xsum, ku, kv,
                    send_col, recv_col, send_row, recv_row,
                    xb, sp, rp, xf, sf, rf, hux, huy, ae, aw, an, as_, cc, ebufa, ebufb, dbuf, gbuf, eacc, bacc,
                    ld_sem, xl_sem, cs_sem, cr_sem, xs_sem, xr_sem, fs_sem, fr_sem, st_sem, ot_sem):
    me_c = lax.axis_index("col")
    me_r = lax.axis_index("row")
    peer = 1 - me_c
    has_n = me_r < 3
    has_s = me_r > 0
    hbm = (u_hbm, v_hbm, t_hbm, s_hbm)

    def loads(c):
        out = []
        for f in range(4):
            for t in range(2):
                out.append(pltpu.make_async_copy(
                    hbm[f].at[pl.ds(c * CHUNK, CHUNK), :, :, pl.ds(t * LN, LN)],
                    buf.at[f, pl.ds(c * CHUNK, CHUNK), :, t, pl.ds(8, ROWS), :], ld_sem.at[c, f * 2 + t]))
        return out

    def ext_loads():
        out = []
        for t in range(2):
            lane = pl.ds(t * LN, LN)
            out.append(pltpu.make_async_copy(h_hbm.at[:, lane], xb.at[1, t, pl.ds(32, ROWS), :], xl_sem.at[t]))
            for i, ref in enumerate((eta_hbm, tx_hbm, ty_hbm)):
                out.append(pltpu.make_async_copy(ref.at[:, :, lane], xb.at[pl.ds(2 + 2 * i, 2), t, pl.ds(32, ROWS), :], xl_sem.at[2 + 2 * i + t]))
        return out

    for copy in loads(0) + ext_loads() + loads(1):
        copy.start()

    barrier = pltpu.get_barrier_semaphore()

    def greet(col, row):
        pl.semaphore_signal(barrier, inc=1, device_id={"col": col, "row": row}, device_id_type=MESH_ID)

    greet(peer, me_r)

    @pl.when(has_n)
    def _():
        greet(me_c, me_r + 1)
        greet(peer, me_r + 1)

    @pl.when(has_s)
    def _():
        greet(me_c, me_r - 1)
        greet(peer, me_r - 1)

    zrow = jnp.zeros((8, LN), F32)
    for ref, count in ((xb, 8), (xf, 4)):
        for f in range(count):
            for t in range(3):
                ref[f, t, 0:8, :] = zrow
                ref[f, t, EXT - 8:EXT, :] = zrow
    for ref, count in ((rp, 4), (rf, 2)):
        for f in range(count):
            ref[f, 0:8, :] = zrow
            ref[f, EXT - 8:EXT, :] = zrow

    def zero_side(side, lo):
        z24 = jnp.zeros((24, LN), F32)
        for f in range(8):
            for t in range(2):
                xb[f, t, lo:lo + 24, :] = z24
        for f in range(4):
            rp[f, lo:lo + 24, :] = z24
            for t in range(2):
                xf[f, t, lo:lo + 24, :] = z24
        for f in range(2):
            rf[f, lo:lo + 24, :] = z24
        for c in range(NCH):
            recv_col[c, 136 * side:136 * side + 8, :] = zrow
            for f in range(4):
                for t in range(2):
                    recv_row[side, c, t, f, :, :] = zrow

    @pl.when(me_r == 0)
    def _():
        zero_side(0, 8)

    @pl.when(me_r == 3)
    def _():
        zero_side(1, 160)

    def zero_planes(i, carry):
        r = pl.multiple_of(i * 16, 16)
        z = jnp.zeros((16, LN), F32)
        for m in range(2):
            for t in range(2):
                pacc[m, t, pl.ds(r, 16), :] = z
            phal[m, pl.ds(r, 16), :] = z
        return carry
    lax.fori_loop(0, PR // 16, zero_planes, 0)

    def zero_planes2(i, carry):
        r = pl.multiple_of(i * 16, 16)
        z = jnp.zeros((16, LN), F32)
        for m in range(2):
            for t in range(2):
                for f in range(2):
                    gsum[f, m, t, pl.ds(r, 16), :] = z
                    xsum[f, m, t, pl.ds(r, 16), :] = z
                for ref in (cu, cv):
                    ref[m, t, pl.ds(r, 16), :] = z
                for ref in (tu, tv):
                    ref[LEVELS, m, t, pl.ds(r, 16), :] = z
        return carry
    lax.fori_loop(0, ROWS // 16, zero_planes2, 0)

    for t in range(2):
        for r in range(0, ROWS, 32):
            xb[0, t, 32 + r:64 + r, :] = kmt_ref[r:r + 32, t * LN:(t + 1) * LN].astype(F32)
    for copy in ext_loads():
        copy.wait()

    @pl.when((me_r == 0) | (me_r == 3))
    def _():
        pl.semaphore_wait(barrier, 3)

    @pl.when((me_r != 0) & (me_r != 3))
    def _():
        pl.semaphore_wait(barrier, 5)

    def remote(src, dst, ssem, rsem, col, row):
        return pltpu.make_async_remote_copy(src_ref=src, dst_ref=dst, send_sem=ssem, recv_sem=rsem,
                                            device_id={"col": col, "row": row}, device_id_type=MESH_ID)

    def wide_copies(own, packed, landing, ssem, rsem):
        north, south = me_r + 1, me_r - 1
        side = remote(packed, landing.at[:, pl.ds(32, ROWS), :], ssem.at[0], rsem.at[0], peer, me_r)
        up = (remote(own.at[:, pl.ds(0, 2), pl.ds(136, 24), :], own.at[:, pl.ds(0, 2), pl.ds(8, 24), :], ssem.at[1], rsem.at[1], me_c, north),
              remote(packed.at[:, pl.ds(104, 24), :], landing.at[:, pl.ds(8, 24), :], ssem.at[2], rsem.at[2], peer, north))
        down = (remote(own.at[:, pl.ds(0, 2), pl.ds(32, 24), :], own.at[:, pl.ds(0, 2), pl.ds(160, 24), :], ssem.at[3], rsem.at[3], me_c, south),
                remote(packed.at[:, pl.ds(0, 24), :], landing.at[:, pl.ds(160, 24), :], ssem.at[4], rsem.at[4], peer, south))
        return side, up, down

    def edge_copies(c):
        north, south = me_r + 1, me_r - 1
        side = remote(send_col.at[c], recv_col.at[c, pl.ds(8, ROWS), :], cs_sem.at[c, 0], cr_sem.at[c, 0], peer, me_r)
        up = (remote(send_row.at[0, c], recv_row.at[0, c], cs_sem.at[c, 1], cr_sem.at[c, 1], me_c, north),
              remote(send_col.at[c, pl.ds(ROWS - 8, 8), :], recv_col.at[c, pl.ds(0, 8), :], cs_sem.at[c, 2], cr_sem.at[c, 2], peer, north))
        down = (remote(send_row.at[1, c], recv_row.at[1, c], cs_sem.at[c, 3], cr_sem.at[c, 3], me_c, south),
                remote(send_col.at[c, pl.ds(0, 8), :], recv_col.at[c, pl.ds(8 + ROWS, 8), :], cs_sem.at[c, 4], cr_sem.at[c, 4], peer, south))
        return side, up, down

    def start_all(copies):
        side, up, down = copies
        if side is not None:
            side.start()

        @pl.when(has_n)
        def _():
            for copy in up:
                copy.start()

        @pl.when(has_s)
        def _():
            for copy in down:
                copy.start()

    def wait_recv_all(copies):
        side, up, down = copies
        if side is not None:
            side.wait_recv()

        @pl.when(has_s)
        def _():
            for copy in up:
                copy.wait_recv()

        @pl.when(has_n)
        def _():
            for copy in down:
                copy.wait_recv()

    def wait_send_all(copies):
        side, up, down = copies
        side.wait_send()

        @pl.when(has_n)
        def _():
            for copy in up:
                copy.wait_send()

        @pl.when(has_s)
        def _():
            for copy in down:
                copy.wait_send()

    def rows_only(copies):
        return None, copies[1][:1], copies[2][:1]

    def columns_only(copies):
        return copies[0], copies[1][1:], copies[2][1:]

    start_all(rows_only(wide_copies(xb, sp, rp, xs_sem, xr_sem)))

    def pack_and_send(c, with_maps=False):
        for copy in loads(c):
            copy.wait()
        lane = lanes(PK)

        def block(i, carry):
            r = pl.multiple_of(i * PK, PK)
            pairs = [(f, c * CHUNK + kk, m) for f in range(4) for kk in range(CHUNK) for m in range(2)]
            column = [[buf[f, k, m, t, pl.ds(8 + r, PK), :] for f, k, m in pairs] for t in range(2)]
            if with_maps:
                for t in range(2):
                    column[t] += [xb[0, t, pl.ds(32 + r, PK), :], xb[1, t, pl.ds(32 + r, PK), :]]
            packed = jnp.zeros((PK, LN), F32)
            count = len(column[0])
            for i in range(count + 1):
                edge = jnp.where(lane == 0, column[0][min(i, count - 1)], column[1][max(i - 1, 0)])
                edge = pltpu.roll(edge, 2 * i, 1) if i else edge
                packed = jnp.where(lane >= 2 * i - 1, edge, packed) if i else edge
            send_col[c, pl.ds(r, PK), :] = packed
            return carry
        for kk in range(CHUNK):
            for m in range(2):
                jj = kk * 2 + m
                k = c * CHUNK + kk
                for side, row in ((0, 8 + ROWS - 1), (1, 8)):
                    for f in range(4):
                        for t in range(2):
                            send_row[side, c, t, f, jj:jj + 1, :] = buf[f, k, m, t, row:row + 1, :]
        lax.fori_loop(0, ROWS // PK, block, 0)
        start_all(edge_copies(c))

    pack_and_send(0, with_maps=True)
    for copy in loads(2):
        copy.start()
    pack_and_send(1)

    RHO_T = np.float32(-THERM_EXP * PRESS_SCALE / LEVELS / 2)
    RHO_S = np.float32(HALINE_CON * PRESS_SCALE / LEVELS / 2)
    BR = 64

    def pressure_rows(k, slot, base, rows):
        for m in range(2):
            for t in range(2):
                half = RHO_T * buf[2, k, m, t, pl.ds(base, rows), :] + RHO_S * buf[3, k, m, t, pl.ds(base, rows), :]
                p = pacc[m, t, pl.ds(base, rows), :] + half
                slot[m, t, pl.ds(base, rows), :] = p
                pacc[m, t, pl.ds(base, rows), :] = p + half

    def level(c, kk, now, later):
        k = c * CHUNK + kk
        pressure_rows(k, now, 8 + ROWS, 8)
        level_no = k.astype(F32)
        before = table[0, k]
        following = jnp.minimum(k + 1, LEVELS - 1)

        def block(i, carry):
            r = pl.multiple_of(i * BR, BR)
            b = pl.multiple_of(8 + i * BR, 8)
            wet_x = [ku[t, pl.ds(r, BR), :] > level_no for t in range(2)]
            wet_y = [kv[t, pl.ds(r, BR), :] > level_no for t in range(2)]
            packed = recv_col[c, pl.ds(b, BR), :]
            packed_w = packed + recv_col[c, pl.ds(b - 1, BR), :]
            packed_z = packed + recv_col[c, pl.ds(b + 1, BR), :]
            packed_r = rhoc[pl.ds(r, BR), :]
            for m in range(2):
                j = kk * 2 + m
                half = halo(packed_r, j)
                p_edge = phal[m, pl.ds(r, BR), :] + half
                phal[m, pl.ds(r, BR), :] = p_edge + half
                u_edge, v_edge = halo(packed, j), halo(packed, PAIRS + j)
                w_edge, z_edge = halo(packed_w, PAIRS + j), halo(packed_z, j)
                u = [buf[0, k, m, t, pl.ds(b, BR), :] for t in range(2)]
                v = [buf[1, k, m, t, pl.ds(b, BR), :] for t in range(2)]
                un = [buf[0, k, m, t, pl.ds(b + 1, BR), :] for t in range(2)]
                vs = [buf[1, k, m, t, pl.ds(b - 1, BR), :] for t in range(2)]
                p = [now[m, t, pl.ds(b, BR), :] for t in range(2)]
                w = [v[t] + vs[t] for t in range(2)]
                z = [u[t] + un[t] for t in range(2)]
                ue, uw = east_pair(*u, u_edge), west_pair(*u, u_edge)
                ve, vw = east_pair(*v, v_edge), west_pair(*v, v_edge)
                pe, we, zw = east_pair(*p, p_edge), east_pair(*w, w_edge), west_pair(*z, z_edge)
                for t in range(2):
                    us = buf[0, k, m, t, pl.ds(b - 1, BR), :]
                    gu = (p[t] - pe[t]) - (0.5 * u[t]) * (ue[t] - uw[t]) - (0.125 * (w[t] + we[t])) * (un[t] - us)
                    gu = jnp.where(wet_x[t], gu, 0.0)
                    gsum[0, m, t, pl.ds(r, BR), :] += gu
                    new = u[t] + gu + before * cu[m, t, pl.ds(r, BR), :]
                    cu[m, t, pl.ds(r, BR), :] = new
                    tu[k, m, t, pl.ds(r, BR), :] = new
                    vn = buf[1, k, m, t, pl.ds(b + 1, BR), :]
                    pn = now[m, t, pl.ds(b + 1, BR), :]
                    gv = (p[t] - pn) - (0.125 * (z[t] + zw[t])) * (ve[t] - vw[t]) - (0.5 * v[t]) * (vn - vs[t])
                    gv = jnp.where(wet_y[t], gv, 0.0)
                    gsum[1, m, t, pl.ds(r, BR), :] += gv
                    new = v[t] + gv + before * cv[m, t, pl.ds(r, BR), :]
                    cv[m, t, pl.ds(r, BR), :] = new
                    tv[k, m, t, pl.ds(r, BR), :] = new
            pressure_rows(following, later, b, BR)
            return carry
        lax.fori_loop(0, ROWS // BR, block, 0)

    def first_pressure(i, carry):
        pressure_rows(0, pbuf.at[0], pl.multiple_of(8 + i * 64, 8), 64)
        return carry
    lax.fori_loop(0, 2, first_pressure, 0)

    def chunk_step(c, carry):
        @pl.when(c + 3 < NCH)
        def _():
            for copy in loads(c + 3):
                copy.start()

        @pl.when(c + 2 < NCH)
        def _():
            pack_and_send(c + 2)

        @pl.when(c == 2)
        def _():
            pack_wide()

        wait_recv_all(edge_copies(c))

        @pl.when(c == 0)
        def _():
            face_maps()

        for kk in range(CHUNK):
            k = c * CHUNK + kk
            for m in range(2):
                jj = kk * 2 + m
                for side, row in ((0, 7), (1, 8 + ROWS)):
                    for f in range(4):
                        for t in range(2):
                            buf[f, k, m, t, row:row + 1, :] = recv_row[side, c, t, f, jj:jj + 1, :]
        packed = recv_col[c, 8:8 + ROWS, :]
        rhoc[...] = RHO_T * pltpu.roll(packed, LN - 4 * PAIRS, 1) + RHO_S * pltpu.roll(packed, LN - 6 * PAIRS, 1)

        def two_levels(h, carry2):
            level(c, 2 * h, pbuf.at[0], pbuf.at[1])
            level(c, 2 * h + 1, pbuf.at[1], pbuf.at[0])
            return carry2
        lax.fori_loop(0, CHUNK // 2, two_levels, 0)
        return carry

    def pack_wide():
        for pair in range(4):
            pack_pair(lambda t, r, p=pair: xb[2 * p, t, pl.ds(32 + r, 64), :],
                      lambda t, r, p=pair: xb[2 * p + 1, t, pl.ds(32 + r, 64), :], sp, pair, 64)
        start_all(columns_only(wide_copies(xb, sp, rp, xs_sem, xr_sem)))

    def face_maps():
        wait_recv_all(rows_only(wide_copies(xb, sp, rp, xs_sem, xr_sem)))

        def maps(i, carry):
            r = pl.multiple_of(i * 64, 64)
            packed = recv_col[0, pl.ds(8 + r, 64), :]
            kt = [xb[0, t, pl.ds(32 + r, 64), :] for t in range(2)]
            ht = [xb[1, t, pl.ds(32 + r, 64), :] for t in range(2)]
            ke = east_pair(*kt, halo(packed, 4 * PAIRS))
            he = east_pair(*ht, halo(packed, 4 * PAIRS + 1))
            for t in range(2):
                kx = jnp.minimum(kt[t], ke[t])
                ky = jnp.minimum(kt[t], xb[0, t, pl.ds(33 + r, 64), :])
                ku[t, pl.ds(r, 64), :] = kx
                kv[t, pl.ds(r, 64), :] = ky
                kmask_out[0, t, pl.ds(r, 64), :] = kt[t]
                kmask_out[1, t, pl.ds(r, 64), :] = kx
                kmask_out[2, t, pl.ds(r, 64), :] = ky
                hux[t, pl.ds(32 + r, 64), :] = jnp.where(kx > 0.0, 0.5 * (ht[t] + he[t]), 0.0)
                huy[t, pl.ds(32 + r, 64), :] = jnp.where(ky > 0.0, 0.5 * (ht[t] + xb[1, t, pl.ds(33 + r, 64), :]), 0.0)
            return carry
        lax.fori_loop(0, 2, maps, 0)

    def pack_pair(first, second, send, slot, rows):
        lane = lanes(rows)

        def block(i, carry):
            r = pl.multiple_of(i * rows, rows)
            a = jnp.where(lane < 64, first(0, r), first(1, r))
            b = jnp.where(lane < 64, second(0, r), second(1, r))
            outer = (lane < 32) | (lane >= 96)
            send[slot, pl.ds(r, rows), :] = jnp.where(outer, a, pltpu.roll(b, 64, 1))
            return carry
        lax.fori_loop(0, ROWS // rows, block, 0)

    lax.fori_loop(0, NCH, chunk_step, 0)

    packet_copies = [pltpu.make_async_copy(recv_col, col_out, ot_sem.at[0]),
                     pltpu.make_async_copy(recv_row, rows_out, ot_sem.at[1])]
    for copy in packet_copies:
        copy.start()

    def forcing(i, carry):
        r = pl.multiple_of(i * 32, 32)
        for t in range(2):
            nx = jnp.maximum(ku[t, pl.ds(r, 32), :], 1.0)
            ny = jnp.maximum(kv[t, pl.ds(r, 32), :], 1.0)
            fx = hux[t, pl.ds(32 + r, 32), :] / nx / SUBS
            fy = huy[t, pl.ds(32 + r, 32), :] / ny / SUBS
            for m in range(2):
                xf[m, t, pl.ds(32 + r, 32), :] = fx * gsum[0, m, t, pl.ds(r, 32), :]
                xf[2 + m, t, pl.ds(32 + r, 32), :] = fy * gsum[1, m, t, pl.ds(r, 32), :]
        return carry
    lax.fori_loop(0, ROWS // 32, forcing, 0)
    for m in range(2):
        pack_pair(lambda t, r, m=m: xf[m, t, pl.ds(32 + r, 64), :],
                  lambda t, r, m=m: xf[2 + m, t, pl.ds(32 + r, 64), :], sf, m, 64)
    start_all(wide_copies(xf, sf, rf, fs_sem, fr_sem))

    def stores(c):
        out = []
        for f, (ref, dst) in enumerate(((tu, us_hbm), (tv, vs_hbm))):
            for t in range(2):
                out.append(pltpu.make_async_copy(ref.at[pl.ds(c * CHUNK, CHUNK), :, t, :, :],
                                                 dst.at[pl.ds(c * CHUNK, CHUNK), :, :, pl.ds(t * LN, LN)], st_sem.at[c, f * 2 + t]))
        return out

    def upward(step, carry):
        c = NCH - 1 - step

        def block(i, carry2):
            r = pl.multiple_of(i * UP, UP)
            for f, (ref, kp) in enumerate(((tu, ku), (tv, kv))):
                for t in range(2):
                    depth = kp[t, pl.ds(r, UP), :]
                    below = [ref[c * CHUNK + CHUNK, m, t, pl.ds(r, UP), :] for m in range(2)]
                    total = [xsum[f, m, t, pl.ds(r, UP), :] for m in range(2)]
                    for kk in range(CHUNK - 1, -1, -1):
                        k = c * CHUNK + kk
                        level_no = k.astype(F32)
                        inv = jnp.where(depth > level_no + 1.0, table[2, k], jnp.where(depth > level_no, table[3, k], 0.0))
                        for m in range(2):
                            below[m] = ref[k, m, t, pl.ds(r, UP), :] * inv + table[1, k] * below[m]
                            ref[k, m, t, pl.ds(r, UP), :] = below[m]
                            total[m] = total[m] + below[m]
                    for m in range(2):
                        xsum[f, m, t, pl.ds(r, UP), :] = total[m]
            return carry2
        lax.fori_loop(0, ROWS // UP, block, 0)
        for copy in stores(c):
            copy.start()
        return carry
    lax.fori_loop(0, NCH, upward, 0)

    wait_recv_all(columns_only(wide_copies(xb, sp, rp, xs_sem, xr_sem)))

    def unpack_wide(i, carry):
        r = pl.multiple_of(i * 32, 32)
        for pair in range(4):
            tile = rp[pair, pl.ds(r, 32), :]
            xb[2 * pair, 2, pl.ds(r, 32), :] = tile
            xb[2 * pair + 1, 2, pl.ds(r, 32), :] = pltpu.roll(tile, 64, 1)
        return carry
    lax.fori_loop(0, EXT // 32, unpack_wide, 0)

    XR = 88

    def depths(i, carry):
        r = pl.multiple_of(8 + i * XR, 8)
        kt = [xb[0, t, pl.ds(r, XR), :] for t in range(3)]
        ht = [xb[1, t, pl.ds(r, XR), :] for t in range(3)]
        for t in range(3):
            kx = jnp.minimum(kt[t], east(kt[t], kt[NEXT[t]]))
            ky = jnp.minimum(kt[t], xb[0, t, pl.ds(r + 1, XR), :])
            hux[t, pl.ds(r, XR), :] = jnp.where(kx > 0.0, 0.5 * (ht[t] + east(ht[t], ht[NEXT[t]])), 0.0)
            huy[t, pl.ds(r, XR), :] = jnp.where(ky > 0.0, 0.5 * (ht[t] + xb[1, t, pl.ds(r + 1, XR), :]), 0.0)
            cc[t, pl.ds(r, XR), :] = jnp.where(kt[t] > 0.0, WAVE_COURANT, 0.0)
        return carry
    for t in range(3):
        for ref in (hux, huy):
            ref[t, 0:8, :] = zrow
        for ref in (ebufa, ebufb):
            for m in range(2):
                ref[m, t, 0:8, :] = zrow
                ref[m, t, EXT - 8:EXT, :] = zrow
    lax.fori_loop(0, 2, depths, 0)

    def coefficients(i, carry):
        r = pl.multiple_of(8 + i * XR, 8)
        hx = [hux[t, pl.ds(r, XR), :] for t in range(3)]
        for t in range(3):
            c0 = cc[t, pl.ds(r, XR), :]
            cw = WAVE_COURANT * c0
            ae[t, pl.ds(r, XR), :] = cw * hx[t]
            aw[t, pl.ds(r, XR), :] = cw * west(hx[t], hx[PREV[t]])
            an[t, pl.ds(r, XR), :] = cw * huy[t, pl.ds(r, XR), :]
            as_[t, pl.ds(r, XR), :] = cw * huy[t, pl.ds(r - 1, XR), :]
        return carry
    lax.fori_loop(0, 2, coefficients, 0)

    def first_subcycle(m, base, rows):
        tx = [xb[4 + m, t, pl.ds(base, rows), :] for t in range(3)]
        for t in range(3):
            c0 = cc[t, pl.ds(base, rows), :]
            ty = xb[6 + m, t, pl.ds(base, rows), :]
            div = tx[t] - west(tx[t], tx[PREV[t]]) + ty - xb[6 + m, t, pl.ds(base - 1, rows), :]
            change = -c0 * div
            dbuf[m, t, pl.ds(base, rows), :] = change
            eta = jnp.where(c0 > 0.0, xb[2 + m, t, pl.ds(base, rows), :], 0.0) + change
            ebufa[m, t, pl.ds(base, rows), :] = eta

    def first_block(i, carry):
        for m in range(2):
            first_subcycle(m, pl.multiple_of(8 + i * XR, 8), XR)
        return carry
    lax.fori_loop(0, 2, first_block, 0)

    wait_recv_all(wide_copies(xf, sf, rf, fs_sem, fr_sem))

    def unpack_force(i, carry):
        r = pl.multiple_of(i * 32, 32)
        for m in range(2):
            tile = rf[m, pl.ds(r, 32), :]
            xf[m, 2, pl.ds(r, 32), :] = tile
            xf[2 + m, 2, pl.ds(r, 32), :] = pltpu.roll(tile, 64, 1)
        return carry
    lax.fori_loop(0, EXT // 32, unpack_force, 0)

    def forcing_divergence(i, carry):
        r = pl.multiple_of(8 + i * XR, 8)
        for m in range(2):
            fx = [xf[m, t, pl.ds(r, XR), :] for t in range(3)]
            for t in range(3):
                div = fx[t] - west(fx[t], fx[PREV[t]]) + xf[2 + m, t, pl.ds(r, XR), :] - xf[2 + m, t, pl.ds(r - 1, XR), :]
                gbuf[m, t, pl.ds(r, XR), :] = cc[t, pl.ds(r, XR), :] * div
        return carry
    lax.fori_loop(0, 2, forcing_divergence, 0)

    whole = weights[SUBS - 1]
    moment = weights[SUBS - 1]
    for n in range(SUBS - 2, -1, -1):
        whole = whole + weights[n]
        moment = moment + whole

    def first_sums(i, carry):
        r = pl.multiple_of(i * 8, 8)
        for m in range(2):
            for t in range(3):
                eta = ebufa[m, t, pl.ds(32 + r, 8), :]
                bacc[m, t, pl.ds(r, 8), :] = whole * eta
                if t < 2:
                    eacc[m, t, pl.ds(r, 8), :] = weights[0] * eta
        return carry
    lax.fori_loop(0, 17, first_sums, 0)

    def subcycle(n, tail, lo, hi, old, new):
        tail = tail - weights[n - 2]
        weight = weights[n - 1]
        for r, end in ((lo, 96), (96, hi)):
            first = max(r, 32)
            for t in range(3):
                c_e, c_w = ae[t, r:end, :], aw[t, r:end, :]
                c_n, c_s = an[t, r:end, :], as_[t, r:end, :]
                for m in range(2):
                    e = old[m, t, r:end, :]
                    to_e = east(e, old[m, NEXT[t], r:end, :])
                    to_w = west(e, old[m, PREV[t], r:end, :])
                    to_n = old[m, t, r + 1:end + 1, :]
                    to_s = old[m, t, r - 1:end - 1, :]
                    d = dbuf[m, t, r:end, :] - gbuf[m, t, r:end, :]
                    d = d + (c_e * (to_e - e) + c_w * (to_w - e)) + (c_n * (to_n - e) + c_s * (to_s - e))
                    dbuf[m, t, r:end, :] = d
                    e = e + d
                    new[m, t, r:end, :] = e
                    last = min(end, 168)
                    bacc[m, t, first - 32:last - 32, :] += tail * e[first - r:last - r]
                    if t < 2:
                        last = min(end, 160)
                        eacc[m, t, first - 32:last - 32, :] += weight * e[first - r:last - r]
        return tail

    tail = subcycle(2, whole, 8, 184, ebufa, ebufb)
    for first_n, steps, lo, hi in ((3, 1, 8, 184), (5, 4, 16, 176), (13, 4, 24, 168)):
        def two_cycles(h, carry, first_n=first_n, lo=lo, hi=hi):
            n = first_n + 2 * h
            carry = subcycle(n, carry, lo, hi, ebufb, ebufa)
            return subcycle(n + 1, carry, lo, hi, ebufa, ebufb)
        tail = lax.fori_loop(0, steps, two_cycles, tail)

    def averages(i, carry):
        r = pl.multiple_of(i * 16, 16)
        g = pl.multiple_of(32 + i * 16, 16)
        for t in range(2):
            depth_x = hux[t, pl.ds(g, 16), :]
            depth_y = huy[t, pl.ds(g, 16), :]
            kx = ku[t, pl.ds(r, 16), :]
            ky = kv[t, pl.ds(r, 16), :]
            inv_x = 1.0 / (depth_x + jnp.where(kx > 0.0, 0.0, 1.0))
            inv_y = 1.0 / (depth_y + jnp.where(ky > 0.0, 0.0, 1.0))
            mean_x = 1.0 / jnp.maximum(kx, 1.0)
            mean_y = 1.0 / jnp.maximum(ky, 1.0)
            for m in range(2):
                lane = slice(t * LN, (t + 1) * LN)
                acc = bacc[m, t, pl.ds(r, 16), :]
                eta_out[m, pl.ds(r, 16), lane] = eacc[m, t, pl.ds(r, 16), :]
                tx = whole * xb[4 + m, t, pl.ds(g, 16), :] + moment * xf[m, t, pl.ds(g, 16), :] \
                    - WAVE_COURANT * depth_x * (east(acc, bacc[m, NEXT[t], pl.ds(r, 16), :]) - acc)
                ty = whole * xb[6 + m, t, pl.ds(g, 16), :] + moment * xf[2 + m, t, pl.ds(g, 16), :] \
                    - WAVE_COURANT * depth_y * (bacc[m, t, pl.ds(r + 1, 16), :] - acc)
                tx = jnp.where(kx > 0.0, tx, 0.0)
                ty = jnp.where(ky > 0.0, ty, 0.0)
                tx_out[m, pl.ds(r, 16), lane] = tx
                ty_out[m, pl.ds(r, 16), lane] = ty
                corr_out[0, m, t, pl.ds(r, 16), :] = tx * inv_x - xsum[0, m, t, pl.ds(r, 16), :] * mean_x
                corr_out[1, m, t, pl.ds(r, 16), :] = ty * inv_y - xsum[1, m, t, pl.ds(r, 16), :] * mean_y
        return carry
    lax.fori_loop(0, ROWS // 16, averages, 0)

    wait_send_all(wide_copies(xb, sp, rp, xs_sem, xr_sem))
    wait_send_all(wide_copies(xf, sf, rf, fs_sem, fr_sem))
    for copy in packet_copies:
        copy.wait()

    def drain(c, carry):
        wait_send_all(edge_copies(c))
        for copy in stores(c):
            copy.wait()
        return carry
    lax.fori_loop(0, NCH, drain, 0)


def tracer_kernel(u_hbm, v_hbm, t_hbm, s_hbm, us_hbm, vs_hbm, eta_in, tx_in, ty_in, corr_in, kmask_in, col_in, rows_in, table,
                  eta_hbm, tx_hbm, ty_hbm, un_hbm, vn_hbm, tn_hbm, sn_hbm,
                  buf, tt, ts, ct, su, sv, small, corr, kmask, cols, rows, ld_sem, ed_sem, st_sem, in_sem, out_sem):
    hbm = (u_hbm, v_hbm, t_hbm, s_hbm)
    sources = (eta_in, tx_in, ty_in)
    sinks = (eta_hbm, tx_hbm, ty_hbm)

    def loads(c):
        out = []
        for f in range(4):
            for t in range(2):
                out.append(pltpu.make_async_copy(
                    hbm[f].at[pl.ds(c * CHUNK, CHUNK), :, :, pl.ds(t * LN, LN)],
                    buf.at[f, pl.ds(c * CHUNK, CHUNK), :, t, pl.ds(8, ROWS), :], ld_sem.at[c, f * 2 + t]))
        for f, (src, dst) in enumerate(((us_hbm, su), (vs_hbm, sv))):
            out.append(pltpu.make_async_copy(src.at[pl.ds(c * CHUNK, CHUNK)], dst.at[pl.ds(c * CHUNK, CHUNK)], ld_sem.at[c, 8 + f]))
        return out

    def stores_v(c):
        return [pltpu.make_async_copy(src.at[pl.ds(c * CHUNK, CHUNK)], dst.at[pl.ds(c * CHUNK, CHUNK)], st_sem.at[c, f])
                for f, (src, dst) in enumerate(((su, un_hbm), (sv, vn_hbm)))]

    def stores_t(c):
        return [pltpu.make_async_copy(src.at[pl.ds(c * CHUNK, CHUNK)], dst.at[pl.ds(c * CHUNK, CHUNK)], st_sem.at[c, 2 + f])
                for f, (src, dst) in enumerate(((tt, tn_hbm), (ts, sn_hbm)))]

    edges = [pltpu.make_async_copy(src, dst, ed_sem.at[i])
             for i, (src, dst) in enumerate(((col_in, cols), (rows_in, rows), (corr_in, corr), (kmask_in, kmask)))]
    for copy in edges:
        copy.start()
    for c in range(NCH):
        for copy in loads(c):
            copy.start()
    small_in = [pltpu.make_async_copy(sources[i], small.at[i], in_sem.at[i]) for i in range(3)]
    small_out = [pltpu.make_async_copy(small.at[i], sinks[i], out_sem.at[i]) for i in range(3)]
    for copy in small_in:
        copy.start()

    def zero_planes(i, carry):
        r = pl.multiple_of(i * 16, 16)
        z = jnp.zeros((16, 2 * LN), F32)
        for f in range(2):
            for m in range(2):
                for t in range(2):
                    ct[f, m, t, pl.ds(r, 16), :] = z[:, :LN]
        for m in range(2):
            for ref in (tt, ts):
                ref[LEVELS, m, pl.ds(r, 16), :] = z
        return carry
    lax.fori_loop(0, ROWS // 16, zero_planes, 0)
    for copy in edges:
        copy.wait()

    BR = 64

    def level(c, kk):
        k = c * CHUNK + kk
        level_no = k.astype(F32)
        before = table[0, k]

        def block(i, carry):
            r = pl.multiple_of(i * BR, BR)
            b = pl.multiple_of(8 + i * BR, 8)
            wet = [kmask[0, t, pl.ds(r, BR), :] > level_no for t in range(2)]
            packed = cols[c, pl.ds(b, BR), :]
            for m in range(2):
                j = kk * 2 + m
                u = [buf[0, k, m, t, pl.ds(b, BR), :] for t in range(2)]
                v = [buf[1, k, m, t, pl.ds(b, BR), :] for t in range(2)]
                vs = [buf[1, k, m, t, pl.ds(b - 1, BR), :] for t in range(2)]
                uw = west_pair(*u, halo(packed, j))
                for f, ref in ((2, tt), (3, ts)):
                    q = [buf[f, k, m, t, pl.ds(b, BR), :] for t in range(2)]
                    edge = halo(packed, f * PAIRS + j)
                    qe, qw = east_pair(*q, edge), west_pair(*q, edge)
                    for t in range(2):
                        lane = slice(t * LN, (t + 1) * LN)
                        fy = v[t] * (q[t] + buf[f, k, m, t, pl.ds(b + 1, BR), :])
                        fs = vs[t] * (q[t] + buf[f, k, m, t, pl.ds(b - 1, BR), :])
                        adv = q[t] - 0.5 * ((u[t] * (q[t] + qe[t]) - uw[t] * (q[t] + qw[t])) + (fy - fs))
                        adv = jnp.where(wet[t], adv, 0.0)
                        new = adv + before * ct[f - 2, m, t, pl.ds(r, BR), :]
                        ct[f - 2, m, t, pl.ds(r, BR), :] = new
                        ref[k, m, pl.ds(r, BR), lane] = new
            for t in range(2):
                lane = slice(t * LN, (t + 1) * LN)
                wet_x = kmask[1, t, pl.ds(r, BR), :] > level_no
                wet_y = kmask[2, t, pl.ds(r, BR), :] > level_no
                for m in range(2):
                    su[k, m, pl.ds(r, BR), lane] = jnp.where(wet_x, su[k, m, pl.ds(r, BR), lane] + corr[0, m, t, pl.ds(r, BR), :], 0.0)
                    sv[k, m, pl.ds(r, BR), lane] = jnp.where(wet_y, sv[k, m, pl.ds(r, BR), lane] + corr[1, m, t, pl.ds(r, BR), :], 0.0)
            return carry
        lax.fori_loop(0, ROWS // BR, block, 0)

    def chunk_step(c, carry):
        for copy in loads(c):
            copy.wait()
        for kk in range(CHUNK):
            k = c * CHUNK + kk
            for m in range(2):
                jj = kk * 2 + m
                for f in (1, 2, 3):
                    for t in range(2):
                        buf[f, k, m, t, 7:8, :] = rows[0, c, t, f, jj:jj + 1, :]
                for f in (2, 3):
                    for t in range(2):
                        buf[f, k, m, t, 8 + ROWS:9 + ROWS, :] = rows[1, c, t, f, jj:jj + 1, :]

        def one_level(kk, carry2):
            level(c, kk)
            return carry2
        lax.fori_loop(0, CHUNK, one_level, 0)
        for copy in stores_v(c):
            copy.start()
        return carry
    lax.fori_loop(0, NCH, chunk_step, 0)

    for copy in small_in:
        copy.wait()
    for copy in small_out:
        copy.start()

    def upward(step, carry):
        c = NCH - 1 - step

        def block(i, carry2):
            r = pl.multiple_of(i * UP, UP)
            for t in range(2):
                lane = slice(t * LN, (t + 1) * LN)
                depth = kmask[0, t, pl.ds(r, UP), :]
                below = [[ref[c * CHUNK + CHUNK, m, pl.ds(r, UP), lane] for m in range(2)] for ref in (tt, ts)]
                for kk in range(CHUNK - 1, -1, -1):
                    k = c * CHUNK + kk
                    level_no = k.astype(F32)
                    inv = jnp.where(depth > level_no + 1.0, table[2, k], jnp.where(depth > level_no, table[3, k], 0.0))
                    for f, ref in enumerate((tt, ts)):
                        for m in range(2):
                            below[f][m] = ref[k, m, pl.ds(r, UP), lane] * inv + table[1, k] * below[f][m]
                            ref[k, m, pl.ds(r, UP), lane] = below[f][m]
            return carry2
        lax.fori_loop(0, ROWS // UP, block, 0)
        for copy in stores_t(c):
            copy.start()
        return carry
    lax.fori_loop(0, NCH, upward, 0)

    for copy in small_out:
        copy.wait()

    def drain(c, carry):
        for copy in stores_v(c) + stores_t(c):
            copy.wait()
        return carry
    lax.fori_loop(0, NCH, drain, 0)


def solution(mesh):
    assert mesh.shape["col"] == 2 and mesh.shape["row"] == 4
    any_spec = pl.BlockSpec(memory_space=pl.ANY)
    vmem_spec = pl.BlockSpec(memory_space=pltpu.VMEM)
    smem_spec = pl.BlockSpec(memory_space=pltpu.SMEM)
    shape = lambda *dims: jax.ShapeDtypeStruct(dims, F32)
    dma = lambda *dims: pltpu.SemaphoreType.DMA(dims)
    vm = lambda *dims: pltpu.VMEM(dims, F32)
    visc = solve_table(VISC_NUMBER)
    diff = solve_table(DIFF_NUMBER)
    full = (LEVELS, 2, ROWS, 2 * LN)
    flat = (2, ROWS, 2 * LN)

    momentum = pl.pallas_call(
        momentum_kernel,
        name="momentum",
        out_shape=(shape(*full), shape(*full), shape(*flat), shape(*flat), shape(*flat), shape(2, 2, 2, ROWS, LN),
                   shape(3, 2, ROWS, LN), shape(NCH, PR, LN), shape(2, NCH, 2, 4, PAIRS, LN)),
        in_specs=[any_spec] * 8 + [vmem_spec, smem_spec, smem_spec],
        out_specs=(any_spec, any_spec, vmem_spec, vmem_spec, vmem_spec, vmem_spec, vmem_spec, any_spec, any_spec),
        scratch_shapes=[
            vm(4, LEVELS, 2, 2, PR, LN), vm(LEVELS + 1, 2, 2, ROWS, LN), vm(LEVELS + 1, 2, 2, ROWS, LN),
            vm(2, 2, ROWS, LN), vm(2, 2, ROWS, LN), vm(2, 2, 2, PR, LN), vm(2, 2, PR, LN), vm(2, PR, LN), vm(ROWS, LN),
            vm(2, 2, 2, ROWS, LN), vm(2, 2, 2, ROWS, LN), vm(2, ROWS, LN), vm(2, ROWS, LN),
            vm(NCH, ROWS, LN), vm(NCH, PR, LN), vm(2, NCH, 2, 4, PAIRS, LN), vm(2, NCH, 2, 4, PAIRS, LN),
            vm(8, 3, EXT, LN), vm(4, ROWS, LN), vm(4, EXT, LN), vm(4, 3, EXT, LN), vm(2, ROWS, LN), vm(2, EXT, LN),
            vm(3, EXT, LN), vm(3, EXT, LN), vm(3, EXT, LN), vm(3, EXT, LN), vm(3, EXT, LN), vm(3, EXT, LN), vm(3, EXT, LN),
            vm(2, 3, EXT, LN), vm(2, 3, EXT, LN), vm(2, 3, EXT, LN), vm(2, 3, EXT, LN), vm(2, 2, ROWS + 8, LN), vm(2, 3, ROWS + 8, LN),
            dma(NCH, 8), dma(8), dma(NCH, 5), dma(NCH, 5), dma(5), dma(5), dma(5), dma(5), dma(NCH, 4), dma(2),
        ],
        compiler_params=pltpu.CompilerParams(collective_id=0, has_side_effects=True, vmem_limit_bytes=67043328),
    )

    tracers = pl.pallas_call(
        tracer_kernel,
        name="tracers",
        out_shape=(shape(*flat), shape(*flat), shape(*flat), shape(*full), shape(*full), shape(*full), shape(*full)),
        in_specs=[any_spec] * 13 + [smem_spec],
        out_specs=(any_spec,) * 7,
        scratch_shapes=[
            vm(4, LEVELS, 2, 2, PR, LN), vm(LEVELS + 1, 2, ROWS, 2 * LN), vm(LEVELS + 1, 2, ROWS, 2 * LN), vm(2, 2, 2, ROWS, LN),
            vm(*full), vm(*full), vm(3, 2, ROWS, 2 * LN), vm(2, 2, 2, ROWS, LN), vm(3, 2, ROWS, LN),
            vm(NCH, PR, LN), vm(2, NCH, 2, 4, PAIRS, LN),
            dma(NCH, 10), dma(4), dma(NCH, 4), dma(3), dma(3),
        ],
        compiler_params=pltpu.CompilerParams(vmem_limit_bytes=67043328),
    )

    def local_step(vel_x, vel_y, pot_temp, salinity, surf_eta, trans_x, trans_y, col_depth, wet_levels, avg_weights):
        star_x, star_y, eta, tx, ty, corr, kmask, cols, rows = momentum(
            vel_x, vel_y, pot_temp, salinity, surf_eta, trans_x, trans_y, col_depth, wet_levels, avg_weights, jnp.asarray(visc))
        return tracers(vel_x, vel_y, pot_temp, salinity, star_x, star_y, eta, tx, ty, corr, kmask, cols, rows, jnp.asarray(diff))

    spec_3d = P(None, None, "row", "col")
    spec_2d = P(None, "row", "col")
    spec_map = P("row", "col")
    return jax.shard_map(local_step, mesh=mesh, in_specs=(spec_3d, spec_3d, spec_3d, spec_3d, spec_2d, spec_2d, spec_2d, spec_map, spec_map, P()),
                         out_specs=(spec_2d, spec_2d, spec_2d, spec_3d, spec_3d, spec_3d, spec_3d), check_vma=False)
```

time: 92.8 us -> 77.1 us (0.83)
  Pallas kernels: 92 us -> 76.4 us
    pallas_call x1, Pallas kernels: 60.8 us -> 51.5 us  [local_step(): momentum(vel_x, vel_y, pot_temp, salinity, surf_eta, trans_x, trans_y, co...]
    pallas_call x1, Pallas kernels: 31.2 us -> 24.9 us  [local_step(): tracers(vel_x, vel_y, pot_temp, salinity, star_x, star_y, eta, tx, ty, co...]
where the time goes in v2:
time: 77.1 us; the launch traced here: 77 us
  Pallas kernels  76.4 us (99%)
    pallas_call x1, Pallas kernels, local_step(): momentum(vel_x, vel_y, pot_temp, salinity, surf_eta, trans_x, trans_y, co...  51.5 us
    pallas_call x1, Pallas kernels, local_step(): tracers(vel_x, vel_y, pot_temp, salinity, star_x, star_y, eta, tx, ty, co...  24.9 us

profile of v2, /device:TPU:0, one launch (start us, length us, event | category | flops | bytes accessed | tf_op | source)
XLA Modules:
  0.0 77.0 jit_solution(9068610820623267765)
XLA Ops:
  0.6 51.5 %momentum.1 = (f32[20,2,128,256]{3,2,1,0:T(8,128)}, f32[20,2,128,256]{3,2,1,0:T(8,128)}, f32[2,128,256]{2,1,0:T(8,128)}, f32[2,128,256]{2,1,0:T(8,128)}, f32[2,1...) custom-call(f32[20,2,128,256]{3,2,1,0:T(8,128)} %u_hbm.3, ...), custom_call_target="tpu_custom_call" | custom-call | tf_op jit(solution)/shard_map/momentum/pallas_call | solution.py:903
  52.1 24.9 %tracers.1 = (f32[2,128,256]{2,1,0:T(8,128)}, f32[2,128,256]{2,1,0:T(8,128)}, f32[2,128,256]{2,1,0:T(8,128)}, f32[20,2,128,256]{3,2,1,0:T(8,128)}, f32[20,2,128,...) custom-call(f32[20,2,128,256]{3,2,1,0:T(8,128)} %u_hbm.3, f32[20,2,128,256]{3,2,1,0:T(8,128)} %v_hbm.3, ...), custom_call_target="tpu_custom_call" | custom-call | tf_op jit(solution)/shard_map/tracers/pallas_call | solution.py:905

commit v3 on v2

--- a/solution.py
+++ b/solution.py
@@ -313,6 +313,7 @@
     RHO_T = np.float32(-THERM_EXP * PRESS_SCALE / LEVELS / 2)
     RHO_S = np.float32(HALINE_CON * PRESS_SCALE / LEVELS / 2)
     BR = 64
+    SB = 16
 
     def pressure_rows(k, slot, base, rows):
         for m in range(2):
@@ -330,49 +331,51 @@
         following = jnp.minimum(k + 1, LEVELS - 1)
 
         def block(i, carry):
-            r = pl.multiple_of(i * BR, BR)
-            b = pl.multiple_of(8 + i * BR, 8)
-            wet_x = [ku[t, pl.ds(r, BR), :] > level_no for t in range(2)]
-            wet_y = [kv[t, pl.ds(r, BR), :] > level_no for t in range(2)]
-            packed = recv_col[c, pl.ds(b, BR), :]
-            packed_w = packed + recv_col[c, pl.ds(b - 1, BR), :]
-            packed_z = packed + recv_col[c, pl.ds(b + 1, BR), :]
-            packed_r = rhoc[pl.ds(r, BR), :]
+            for q in range(0, BR, SB):
+                piece(pl.multiple_of(i * BR + q, SB), pl.multiple_of(8 + i * BR + q, 8))
+            return carry
+
+        def piece(r, b):
+            wet_x = [ku[t, pl.ds(r, SB), :] > level_no for t in range(2)]
+            wet_y = [kv[t, pl.ds(r, SB), :] > level_no for t in range(2)]
+            packed = recv_col[c, pl.ds(b, SB), :]
+            packed_w = packed + recv_col[c, pl.ds(b - 1, SB), :]
+            packed_z = packed + recv_col[c, pl.ds(b + 1, SB), :]
+            packed_r = rhoc[pl.ds(r, SB), :]
             for m in range(2):
                 j = kk * 2 + m
                 half = halo(packed_r, j)
-                p_edge = phal[m, pl.ds(r, BR), :] + half
-                phal[m, pl.ds(r, BR), :] = p_edge + half
+                p_edge = phal[m, pl.ds(r, SB), :] + half
+                phal[m, pl.ds(r, SB), :] = p_edge + half
                 u_edge, v_edge = halo(packed, j), halo(packed, PAIRS + j)
                 w_edge, z_edge = halo(packed_w, PAIRS + j), halo(packed_z, j)
-                u = [buf[0, k, m, t, pl.ds(b, BR), :] for t in range(2)]
-                v = [buf[1, k, m, t, pl.ds(b, BR), :] for t in range(2)]
-                un = [buf[0, k, m, t, pl.ds(b + 1, BR), :] for t in range(2)]
-                vs = [buf[1, k, m, t, pl.ds(b - 1, BR), :] for t in range(2)]
-                p = [now[m, t, pl.ds(b, BR), :] for t in range(2)]
+                u = [buf[0, k, m, t, pl.ds(b, SB), :] for t in range(2)]
+                v = [buf[1, k, m, t, pl.ds(b, SB), :] for t in range(2)]
+                un = [buf[0, k, m, t, pl.ds(b + 1, SB), :] for t in range(2)]
+                vs = [buf[1, k, m, t, pl.ds(b - 1, SB), :] for t in range(2)]
+                p = [now[m, t, pl.ds(b, SB), :] for t in range(2)]
                 w = [v[t] + vs[t] for t in range(2)]
                 z = [u[t] + un[t] for t in range(2)]
                 ue, uw = east_pair(*u, u_edge), west_pair(*u, u_edge)
                 ve, vw = east_pair(*v, v_edge), west_pair(*v, v_edge)
                 pe, we, zw = east_pair(*p, p_edge), east_pair(*w, w_edge), west_pair(*z, z_edge)
                 for t in range(2):
-                    us = buf[0, k, m, t, pl.ds(b - 1, BR), :]
+                    us = buf[0, k, m, t, pl.ds(b - 1, SB), :]
                     gu = (p[t] - pe[t]) - (0.5 * u[t]) * (ue[t] - uw[t]) - (0.125 * (w[t] + we[t])) * (un[t] - us)
                     gu = jnp.where(wet_x[t], gu, 0.0)
-                    gsum[0, m, t, pl.ds(r, BR), :] += gu
-                    new = u[t] + gu + before * cu[m, t, pl.ds(r, BR), :]
-                    cu[m, t, pl.ds(r, BR), :] = new
-                    tu[k, m, t, pl.ds(r, BR), :] = new
-                    vn = buf[1, k, m, t, pl.ds(b + 1, BR), :]
-                    pn = now[m, t, pl.ds(b + 1, BR), :]
+                    gsum[0, m, t, pl.ds(r, SB), :] += gu
+                    new = u[t] + gu + before * cu[m, t, pl.ds(r, SB), :]
+                    cu[m, t, pl.ds(r, SB), :] = new
+                    tu[k, m, t, pl.ds(r, SB), :] = new
+                    vn = buf[1, k, m, t, pl.ds(b + 1, SB), :]
+                    pn = now[m, t, pl.ds(b + 1, SB), :]
                     gv = (p[t] - pn) - (0.125 * (z[t] + zw[t])) * (ve[t] - vw[t]) - (0.5 * v[t]) * (vn - vs[t])
                     gv = jnp.where(wet_y[t], gv, 0.0)
-                    gsum[1, m, t, pl.ds(r, BR), :] += gv
-                    new = v[t] + gv + before * cv[m, t, pl.ds(r, BR), :]
-                    cv[m, t, pl.ds(r, BR), :] = new
-                    tv[k, m, t, pl.ds(r, BR), :] = new
-            pressure_rows(following, later, b, BR)
-            return carry
+                    gsum[1, m, t, pl.ds(r, SB), :] += gv
+                    new = v[t] + gv + before * cv[m, t, pl.ds(r, SB), :]
+                    cv[m, t, pl.ds(r, SB), :] = new
+                    tv[k, m, t, pl.ds(r, SB), :] = new
+            pressure_rows(following, later, b, SB)
         lax.fori_loop(0, ROWS // BR, block, 0)
 
     def first_pressure(i, carry):
@@ -748,7 +751,8 @@
     for copy in edges:
         copy.wait()
 
-    BR = 64
+    BR = 128
+    SB = 16
 
     def level(c, kk):
         k = c * CHUNK + kk
@@ -756,37 +760,39 @@
         before = table[0, k]
 
         def block(i, carry):
-            r = pl.multiple_of(i * BR, BR)
-            b = pl.multiple_of(8 + i * BR, 8)
-            wet = [kmask[0, t, pl.ds(r, BR), :] > level_no for t in range(2)]
-            packed = cols[c, pl.ds(b, BR), :]
+            for q in range(0, BR, SB):
+                piece(pl.multiple_of(i * BR + q, SB), pl.multiple_of(8 + i * BR + q, 8))
+            return carry
+
+        def piece(r, b):
+            wet = [kmask[0, t, pl.ds(r, SB), :] > level_no for t in range(2)]
+            packed = cols[c, pl.ds(b, SB), :]
             for m in range(2):
                 j = kk * 2 + m
-                u = [buf[0, k, m, t, pl.ds(b, BR), :] for t in range(2)]
-                v = [buf[1, k, m, t, pl.ds(b, BR), :] for t in range(2)]
-                vs = [buf[1, k, m, t, pl.ds(b - 1, BR), :] for t in range(2)]
+                u = [buf[0, k, m, t, pl.ds(b, SB), :] for t in range(2)]
+                v = [buf[1, k, m, t, pl.ds(b, SB), :] for t in range(2)]
+                vs = [buf[1, k, m, t, pl.ds(b - 1, SB), :] for t in range(2)]
                 uw = west_pair(*u, halo(packed, j))
                 for f, ref in ((2, tt), (3, ts)):
-                    q = [buf[f, k, m, t, pl.ds(b, BR), :] for t in range(2)]
+                    q = [buf[f, k, m, t, pl.ds(b, SB), :] for t in range(2)]
                     edge = halo(packed, f * PAIRS + j)
                     qe, qw = east_pair(*q, edge), west_pair(*q, edge)
                     for t in range(2):
                         lane = slice(t * LN, (t + 1) * LN)
-                        fy = v[t] * (q[t] + buf[f, k, m, t, pl.ds(b + 1, BR), :])
-                        fs = vs[t] * (q[t] + buf[f, k, m, t, pl.ds(b - 1, BR), :])
+                        fy = v[t] * (q[t] + buf[f, k, m, t, pl.ds(b + 1, SB), :])
+                        fs = vs[t] * (q[t] + buf[f, k, m, t, pl.ds(b - 1, SB), :])
                         adv = q[t] - 0.5 * ((u[t] * (q[t] + qe[t]) - uw[t] * (q[t] + qw[t])) + (fy - fs))
                         adv = jnp.where(wet[t], adv, 0.0)
-                        new = adv + before * ct[f - 2, m, t, pl.ds(r, BR), :]
-                        ct[f - 2, m, t, pl.ds(r, BR), :] = new
-                        ref[k, m, pl.ds(r, BR), lane] = new
+                        new = adv + before * ct[f - 2, m, t, pl.ds(r, SB), :]
+                        ct[f - 2, m, t, pl.ds(r, SB), :] = new
+                        ref[k, m, pl.ds(r, SB), lane] = new
             for t in range(2):
                 lane = slice(t * LN, (t + 1) * LN)
-                wet_x = kmask[1, t, pl.ds(r, BR), :] > level_no
-                wet_y = kmask[2, t, pl.ds(r, BR), :] > level_no
+                wet_x = kmask[1, t, pl.ds(r, SB), :] > level_no
+                wet_y = kmask[2, t, pl.ds(r, SB), :] > level_no
                 for m in range(2):
-                    su[k, m, pl.ds(r, BR), lane] = jnp.where(wet_x, su[k, m, pl.ds(r, BR), lane] + corr[0, m, t, pl.ds(r, BR), :], 0.0)
-                    sv[k, m, pl.ds(r, BR), lane] = jnp.where(wet_y, sv[k, m, pl.ds(r, BR), lane] + corr[1, m, t, pl.ds(r, BR), :], 0.0)
-            return carry
+                    su[k, m, pl.ds(r, SB), lane] = jnp.where(wet_x, su[k, m, pl.ds(r, SB), lane] + corr[0, m, t, pl.ds(r, SB), :], 0.0)
+                    sv[k, m, pl.ds(r, SB), lane] = jnp.where(wet_y, sv[k, m, pl.ds(r, SB), lane] + corr[1, m, t, pl.ds(r, SB), :], 0.0)
         lax.fori_loop(0, ROWS // BR, block, 0)
 
     def chunk_step(c, carry):

time: 77.1 us -> 70.4 us (0.913)
  Pallas kernels: 76.4 us -> 69.7 us
    pallas_call x1, Pallas kernels: 51.5 us -> 48 us  [local_step(): momentum(vel_x, vel_y, pot_temp, salinity, surf_eta, trans_x, trans_y, co...]
    pallas_call x1, Pallas kernels: 24.9 us -> 21.7 us  [local_step(): tracers(vel_x, vel_y, pot_temp, salinity, star_x, star_y, eta, tx, ty, co...]
where the time goes in v3:
time: 70.4 us; the launch traced here: 70.3 us
  Pallas kernels  69.7 us (99%)
    pallas_call x1, Pallas kernels, local_step(): momentum(vel_x, vel_y, pot_temp, salinity, surf_eta, trans_x, trans_y, co...  48 us
    pallas_call x1, Pallas kernels, local_step(): tracers(vel_x, vel_y, pot_temp, salinity, star_x, star_y, eta, tx, ty, co...  21.7 us

profile of v3, /device:TPU:0, one launch (start us, length us, event | category | flops | bytes accessed | tf_op | source)
XLA Modules:
  0.0 70.3 jit_solution(9538238219976773003)
XLA Ops:
  0.6 48.0 %momentum.1 = (f32[20,2,128,256]{3,2,1,0:T(8,128)}, f32[20,2,128,256]{3,2,1,0:T(8,128)}, f32[2,128,256]{2,1,0:T(8,128)}, f32[2,128,256]{2,1,0:T(8,128)}, f32[2,1...) custom-call(f32[20,2,128,256]{3,2,1,0:T(8,128)} %u_hbm.3, ...), custom_call_target="tpu_custom_call" | custom-call | tf_op jit(solution)/shard_map/momentum/pallas_call | solution.py:909
  48.6 21.7 %tracers.1 = (f32[2,128,256]{2,1,0:T(8,128)}, f32[2,128,256]{2,1,0:T(8,128)}, f32[2,128,256]{2,1,0:T(8,128)}, f32[20,2,128,256]{3,2,1,0:T(8,128)}, f32[20,2,128,...) custom-call(f32[20,2,128,256]{3,2,1,0:T(8,128)} %u_hbm.3, f32[20,2,128,256]{3,2,1,0:T(8,128)} %v_hbm.3, ...), custom_call_target="tpu_custom_call" | custom-call | tf_op jit(solution)/shard_map/tracers/pallas_call | solution.py:911

commit v4 on v3

--- a/solution.py
+++ b/solution.py
@@ -74,12 +74,13 @@
     return jnp.where(origin, edge, a), jnp.where(origin, a, b)
 
 
-def momentum_kernel(u_hbm, v_hbm, t_hbm, s_hbm, eta_hbm, tx_hbm, ty_hbm, h_hbm, kmt_ref, weights, table,
-                    us_hbm, vs_hbm, eta_out, tx_out, ty_out, corr_out, kmask_out, col_out, rows_out,
-                    buf, tu, tv, cu, cv, pbuf, pacc, phal, rhoc, gsum, xsum, ku, kv,
+def momentum_kernel(u_hbm, v_hbm, t_hbm, s_hbm, eta_hbm, tx_hbm, ty_hbm, h_hbm, kmt_hbm, weights, table,
+                    us_hbm, vs_hbm, eta_out, tx_out, ty_out, corr_out, kmask_out, col_out, own_out, rows_out,
+                    buf, tu, tv, cu, cv, pbufa, pbufb, pacc, phal, rhoc, gsum, xsum, kmask, kmt, vep, uwp, dup, txb, tyb, corr,
                     send_col, recv_col, send_row, recv_row,
                     xb, sp, rp, xf, sf, rf, hux, huy, ae, aw, an, as_, cc, ebufa, ebufb, dbuf, gbuf, eacc, bacc,
-                    ld_sem, xl_sem, cs_sem, cr_sem, xs_sem, xr_sem, fs_sem, fr_sem, st_sem, ot_sem):
+                    ld_sem, xl_sem, cs_sem, cr_sem, xs_sem, xr_sem, fs_sem, fr_sem, st_sem, ot_sem, av_sem):
+    ku, kv = kmask.at[1], kmask.at[2]
     me_c = lax.axis_index("col")
     me_r = lax.axis_index("row")
     peer = 1 - me_c
@@ -96,16 +97,15 @@
                     buf.at[f, pl.ds(c * CHUNK, CHUNK), :, t, pl.ds(8, ROWS), :], ld_sem.at[c, f * 2 + t]))
         return out
 
-    def ext_loads():
-        out = []
-        for t in range(2):
-            lane = pl.ds(t * LN, LN)
-            out.append(pltpu.make_async_copy(h_hbm.at[:, lane], xb.at[1, t, pl.ds(32, ROWS), :], xl_sem.at[t]))
-            for i, ref in enumerate((eta_hbm, tx_hbm, ty_hbm)):
-                out.append(pltpu.make_async_copy(ref.at[:, :, lane], xb.at[pl.ds(2 + 2 * i, 2), t, pl.ds(32, ROWS), :], xl_sem.at[2 + 2 * i + t]))
-        return out
-
-    for copy in loads(0) + ext_loads() + loads(1):
+    def map_loads():
+        return [pltpu.make_async_copy(kmt_hbm, kmt, xl_sem.at[8])] + [
+            pltpu.make_async_copy(h_hbm.at[:, pl.ds(t * LN, LN)], xb.at[1, t, pl.ds(32, ROWS), :], xl_sem.at[t]) for t in range(2)]
+
+    def flow_loads():
+        return [pltpu.make_async_copy(ref.at[:, :, pl.ds(t * LN, LN)], xb.at[pl.ds(2 + 2 * i, 2), t, pl.ds(32, ROWS), :], xl_sem.at[2 + 2 * i + t])
+                for t in range(2) for i, ref in enumerate((eta_hbm, tx_hbm, ty_hbm))]
+
+    for copy in map_loads() + loads(0) + loads(1) + loads(2) + flow_loads():
         copy.start()
 
     barrier = pltpu.get_barrier_semaphore()
@@ -186,11 +186,13 @@
         return carry
     lax.fori_loop(0, ROWS // 16, zero_planes2, 0)
 
+    for copy in map_loads():
+        copy.wait()
     for t in range(2):
-        for r in range(0, ROWS, 32):
-            xb[0, t, 32 + r:64 + r, :] = kmt_ref[r:r + 32, t * LN:(t + 1) * LN].astype(F32)
-    for copy in ext_loads():
-        copy.wait()
+        for r in range(0, ROWS, 64):
+            level_count = kmt[r:r + 64, t * LN:(t + 1) * LN].astype(F32)
+            xb[0, t, 32 + r:96 + r, :] = level_count
+            kmask[0, t, r:r + 64, :] = level_count
 
     @pl.when((me_r == 0) | (me_r == 3))
     def _():
@@ -204,14 +206,28 @@
         return pltpu.make_async_remote_copy(src_ref=src, dst_ref=dst, send_sem=ssem, recv_sem=rsem,
                                             device_id={"col": col, "row": row}, device_id_type=MESH_ID)
 
-    def wide_copies(own, packed, landing, ssem, rsem):
-        north, south = me_r + 1, me_r - 1
+    def wide_rows(own, first, count, ssem, rsem, slot):
+        fields = pl.ds(first, count)
+        return ((remote(own.at[fields, pl.ds(0, 2), pl.ds(136, 24), :], own.at[fields, pl.ds(0, 2), pl.ds(8, 24), :],
+                        ssem.at[slot], rsem.at[slot], me_c, me_r + 1),),
+                (remote(own.at[fields, pl.ds(0, 2), pl.ds(32, 24), :], own.at[fields, pl.ds(0, 2), pl.ds(160, 24), :],
+                        ssem.at[slot + 1], rsem.at[slot + 1], me_c, me_r - 1),))
+
+    def wide_copies(own, first, count, packed, landing, ssem, rsem):
         side = remote(packed, landing.at[:, pl.ds(32, ROWS), :], ssem.at[0], rsem.at[0], peer, me_r)
-        up = (remote(own.at[:, pl.ds(0, 2), pl.ds(136, 24), :], own.at[:, pl.ds(0, 2), pl.ds(8, 24), :], ssem.at[1], rsem.at[1], me_c, north),
-              remote(packed.at[:, pl.ds(104, 24), :], landing.at[:, pl.ds(8, 24), :], ssem.at[2], rsem.at[2], peer, north))
-        down = (remote(own.at[:, pl.ds(0, 2), pl.ds(32, 24), :], own.at[:, pl.ds(0, 2), pl.ds(160, 24), :], ssem.at[3], rsem.at[3], me_c, south),
-                remote(packed.at[:, pl.ds(0, 24), :], landing.at[:, pl.ds(160, 24), :], ssem.at[4], rsem.at[4], peer, south))
+        up, down = wide_rows(own, first, count, ssem, rsem, 1)
+        up += (remote(packed.at[:, pl.ds(104, 24), :], landing.at[:, pl.ds(8, 24), :], ssem.at[3], rsem.at[3], peer, me_r + 1),)
+        down += (remote(packed.at[:, pl.ds(0, 24), :], landing.at[:, pl.ds(160, 24), :], ssem.at[4], rsem.at[4], peer, me_r - 1),)
         return side, up, down
+
+    def map_copies():
+        return (None, *wide_rows(xb, 0, 2, xs_sem, xr_sem, 5))
+
+    def flow_copies():
+        return wide_copies(xb, 2, 6, sp, rp, xs_sem, xr_sem)
+
+    def force_copies():
+        return wide_copies(xf, 0, 4, sf, rf, fs_sem, fr_sem)
 
     def edge_copies(c):
         north, south = me_r + 1, me_r - 1
@@ -254,7 +270,8 @@
 
     def wait_send_all(copies):
         side, up, down = copies
-        side.wait_send()
+        if side is not None:
+            side.wait_send()
 
         @pl.when(has_n)
         def _():
@@ -266,13 +283,7 @@
             for copy in down:
                 copy.wait_send()
 
-    def rows_only(copies):
-        return None, copies[1][:1], copies[2][:1]
-
-    def columns_only(copies):
-        return copies[0], copies[1][1:], copies[2][1:]
-
-    start_all(rows_only(wide_copies(xb, sp, rp, xs_sem, xr_sem)))
+    start_all(map_copies())
 
     def pack_and_send(c, with_maps=False):
         for copy in loads(c):
@@ -306,8 +317,6 @@
         start_all(edge_copies(c))
 
     pack_and_send(0, with_maps=True)
-    for copy in loads(2):
-        copy.start()
     pack_and_send(1)
 
     RHO_T = np.float32(-THERM_EXP * PRESS_SCALE / LEVELS / 2)
@@ -323,9 +332,22 @@
                 slot[m, t, pl.ds(base, rows), :] = p
                 pacc[m, t, pl.ds(base, rows), :] = p + half
 
+    def shift_u(c, kk, m, base, rows):
+        u = [buf[0, c * CHUNK + kk, m, t, pl.ds(base, rows), :] for t in range(2)]
+        edge = halo(recv_col[c, pl.ds(base, rows), :], kk * 2 + m)
+        ue, uw = east_pair(*u, edge), west_pair(*u, edge)
+        for t in range(2):
+            uwp[m, t, pl.ds(base, rows), :] = uw[t]
+            dup[m, t, pl.ds(base, rows), :] = ue[t] - uw[t]
+
     def level(c, kk, now, later):
         k = c * CHUNK + kk
         pressure_rows(k, now, 8 + ROWS, 8)
+        for m in range(2):
+            shift_u(c, kk, m, 8, 8)
+            ve = east_pair(*(buf[1, k, m, t, 0:8, :] for t in range(2)), halo(recv_col[c, 0:8, :], PAIRS + kk * 2 + m))
+            for t in range(2):
+                vep[m, t, 0:8, :] = ve[t]
         level_no = k.astype(F32)
         before = table[0, k]
         following = jnp.minimum(k + 1, LEVELS - 1)
@@ -339,37 +361,35 @@
             wet_x = [ku[t, pl.ds(r, SB), :] > level_no for t in range(2)]
             wet_y = [kv[t, pl.ds(r, SB), :] > level_no for t in range(2)]
             packed = recv_col[c, pl.ds(b, SB), :]
-            packed_w = packed + recv_col[c, pl.ds(b - 1, SB), :]
-            packed_z = packed + recv_col[c, pl.ds(b + 1, SB), :]
             packed_r = rhoc[pl.ds(r, SB), :]
             for m in range(2):
                 j = kk * 2 + m
+                shift_u(c, kk, m, pl.multiple_of(b + 8, 8), SB)
                 half = halo(packed_r, j)
                 p_edge = phal[m, pl.ds(r, SB), :] + half
                 phal[m, pl.ds(r, SB), :] = p_edge + half
-                u_edge, v_edge = halo(packed, j), halo(packed, PAIRS + j)
-                w_edge, z_edge = halo(packed_w, PAIRS + j), halo(packed_z, j)
-                u = [buf[0, k, m, t, pl.ds(b, SB), :] for t in range(2)]
                 v = [buf[1, k, m, t, pl.ds(b, SB), :] for t in range(2)]
-                un = [buf[0, k, m, t, pl.ds(b + 1, SB), :] for t in range(2)]
-                vs = [buf[1, k, m, t, pl.ds(b - 1, SB), :] for t in range(2)]
                 p = [now[m, t, pl.ds(b, SB), :] for t in range(2)]
-                w = [v[t] + vs[t] for t in range(2)]
-                z = [u[t] + un[t] for t in range(2)]
-                ue, uw = east_pair(*u, u_edge), west_pair(*u, u_edge)
+                v_edge = halo(packed, PAIRS + j)
                 ve, vw = east_pair(*v, v_edge), west_pair(*v, v_edge)
-                pe, we, zw = east_pair(*p, p_edge), east_pair(*w, w_edge), west_pair(*z, z_edge)
+                pe = east_pair(*p, p_edge)
                 for t in range(2):
+                    vep[m, t, pl.ds(b, SB), :] = ve[t]
+                    u = buf[0, k, m, t, pl.ds(b, SB), :]
+                    un = buf[0, k, m, t, pl.ds(b + 1, SB), :]
                     us = buf[0, k, m, t, pl.ds(b - 1, SB), :]
-                    gu = (p[t] - pe[t]) - (0.5 * u[t]) * (ue[t] - uw[t]) - (0.125 * (w[t] + we[t])) * (un[t] - us)
+                    vs = buf[1, k, m, t, pl.ds(b - 1, SB), :]
+                    vn = buf[1, k, m, t, pl.ds(b + 1, SB), :]
+                    pn = now[m, t, pl.ds(b + 1, SB), :]
+                    w = (v[t] + vs) + (ve[t] + vep[m, t, pl.ds(b - 1, SB), :])
+                    z = (u + un) + (uwp[m, t, pl.ds(b, SB), :] + uwp[m, t, pl.ds(b + 1, SB), :])
+                    gu = (p[t] - pe[t]) - (0.5 * u) * dup[m, t, pl.ds(b, SB), :] - (0.125 * w) * (un - us)
                     gu = jnp.where(wet_x[t], gu, 0.0)
                     gsum[0, m, t, pl.ds(r, SB), :] += gu
-                    new = u[t] + gu + before * cu[m, t, pl.ds(r, SB), :]
+                    new = u + gu + before * cu[m, t, pl.ds(r, SB), :]
                     cu[m, t, pl.ds(r, SB), :] = new
                     tu[k, m, t, pl.ds(r, SB), :] = new
-                    vn = buf[1, k, m, t, pl.ds(b + 1, SB), :]
-                    pn = now[m, t, pl.ds(b + 1, SB), :]
-                    gv = (p[t] - pn) - (0.125 * (z[t] + zw[t])) * (ve[t] - vw[t]) - (0.5 * v[t]) * (vn - vs[t])
+                    gv = (p[t] - pn) - (0.125 * z) * (ve[t] - vw[t]) - (0.5 * v[t]) * (vn - vs)
                     gv = jnp.where(wet_y[t], gv, 0.0)
                     gsum[1, m, t, pl.ds(r, SB), :] += gv
                     new = v[t] + gv + before * cv[m, t, pl.ds(r, SB), :]
@@ -379,7 +399,7 @@
         lax.fori_loop(0, ROWS // BR, block, 0)
 
     def first_pressure(i, carry):
-        pressure_rows(0, pbuf.at[0], pl.multiple_of(8 + i * 64, 8), 64)
+        pressure_rows(0, pbufa, pl.multiple_of(8 + i * 64, 8), 64)
         return carry
     lax.fori_loop(0, 2, first_pressure, 0)
 
@@ -415,20 +435,22 @@
         rhoc[...] = RHO_T * pltpu.roll(packed, LN - 4 * PAIRS, 1) + RHO_S * pltpu.roll(packed, LN - 6 * PAIRS, 1)
 
         def two_levels(h, carry2):
-            level(c, 2 * h, pbuf.at[0], pbuf.at[1])
-            level(c, 2 * h + 1, pbuf.at[1], pbuf.at[0])
+            level(c, 2 * h, pbufa, pbufb)
+            level(c, 2 * h + 1, pbufb, pbufa)
             return carry2
         lax.fori_loop(0, CHUNK // 2, two_levels, 0)
         return carry
 
     def pack_wide():
+        for copy in flow_loads():
+            copy.wait()
         for pair in range(4):
             pack_pair(lambda t, r, p=pair: xb[2 * p, t, pl.ds(32 + r, 64), :],
                       lambda t, r, p=pair: xb[2 * p + 1, t, pl.ds(32 + r, 64), :], sp, pair, 64)
-        start_all(columns_only(wide_copies(xb, sp, rp, xs_sem, xr_sem)))
+        start_all(flow_copies())
 
     def face_maps():
-        wait_recv_all(rows_only(wide_copies(xb, sp, rp, xs_sem, xr_sem)))
+        wait_recv_all(map_copies())
 
         def maps(i, carry):
             r = pl.multiple_of(i * 64, 64)
@@ -442,9 +464,6 @@
                 ky = jnp.minimum(kt[t], xb[0, t, pl.ds(33 + r, 64), :])
                 ku[t, pl.ds(r, 64), :] = kx
                 kv[t, pl.ds(r, 64), :] = ky
-                kmask_out[0, t, pl.ds(r, 64), :] = kt[t]
-                kmask_out[1, t, pl.ds(r, 64), :] = kx
-                kmask_out[2, t, pl.ds(r, 64), :] = ky
                 hux[t, pl.ds(32 + r, 64), :] = jnp.where(kx > 0.0, 0.5 * (ht[t] + he[t]), 0.0)
                 huy[t, pl.ds(32 + r, 64), :] = jnp.where(ky > 0.0, 0.5 * (ht[t] + xb[1, t, pl.ds(33 + r, 64), :]), 0.0)
             return carry
@@ -464,8 +483,8 @@
 
     lax.fori_loop(0, NCH, chunk_step, 0)
 
-    packet_copies = [pltpu.make_async_copy(recv_col, col_out, ot_sem.at[0]),
-                     pltpu.make_async_copy(recv_row, rows_out, ot_sem.at[1])]
+    packet_copies = [pltpu.make_async_copy(src, dst, ot_sem.at[i]) for i, (src, dst) in enumerate(
+        ((recv_col, col_out), (recv_row, rows_out), (kmask, kmask_out), (send_col, own_out)))]
     for copy in packet_copies:
         copy.start()
 
@@ -484,7 +503,7 @@
     for m in range(2):
         pack_pair(lambda t, r, m=m: xf[m, t, pl.ds(32 + r, 64), :],
                   lambda t, r, m=m: xf[2 + m, t, pl.ds(32 + r, 64), :], sf, m, 64)
-    start_all(wide_copies(xf, sf, rf, fs_sem, fr_sem))
+    start_all(force_copies())
 
     def stores(c):
         out = []
@@ -521,7 +540,7 @@
         return carry
     lax.fori_loop(0, NCH, upward, 0)
 
-    wait_recv_all(columns_only(wide_copies(xb, sp, rp, xs_sem, xr_sem)))
+    wait_recv_all(flow_copies())
 
     def unpack_wide(i, carry):
         r = pl.multiple_of(i * 32, 32)
@@ -584,7 +603,7 @@
         return carry
     lax.fori_loop(0, 2, first_block, 0)
 
-    wait_recv_all(wide_copies(xf, sf, rf, fs_sem, fr_sem))
+    wait_recv_all(force_copies())
 
     def unpack_force(i, carry):
         r = pl.multiple_of(i * 32, 32)
@@ -656,39 +675,57 @@
             return subcycle(n + 1, carry, lo, hi, ebufa, ebufb)
         tail = lax.fori_loop(0, steps, two_cycles, tail)
 
+    eta_copies = [pltpu.make_async_copy(eacc.at[:, t, pl.ds(0, ROWS), :], eta_out.at[:, :, pl.ds(t * LN, LN)], ot_sem.at[4 + t]) for t in range(2)]
+    for copy in eta_copies:
+        copy.start()
+
+    AV = 64
+
+    def average_copies(i):
+        r = pl.multiple_of(i * AV, AV)
+        return [pltpu.make_async_copy(src, dst, av_sem.at[i, n]) for n, (src, dst) in enumerate((
+            (txb.at[:, pl.ds(r, AV), :], tx_out.at[:, pl.ds(r, AV), :]), (tyb.at[:, pl.ds(r, AV), :], ty_out.at[:, pl.ds(r, AV), :]),
+            (corr.at[:, :, :, pl.ds(r, AV), :], corr_out.at[:, :, :, pl.ds(r, AV), :])))]
+
     def averages(i, carry):
-        r = pl.multiple_of(i * 16, 16)
-        g = pl.multiple_of(32 + i * 16, 16)
-        for t in range(2):
-            depth_x = hux[t, pl.ds(g, 16), :]
-            depth_y = huy[t, pl.ds(g, 16), :]
-            kx = ku[t, pl.ds(r, 16), :]
-            ky = kv[t, pl.ds(r, 16), :]
-            inv_x = 1.0 / (depth_x + jnp.where(kx > 0.0, 0.0, 1.0))
-            inv_y = 1.0 / (depth_y + jnp.where(ky > 0.0, 0.0, 1.0))
-            mean_x = 1.0 / jnp.maximum(kx, 1.0)
-            mean_y = 1.0 / jnp.maximum(ky, 1.0)
-            for m in range(2):
-                lane = slice(t * LN, (t + 1) * LN)
-                acc = bacc[m, t, pl.ds(r, 16), :]
-                eta_out[m, pl.ds(r, 16), lane] = eacc[m, t, pl.ds(r, 16), :]
-                tx = whole * xb[4 + m, t, pl.ds(g, 16), :] + moment * xf[m, t, pl.ds(g, 16), :] \
-                    - WAVE_COURANT * depth_x * (east(acc, bacc[m, NEXT[t], pl.ds(r, 16), :]) - acc)
-                ty = whole * xb[6 + m, t, pl.ds(g, 16), :] + moment * xf[2 + m, t, pl.ds(g, 16), :] \
-                    - WAVE_COURANT * depth_y * (bacc[m, t, pl.ds(r + 1, 16), :] - acc)
-                tx = jnp.where(kx > 0.0, tx, 0.0)
-                ty = jnp.where(ky > 0.0, ty, 0.0)
-                tx_out[m, pl.ds(r, 16), lane] = tx
-                ty_out[m, pl.ds(r, 16), lane] = ty
-                corr_out[0, m, t, pl.ds(r, 16), :] = tx * inv_x - xsum[0, m, t, pl.ds(r, 16), :] * mean_x
-                corr_out[1, m, t, pl.ds(r, 16), :] = ty * inv_y - xsum[1, m, t, pl.ds(r, 16), :] * mean_y
-        return carry
-    lax.fori_loop(0, ROWS // 16, averages, 0)
-
-    wait_send_all(wide_copies(xb, sp, rp, xs_sem, xr_sem))
-    wait_send_all(wide_copies(xf, sf, rf, fs_sem, fr_sem))
-    for copy in packet_copies:
+        for q in range(0, AV, 16):
+            r = pl.multiple_of(i * AV + q, 16)
+            g = pl.multiple_of(32 + i * AV + q, 16)
+            for t in range(2):
+                depth_x = hux[t, pl.ds(g, 16), :]
+                depth_y = huy[t, pl.ds(g, 16), :]
+                kx = ku[t, pl.ds(r, 16), :]
+                ky = kv[t, pl.ds(r, 16), :]
+                inv_x = 1.0 / (depth_x + jnp.where(kx > 0.0, 0.0, 1.0))
+                inv_y = 1.0 / (depth_y + jnp.where(ky > 0.0, 0.0, 1.0))
+                mean_x = 1.0 / jnp.maximum(kx, 1.0)
+                mean_y = 1.0 / jnp.maximum(ky, 1.0)
+                for m in range(2):
+                    lane = slice(t * LN, (t + 1) * LN)
+                    acc = bacc[m, t, pl.ds(r, 16), :]
+                    tx = whole * xb[4 + m, t, pl.ds(g, 16), :] + moment * xf[m, t, pl.ds(g, 16), :] \
+                        - WAVE_COURANT * depth_x * (east(acc, bacc[m, NEXT[t], pl.ds(r, 16), :]) - acc)
+                    ty = whole * xb[6 + m, t, pl.ds(g, 16), :] + moment * xf[2 + m, t, pl.ds(g, 16), :] \
+                        - WAVE_COURANT * depth_y * (bacc[m, t, pl.ds(r + 1, 16), :] - acc)
+                    tx = jnp.where(kx > 0.0, tx, 0.0)
+                    ty = jnp.where(ky > 0.0, ty, 0.0)
+                    txb[m, pl.ds(r, 16), lane] = tx
+                    tyb[m, pl.ds(r, 16), lane] = ty
+                    corr[0, m, t, pl.ds(r, 16), :] = tx * inv_x - xsum[0, m, t, pl.ds(r, 16), :] * mean_x
+                    corr[1, m, t, pl.ds(r, 16), :] = ty * inv_y - xsum[1, m, t, pl.ds(r, 16), :] * mean_y
+        for copy in average_copies(i):
+            copy.start()
+        return carry
+    lax.fori_loop(0, ROWS // AV, averages, 0)
+
+    wait_send_all(map_copies())
+    wait_send_all(flow_copies())
+    wait_send_all(force_copies())
+    for copy in packet_copies + eta_copies:
         copy.wait()
+    for i in range(ROWS // AV):
+        for copy in average_copies(i):
+            copy.wait()
 
     def drain(c, carry):
         wait_send_all(edge_copies(c))
@@ -698,9 +735,9 @@
     lax.fori_loop(0, NCH, drain, 0)
 
 
-def tracer_kernel(u_hbm, v_hbm, t_hbm, s_hbm, us_hbm, vs_hbm, eta_in, tx_in, ty_in, corr_in, kmask_in, col_in, rows_in, table,
+def tracer_kernel(u_hbm, v_hbm, t_hbm, s_hbm, us_hbm, vs_hbm, eta_in, tx_in, ty_in, corr_in, kmask_in, col_in, own_in, rows_in, table,
                   eta_hbm, tx_hbm, ty_hbm, un_hbm, vn_hbm, tn_hbm, sn_hbm,
-                  buf, tt, ts, ct, su, sv, small, corr, kmask, cols, rows, ld_sem, ed_sem, st_sem, in_sem, out_sem):
+                  buf, tt, ts, ct, su, sv, small, corr, kmask, cols, own, rows, qcol, ld_sem, ed_sem, st_sem, in_sem, out_sem):
     hbm = (u_hbm, v_hbm, t_hbm, s_hbm)
     sources = (eta_in, tx_in, ty_in)
     sinks = (eta_hbm, tx_hbm, ty_hbm)
@@ -725,7 +762,7 @@
                 for f, (src, dst) in enumerate(((tt, tn_hbm), (ts, sn_hbm)))]
 
     edges = [pltpu.make_async_copy(src, dst, ed_sem.at[i])
-             for i, (src, dst) in enumerate(((col_in, cols), (rows_in, rows), (corr_in, corr), (kmask_in, kmask)))]
+             for i, (src, dst) in enumerate(((col_in, cols), (rows_in, rows), (corr_in, corr), (kmask_in, kmask), (own_in, own)))]
     for copy in edges:
         copy.start()
     for c in range(NCH):
@@ -766,22 +803,23 @@
 
         def piece(r, b):
             wet = [kmask[0, t, pl.ds(r, SB), :] > level_no for t in range(2)]
-            packed = cols[c, pl.ds(b, SB), :]
+            packed = qcol[pl.ds(r, SB), :]
             for m in range(2):
                 j = kk * 2 + m
                 u = [buf[0, k, m, t, pl.ds(b, SB), :] for t in range(2)]
                 v = [buf[1, k, m, t, pl.ds(b, SB), :] for t in range(2)]
                 vs = [buf[1, k, m, t, pl.ds(b - 1, SB), :] for t in range(2)]
-                uw = west_pair(*u, halo(packed, j))
                 for f, ref in ((2, tt), (3, ts)):
                     q = [buf[f, k, m, t, pl.ds(b, SB), :] for t in range(2)]
                     edge = halo(packed, f * PAIRS + j)
-                    qe, qw = east_pair(*q, edge), west_pair(*q, edge)
+                    qe = east_pair(*q, edge)
+                    fx = [u[t] * (q[t] + qe[t]) for t in range(2)]
+                    fw = west_pair(*fx, edge)
                     for t in range(2):
                         lane = slice(t * LN, (t + 1) * LN)
                         fy = v[t] * (q[t] + buf[f, k, m, t, pl.ds(b + 1, SB), :])
                         fs = vs[t] * (q[t] + buf[f, k, m, t, pl.ds(b - 1, SB), :])
-                        adv = q[t] - 0.5 * ((u[t] * (q[t] + qe[t]) - uw[t] * (q[t] + qw[t])) + (fy - fs))
+                        adv = q[t] - 0.5 * ((fx[t] - fw[t]) + (fy - fs))
                         adv = jnp.where(wet[t], adv, 0.0)
                         new = adv + before * ct[f - 2, m, t, pl.ds(r, SB), :]
                         ct[f - 2, m, t, pl.ds(r, SB), :] = new
@@ -808,6 +846,12 @@
                 for f in (2, 3):
                     for t in range(2):
                         buf[f, k, m, t, 8 + ROWS:9 + ROWS, :] = rows[1, c, t, f, jj:jj + 1, :]
+
+        packed = cols[c, 8:8 + ROWS, :]
+        lane = lanes(ROWS)
+        west_u = jnp.where(lane < 6 * PAIRS, pltpu.roll(packed, 4 * PAIRS, 1), pltpu.roll(packed, 6 * PAIRS, 1))
+        flux = west_u * (packed + pltpu.roll(own[c], 1, 1))
+        qcol[...] = jnp.where(lax.rem(lane, 2) == 1, flux, packed)
 
         def one_level(kk, carry2):
             level(c, kk)
@@ -874,18 +918,19 @@
         momentum_kernel,
         name="momentum",
         out_shape=(shape(*full), shape(*full), shape(*flat), shape(*flat), shape(*flat), shape(2, 2, 2, ROWS, LN),
-                   shape(3, 2, ROWS, LN), shape(NCH, PR, LN), shape(2, NCH, 2, 4, PAIRS, LN)),
-        in_specs=[any_spec] * 8 + [vmem_spec, smem_spec, smem_spec],
-        out_specs=(any_spec, any_spec, vmem_spec, vmem_spec, vmem_spec, vmem_spec, vmem_spec, any_spec, any_spec),
+                   shape(3, 2, ROWS, LN), shape(NCH, PR, LN), shape(NCH, ROWS, LN), shape(2, NCH, 2, 4, PAIRS, LN)),
+        in_specs=[any_spec] * 9 + [smem_spec, smem_spec],
+        out_specs=(any_spec,) * 10,
         scratch_shapes=[
             vm(4, LEVELS, 2, 2, PR, LN), vm(LEVELS + 1, 2, 2, ROWS, LN), vm(LEVELS + 1, 2, 2, ROWS, LN),
-            vm(2, 2, ROWS, LN), vm(2, 2, ROWS, LN), vm(2, 2, 2, PR, LN), vm(2, 2, PR, LN), vm(2, PR, LN), vm(ROWS, LN),
-            vm(2, 2, 2, ROWS, LN), vm(2, 2, 2, ROWS, LN), vm(2, ROWS, LN), vm(2, ROWS, LN),
+            vm(2, 2, ROWS, LN), vm(2, 2, ROWS, LN), vm(2, 2, PR, LN), vm(2, 2, PR, LN), vm(2, 2, PR, LN), vm(2, PR, LN), vm(ROWS, LN),
+            vm(2, 2, 2, ROWS, LN), vm(2, 2, 2, ROWS, LN), vm(3, 2, ROWS, LN), pltpu.VMEM((ROWS, 2 * LN), jnp.int32),
+            vm(2, 2, PR, LN), vm(2, 2, PR, LN), vm(2, 2, PR, LN), vm(*flat), vm(*flat), vm(2, 2, 2, ROWS, LN),
             vm(NCH, ROWS, LN), vm(NCH, PR, LN), vm(2, NCH, 2, 4, PAIRS, LN), vm(2, NCH, 2, 4, PAIRS, LN),
             vm(8, 3, EXT, LN), vm(4, ROWS, LN), vm(4, EXT, LN), vm(4, 3, EXT, LN), vm(2, ROWS, LN), vm(2, EXT, LN),
             vm(3, EXT, LN), vm(3, EXT, LN), vm(3, EXT, LN), vm(3, EXT, LN), vm(3, EXT, LN), vm(3, EXT, LN), vm(3, EXT, LN),
             vm(2, 3, EXT, LN), vm(2, 3, EXT, LN), vm(2, 3, EXT, LN), vm(2, 3, EXT, LN), vm(2, 2, ROWS + 8, LN), vm(2, 3, ROWS + 8, LN),
-            dma(NCH, 8), dma(8), dma(NCH, 5), dma(NCH, 5), dma(5), dma(5), dma(5), dma(5), dma(NCH, 4), dma(2),
+            dma(NCH, 8), dma(9), dma(NCH, 5), dma(NCH, 5), dma(7), dma(7), dma(5), dma(5), dma(NCH, 4), dma(6), dma(2, 3),
         ],
         compiler_params=pltpu.CompilerParams(collective_id=0, has_side_effects=True, vmem_limit_bytes=67043328),
     )
@@ -894,21 +939,21 @@
         tracer_kernel,
         name="tracers",
         out_shape=(shape(*flat), shape(*flat), shape(*flat), shape(*full), shape(*full), shape(*full), shape(*full)),
-        in_specs=[any_spec] * 13 + [smem_spec],
+        in_specs=[any_spec] * 14 + [smem_spec],
         out_specs=(any_spec,) * 7,
         scratch_shapes=[
             vm(4, LEVELS, 2, 2, PR, LN), vm(LEVELS + 1, 2, ROWS, 2 * LN), vm(LEVELS + 1, 2, ROWS, 2 * LN), vm(2, 2, 2, ROWS, LN),
             vm(*full), vm(*full), vm(3, 2, ROWS, 2 * LN), vm(2, 2, 2, ROWS, LN), vm(3, 2, ROWS, LN),
-            vm(NCH, PR, LN), vm(2, NCH, 2, 4, PAIRS, LN),
-            dma(NCH, 10), dma(4), dma(NCH, 4), dma(3), dma(3),
+            vm(NCH, PR, LN), vm(NCH, ROWS, LN), vm(2, NCH, 2, 4, PAIRS, LN), vm(ROWS, LN),
+            dma(NCH, 10), dma(5), dma(NCH, 4), dma(3), dma(3),
         ],
         compiler_params=pltpu.CompilerParams(vmem_limit_bytes=67043328),
     )
 
     def local_step(vel_x, vel_y, pot_temp, salinity, surf_eta, trans_x, trans_y, col_depth, wet_levels, avg_weights):
-        star_x, star_y, eta, tx, ty, corr, kmask, cols, rows = momentum(
+        star_x, star_y, eta, tx, ty, corr, kmask, cols, own, rows = momentum(
             vel_x, vel_y, pot_temp, salinity, surf_eta, trans_x, trans_y, col_depth, wet_levels, avg_weights, jnp.asarray(visc))
-        return tracers(vel_x, vel_y, pot_temp, salinity, star_x, star_y, eta, tx, ty, corr, kmask, cols, rows, jnp.asarray(diff))
+        return tracers(vel_x, vel_y, pot_temp, salinity, star_x, star_y, eta, tx, ty, corr, kmask, cols, own, rows, jnp.asarray(diff))
 
     spec_3d = P(None, None, "row", "col")
     spec_2d = P(None, "row", "col")

time: 70.4 us -> 91.5 us (1.30)
  Pallas kernels: 69.7 us -> 90.7 us
    pallas_call x1, Pallas kernels: 21.7 us -> 45.2 us  [local_step(): tracers(vel_x, vel_y, pot_temp, salinity, star_x, star_y, eta, tx, ty, co...]
    pallas_call x1, Pallas kernels: 48 us -> 45.5 us  [local_step(): momentum(vel_x, vel_y, pot_temp, salinity, surf_eta, trans_x, trans_y, co...]
where the time goes in v4:
time: 91.5 us; the launch traced here: 91.4 us
  Pallas kernels  90.7 us (99%)
    pallas_call x1, Pallas kernels, local_step(): momentum(vel_x, vel_y, pot_temp, salinity, surf_eta, trans_x, trans_y, co...  45.5 us
    pallas_call x1, Pallas kernels, local_step(): tracers(vel_x, vel_y, pot_temp, salinity, star_x, star_y, eta, tx, ty, co...  45.2 us

profile of v4, /device:TPU:0, one launch (start us, length us, event | category | flops | bytes accessed | tf_op | source)
XLA Modules:
  0.0 91.4 jit_solution(18145288548399117529)
XLA Ops:
  0.6 45.5 %momentum.1 = (f32[20,2,128,256]{3,2,1,0:T(8,128)}, f32[20,2,128,256]{3,2,1,0:T(8,128)}, f32[2,128,256]{2,1,0:T(8,128)}, f32[2,128,256]{2,1,0:T(8,128)}, f32[2,1...) custom-call(f32[20,2,128,256]{3,2,1,0:T(8,128)} %u_hbm.3, ...), custom_call_target="tpu_custom_call" | custom-call | tf_op jit(solution)/shard_map/momentum/pallas_call | solution.py:954
  46.1 45.2 %tracers.1 = (f32[2,128,256]{2,1,0:T(8,128)}, f32[2,128,256]{2,1,0:T(8,128)}, f32[2,128,256]{2,1,0:T(8,128)}, f32[20,2,128,256]{3,2,1,0:T(8,128)}, f32[20,2,128,...) custom-call(f32[20,2,128,256]{3,2,1,0:T(8,128)} %u_hbm.3, f32[20,2,128,256]{3,2,1,0:T(8,128)} %v_hbm.3, ...), custom_call_target="tpu_custom_call" | custom-call | tf_op jit(solution)/shard_map/tracers/pallas_call | solution.py:956

commit v5 on v4

--- a/solution.py
+++ b/solution.py
@@ -75,7 +75,7 @@
 
 
 def momentum_kernel(u_hbm, v_hbm, t_hbm, s_hbm, eta_hbm, tx_hbm, ty_hbm, h_hbm, kmt_hbm, weights, table,
-                    us_hbm, vs_hbm, eta_out, tx_out, ty_out, corr_out, kmask_out, col_out, own_out, rows_out,
+                    us_hbm, vs_hbm, eta_out, tx_out, ty_out, corr_out, kmask_out, col_out, rows_out,
                     buf, tu, tv, cu, cv, pbufa, pbufb, pacc, phal, rhoc, gsum, xsum, kmask, kmt, vep, uwp, dup, txb, tyb, corr,
                     send_col, recv_col, send_row, recv_row,
                     xb, sp, rp, xf, sf, rf, hux, huy, ae, aw, an, as_, cc, ebufa, ebufb, dbuf, gbuf, eacc, bacc,
@@ -321,7 +321,7 @@
 
     RHO_T = np.float32(-THERM_EXP * PRESS_SCALE / LEVELS / 2)
     RHO_S = np.float32(HALINE_CON * PRESS_SCALE / LEVELS / 2)
-    BR = 64
+    BR = 128
     SB = 16
 
     def pressure_rows(k, slot, base, rows):
@@ -484,7 +484,7 @@
     lax.fori_loop(0, NCH, chunk_step, 0)
 
     packet_copies = [pltpu.make_async_copy(src, dst, ot_sem.at[i]) for i, (src, dst) in enumerate(
-        ((recv_col, col_out), (recv_row, rows_out), (kmask, kmask_out), (send_col, own_out)))]
+        ((recv_col, col_out), (recv_row, rows_out), (kmask, kmask_out)))]
     for copy in packet_copies:
         copy.start()
 
@@ -735,9 +735,9 @@
     lax.fori_loop(0, NCH, drain, 0)
 
 
-def tracer_kernel(u_hbm, v_hbm, t_hbm, s_hbm, us_hbm, vs_hbm, eta_in, tx_in, ty_in, corr_in, kmask_in, col_in, own_in, rows_in, table,
+def tracer_kernel(u_hbm, v_hbm, t_hbm, s_hbm, us_hbm, vs_hbm, eta_in, tx_in, ty_in, corr_in, kmask_in, col_in, rows_in, table,
                   eta_hbm, tx_hbm, ty_hbm, un_hbm, vn_hbm, tn_hbm, sn_hbm,
-                  buf, tt, ts, ct, su, sv, small, corr, kmask, cols, own, rows, qcol, ld_sem, ed_sem, st_sem, in_sem, out_sem):
+                  buf, tt, ts, ct, su, sv, small, corr, kmask, cols, rows, ld_sem, ed_sem, st_sem, in_sem, out_sem):
     hbm = (u_hbm, v_hbm, t_hbm, s_hbm)
     sources = (eta_in, tx_in, ty_in)
     sinks = (eta_hbm, tx_hbm, ty_hbm)
@@ -762,7 +762,7 @@
                 for f, (src, dst) in enumerate(((tt, tn_hbm), (ts, sn_hbm)))]
 
     edges = [pltpu.make_async_copy(src, dst, ed_sem.at[i])
-             for i, (src, dst) in enumerate(((col_in, cols), (rows_in, rows), (corr_in, corr), (kmask_in, kmask), (own_in, own)))]
+             for i, (src, dst) in enumerate(((col_in, cols), (rows_in, rows), (corr_in, corr), (kmask_in, kmask)))]
     for copy in edges:
         copy.start()
     for c in range(NCH):
@@ -803,23 +803,22 @@
 
         def piece(r, b):
             wet = [kmask[0, t, pl.ds(r, SB), :] > level_no for t in range(2)]
-            packed = qcol[pl.ds(r, SB), :]
+            packed = cols[c, pl.ds(b, SB), :]
             for m in range(2):
                 j = kk * 2 + m
                 u = [buf[0, k, m, t, pl.ds(b, SB), :] for t in range(2)]
                 v = [buf[1, k, m, t, pl.ds(b, SB), :] for t in range(2)]
                 vs = [buf[1, k, m, t, pl.ds(b - 1, SB), :] for t in range(2)]
+                uw = west_pair(*u, halo(packed, j))
                 for f, ref in ((2, tt), (3, ts)):
                     q = [buf[f, k, m, t, pl.ds(b, SB), :] for t in range(2)]
                     edge = halo(packed, f * PAIRS + j)
-                    qe = east_pair(*q, edge)
-                    fx = [u[t] * (q[t] + qe[t]) for t in range(2)]
-                    fw = west_pair(*fx, edge)
+                    qe, qw = east_pair(*q, edge), west_pair(*q, edge)
                     for t in range(2):
                         lane = slice(t * LN, (t + 1) * LN)
                         fy = v[t] * (q[t] + buf[f, k, m, t, pl.ds(b + 1, SB), :])
                         fs = vs[t] * (q[t] + buf[f, k, m, t, pl.ds(b - 1, SB), :])
-                        adv = q[t] - 0.5 * ((fx[t] - fw[t]) + (fy - fs))
+                        adv = q[t] - 0.5 * ((u[t] * (q[t] + qe[t]) - uw[t] * (q[t] + qw[t])) + (fy - fs))
                         adv = jnp.where(wet[t], adv, 0.0)
                         new = adv + before * ct[f - 2, m, t, pl.ds(r, SB), :]
                         ct[f - 2, m, t, pl.ds(r, SB), :] = new
@@ -846,12 +845,6 @@
                 for f in (2, 3):
                     for t in range(2):
                         buf[f, k, m, t, 8 + ROWS:9 + ROWS, :] = rows[1, c, t, f, jj:jj + 1, :]
-
-        packed = cols[c, 8:8 + ROWS, :]
-        lane = lanes(ROWS)
-        west_u = jnp.where(lane < 6 * PAIRS, pltpu.roll(packed, 4 * PAIRS, 1), pltpu.roll(packed, 6 * PAIRS, 1))
-        flux = west_u * (packed + pltpu.roll(own[c], 1, 1))
-        qcol[...] = jnp.where(lax.rem(lane, 2) == 1, flux, packed)
 
         def one_level(kk, carry2):
             level(c, kk)
@@ -918,9 +911,9 @@
         momentum_kernel,
         name="momentum",
         out_shape=(shape(*full), shape(*full), shape(*flat), shape(*flat), shape(*flat), shape(2, 2, 2, ROWS, LN),
-                   shape(3, 2, ROWS, LN), shape(NCH, PR, LN), shape(NCH, ROWS, LN), shape(2, NCH, 2, 4, PAIRS, LN)),
+                   shape(3, 2, ROWS, LN), shape(NCH, PR, LN), shape(2, NCH, 2, 4, PAIRS, LN)),
         in_specs=[any_spec] * 9 + [smem_spec, smem_spec],
-        out_specs=(any_spec,) * 10,
+        out_specs=(any_spec,) * 9,
         scratch_shapes=[
             vm(4, LEVELS, 2, 2, PR, LN), vm(LEVELS + 1, 2, 2, ROWS, LN), vm(LEVELS + 1, 2, 2, ROWS, LN),
             vm(2, 2, ROWS, LN), vm(2, 2, ROWS, LN), vm(2, 2, PR, LN), vm(2, 2, PR, LN), vm(2, 2, PR, LN), vm(2, PR, LN), vm(ROWS, LN),
@@ -939,21 +932,21 @@
         tracer_kernel,
         name="tracers",
         out_shape=(shape(*flat), shape(*flat), shape(*flat), shape(*full), shape(*full), shape(*full), shape(*full)),
-        in_specs=[any_spec] * 14 + [smem_spec],
+        in_specs=[any_spec] * 13 + [smem_spec],
         out_specs=(any_spec,) * 7,
         scratch_shapes=[
             vm(4, LEVELS, 2, 2, PR, LN), vm(LEVELS + 1, 2, ROWS, 2 * LN), vm(LEVELS + 1, 2, ROWS, 2 * LN), vm(2, 2, 2, ROWS, LN),
             vm(*full), vm(*full), vm(3, 2, ROWS, 2 * LN), vm(2, 2, 2, ROWS, LN), vm(3, 2, ROWS, LN),
-            vm(NCH, PR, LN), vm(NCH, ROWS, LN), vm(2, NCH, 2, 4, PAIRS, LN), vm(ROWS, LN),
-            dma(NCH, 10), dma(5), dma(NCH, 4), dma(3), dma(3),
+            vm(NCH, PR, LN), vm(2, NCH, 2, 4, PAIRS, LN),
+            dma(NCH, 10), dma(4), dma(NCH, 4), dma(3), dma(3),
         ],
         compiler_params=pltpu.CompilerParams(vmem_limit_bytes=67043328),
     )
 
     def local_step(vel_x, vel_y, pot_temp, salinity, surf_eta, trans_x, trans_y, col_depth, wet_levels, avg_weights):
-        star_x, star_y, eta, tx, ty, corr, kmask, cols, own, rows = momentum(
+        star_x, star_y, eta, tx, ty, corr, kmask, cols, rows = momentum(
             vel_x, vel_y, pot_temp, salinity, surf_eta, trans_x, trans_y, col_depth, wet_levels, avg_weights, jnp.asarray(visc))
-        return tracers(vel_x, vel_y, pot_temp, salinity, star_x, star_y, eta, tx, ty, corr, kmask, cols, own, rows, jnp.asarray(diff))
+        return tracers(vel_x, vel_y, pot_temp, salinity, star_x, star_y, eta, tx, ty, corr, kmask, cols, rows, jnp.asarray(diff))
 
     spec_3d = P(None, None, "row", "col")
     spec_2d = P(None, "row", "col")

time: 91.5 us -> 64 us (0.70)
  Pallas kernels: 90.7 us -> 63.2 us
    pallas_call x1, Pallas kernels: 45.2 us -> 21.7 us  [local_step(): tracers(vel_x, vel_y, pot_temp, salinity, star_x, star_y, eta, tx, ty, co...]
    pallas_call x1, Pallas kernels: 45.5 us -> 41.5 us  [local_step(): momentum(vel_x, vel_y, pot_temp, salinity, surf_eta, trans_x, trans_y, co...]
where the time goes in v5:
time: 64 us; the launch traced here: 63.8 us
  Pallas kernels  63.2 us (99%)
  between operations  0.64 us (1%)
    pallas_call x1, Pallas kernels, local_step(): momentum(vel_x, vel_y, pot_temp, salinity, surf_eta, trans_x, trans_y, co...  41.5 us
    pallas_call x1, Pallas kernels, local_step(): tracers(vel_x, vel_y, pot_temp, salinity, star_x, star_y, eta, tx, ty, co...  21.7 us

profile of v5, /device:TPU:0, one launch (start us, length us, event | category | flops | bytes accessed | tf_op | source)
XLA Modules:
  0.0 63.8 jit_solution(11758253319486514327)
XLA Ops:
  0.6 41.5 %momentum.1 = (f32[20,2,128,256]{3,2,1,0:T(8,128)}, f32[20,2,128,256]{3,2,1,0:T(8,128)}, f32[2,128,256]{2,1,0:T(8,128)}, f32[2,128,256]{2,1,0:T(8,128)}, f32[2,1...) custom-call(f32[20,2,128,256]{3,2,1,0:T(8,128)} %u_hbm.3, ...), custom_call_target="tpu_custom_call" | custom-call | tf_op jit(solution)/shard_map/momentum/pallas_call | solution.py:947
  42.2 21.7 %tracers.1 = (f32[2,128,256]{2,1,0:T(8,128)}, f32[2,128,256]{2,1,0:T(8,128)}, f32[2,128,256]{2,1,0:T(8,128)}, f32[20,2,128,256]{3,2,1,0:T(8,128)}, f32[20,2,128,...) custom-call(f32[20,2,128,256]{3,2,1,0:T(8,128)} %u_hbm.3, f32[20,2,128,256]{3,2,1,0:T(8,128)} %v_hbm.3, ...), custom_call_target="tpu_custom_call" | custom-call | tf_op jit(solution)/shard_map/tracers/pallas_call | solution.py:949

commit v6 on v5

--- a/solution.py
+++ b/solution.py
@@ -24,6 +24,8 @@
 PR = 144
 EXT = 192
 F32 = jnp.float32
+TC = 2
+AHEAD = 4
 PK = 64
 UP = 32
 MESH_ID = pl.DeviceIdType.MESH
@@ -105,7 +107,7 @@
         return [pltpu.make_async_copy(ref.at[:, :, pl.ds(t * LN, LN)], xb.at[pl.ds(2 + 2 * i, 2), t, pl.ds(32, ROWS), :], xl_sem.at[2 + 2 * i + t])
                 for t in range(2) for i, ref in enumerate((eta_hbm, tx_hbm, ty_hbm))]
 
-    for copy in map_loads() + loads(0) + loads(1) + loads(2) + flow_loads():
+    for copy in map_loads() + loads(0) + loads(1) + loads(2) + flow_loads() + loads(3) + loads(4):
         copy.start()
 
     barrier = pltpu.get_barrier_semaphore()
@@ -317,7 +319,25 @@
         start_all(edge_copies(c))
 
     pack_and_send(0, with_maps=True)
-    pack_and_send(1)
+
+    def pack_pairs(source, firsts, seconds, send):
+        lane = lanes(ROWS)
+        outer = (lane < 32) | (lane >= 96)
+        for slot, (f, g) in enumerate(zip(firsts, seconds)):
+            a, b = (jnp.where(lane < 64, source[n, 0, 32:32 + ROWS, :], source[n, 1, 32:32 + ROWS, :]) for n in (f, g))
+            send[slot, :, :] = jnp.where(outer, a, pltpu.roll(b, 64, 1))
+
+    def pack_wide():
+        for copy in flow_loads():
+            copy.wait()
+        pack_pairs(xb, (0, 2, 4, 6), (1, 3, 5, 7), sp)
+        start_all(flow_copies())
+
+    def pack_rest(c, carry):
+        pack_and_send(c)
+        return carry
+    lax.fori_loop(1, NCH, pack_rest, 0)
+    pack_wide()
 
     RHO_T = np.float32(-THERM_EXP * PRESS_SCALE / LEVELS / 2)
     RHO_S = np.float32(HALINE_CON * PRESS_SCALE / LEVELS / 2)
@@ -404,19 +424,6 @@
     lax.fori_loop(0, 2, first_pressure, 0)
 
     def chunk_step(c, carry):
-        @pl.when(c + 3 < NCH)
-        def _():
-            for copy in loads(c + 3):
-                copy.start()
-
-        @pl.when(c + 2 < NCH)
-        def _():
-            pack_and_send(c + 2)
-
-        @pl.when(c == 2)
-        def _():
-            pack_wide()
-
         wait_recv_all(edge_copies(c))
 
         @pl.when(c == 0)
@@ -441,14 +448,6 @@
         lax.fori_loop(0, CHUNK // 2, two_levels, 0)
         return carry
 
-    def pack_wide():
-        for copy in flow_loads():
-            copy.wait()
-        for pair in range(4):
-            pack_pair(lambda t, r, p=pair: xb[2 * p, t, pl.ds(32 + r, 64), :],
-                      lambda t, r, p=pair: xb[2 * p + 1, t, pl.ds(32 + r, 64), :], sp, pair, 64)
-        start_all(flow_copies())
-
     def face_maps():
         wait_recv_all(map_copies())
 
@@ -468,18 +467,6 @@
                 huy[t, pl.ds(32 + r, 64), :] = jnp.where(ky > 0.0, 0.5 * (ht[t] + xb[1, t, pl.ds(33 + r, 64), :]), 0.0)
             return carry
         lax.fori_loop(0, 2, maps, 0)
-
-    def pack_pair(first, second, send, slot, rows):
-        lane = lanes(rows)
-
-        def block(i, carry):
-            r = pl.multiple_of(i * rows, rows)
-            a = jnp.where(lane < 64, first(0, r), first(1, r))
-            b = jnp.where(lane < 64, second(0, r), second(1, r))
-            outer = (lane < 32) | (lane >= 96)
-            send[slot, pl.ds(r, rows), :] = jnp.where(outer, a, pltpu.roll(b, 64, 1))
-            return carry
-        lax.fori_loop(0, ROWS // rows, block, 0)
 
     lax.fori_loop(0, NCH, chunk_step, 0)
 
@@ -500,9 +487,7 @@
                 xf[2 + m, t, pl.ds(32 + r, 32), :] = fy * gsum[1, m, t, pl.ds(r, 32), :]
         return carry
     lax.fori_loop(0, ROWS // 32, forcing, 0)
-    for m in range(2):
-        pack_pair(lambda t, r, m=m: xf[m, t, pl.ds(32 + r, 64), :],
-                  lambda t, r, m=m: xf[2 + m, t, pl.ds(32 + r, 64), :], sf, m, 64)
+    pack_pairs(xf, (0, 1), (2, 3), sf)
     start_all(force_copies())
 
     def stores(c):
@@ -543,13 +528,13 @@
     wait_recv_all(flow_copies())
 
     def unpack_wide(i, carry):
-        r = pl.multiple_of(i * 32, 32)
+        r = pl.multiple_of(i * 96, 32)
         for pair in range(4):
-            tile = rp[pair, pl.ds(r, 32), :]
-            xb[2 * pair, 2, pl.ds(r, 32), :] = tile
-            xb[2 * pair + 1, 2, pl.ds(r, 32), :] = pltpu.roll(tile, 64, 1)
-        return carry
-    lax.fori_loop(0, EXT // 32, unpack_wide, 0)
+            tile = rp[pair, pl.ds(r, 96), :]
+            xb[2 * pair, 2, pl.ds(r, 96), :] = tile
+            xb[2 * pair + 1, 2, pl.ds(r, 96), :] = pltpu.roll(tile, 64, 1)
+        return carry
+    lax.fori_loop(0, EXT // 96, unpack_wide, 0)
 
     XR = 88
 
@@ -603,27 +588,6 @@
         return carry
     lax.fori_loop(0, 2, first_block, 0)
 
-    wait_recv_all(force_copies())
-
-    def unpack_force(i, carry):
-        r = pl.multiple_of(i * 32, 32)
-        for m in range(2):
-            tile = rf[m, pl.ds(r, 32), :]
-            xf[m, 2, pl.ds(r, 32), :] = tile
-            xf[2 + m, 2, pl.ds(r, 32), :] = pltpu.roll(tile, 64, 1)
-        return carry
-    lax.fori_loop(0, EXT // 32, unpack_force, 0)
-
-    def forcing_divergence(i, carry):
-        r = pl.multiple_of(8 + i * XR, 8)
-        for m in range(2):
-            fx = [xf[m, t, pl.ds(r, XR), :] for t in range(3)]
-            for t in range(3):
-                div = fx[t] - west(fx[t], fx[PREV[t]]) + xf[2 + m, t, pl.ds(r, XR), :] - xf[2 + m, t, pl.ds(r - 1, XR), :]
-                gbuf[m, t, pl.ds(r, XR), :] = cc[t, pl.ds(r, XR), :] * div
-        return carry
-    lax.fori_loop(0, 2, forcing_divergence, 0)
-
     whole = weights[SUBS - 1]
     moment = weights[SUBS - 1]
     for n in range(SUBS - 2, -1, -1):
@@ -640,6 +604,27 @@
                     eacc[m, t, pl.ds(r, 8), :] = weights[0] * eta
         return carry
     lax.fori_loop(0, 17, first_sums, 0)
+
+    wait_recv_all(force_copies())
+
+    def unpack_force(i, carry):
+        r = pl.multiple_of(i * 96, 32)
+        for m in range(2):
+            tile = rf[m, pl.ds(r, 96), :]
+            xf[m, 2, pl.ds(r, 96), :] = tile
+            xf[2 + m, 2, pl.ds(r, 96), :] = pltpu.roll(tile, 64, 1)
+        return carry
+    lax.fori_loop(0, EXT // 96, unpack_force, 0)
+
+    def forcing_divergence(i, carry):
+        r = pl.multiple_of(8 + i * XR, 8)
+        for m in range(2):
+            fx = [xf[m, t, pl.ds(r, XR), :] for t in range(3)]
+            for t in range(3):
+                div = fx[t] - west(fx[t], fx[PREV[t]]) + xf[2 + m, t, pl.ds(r, XR), :] - xf[2 + m, t, pl.ds(r - 1, XR), :]
+                gbuf[m, t, pl.ds(r, XR), :] = cc[t, pl.ds(r, XR), :] * div
+        return carry
+    lax.fori_loop(0, 2, forcing_divergence, 0)
 
     def subcycle(n, tail, lo, hi, old, new):
         tail = tail - weights[n - 2]
@@ -737,7 +722,7 @@
 
 def tracer_kernel(u_hbm, v_hbm, t_hbm, s_hbm, us_hbm, vs_hbm, eta_in, tx_in, ty_in, corr_in, kmask_in, col_in, rows_in, table,
                   eta_hbm, tx_hbm, ty_hbm, un_hbm, vn_hbm, tn_hbm, sn_hbm,
-                  buf, tt, ts, ct, su, sv, small, corr, kmask, cols, rows, ld_sem, ed_sem, st_sem, in_sem, out_sem):
+                  buf, tt, ts, ct, su, sv, small, corr, kmask, cols, rows, ld_sem, ed_sem, st_sem, sv_sem, in_sem, out_sem):
     hbm = (u_hbm, v_hbm, t_hbm, s_hbm)
     sources = (eta_in, tx_in, ty_in)
     sinks = (eta_hbm, tx_hbm, ty_hbm)
@@ -747,25 +732,25 @@
         for f in range(4):
             for t in range(2):
                 out.append(pltpu.make_async_copy(
-                    hbm[f].at[pl.ds(c * CHUNK, CHUNK), :, :, pl.ds(t * LN, LN)],
-                    buf.at[f, pl.ds(c * CHUNK, CHUNK), :, t, pl.ds(8, ROWS), :], ld_sem.at[c, f * 2 + t]))
+                    hbm[f].at[pl.ds(c * TC, TC), :, :, pl.ds(t * LN, LN)],
+                    buf.at[f, pl.ds(c * TC, TC), :, t, pl.ds(8, ROWS), :], ld_sem.at[c, f * 2 + t]))
         for f, (src, dst) in enumerate(((us_hbm, su), (vs_hbm, sv))):
-            out.append(pltpu.make_async_copy(src.at[pl.ds(c * CHUNK, CHUNK)], dst.at[pl.ds(c * CHUNK, CHUNK)], ld_sem.at[c, 8 + f]))
+            out.append(pltpu.make_async_copy(src.at[pl.ds(c * TC, TC)], dst.at[pl.ds(c * TC, TC)], ld_sem.at[c, 8 + f]))
         return out
 
     def stores_v(c):
+        return [pltpu.make_async_copy(src.at[pl.ds(c * TC, TC)], dst.at[pl.ds(c * TC, TC)], sv_sem.at[c, f])
+                for f, (src, dst) in enumerate(((su, un_hbm), (sv, vn_hbm)))]
+
+    def stores_t(c):
         return [pltpu.make_async_copy(src.at[pl.ds(c * CHUNK, CHUNK)], dst.at[pl.ds(c * CHUNK, CHUNK)], st_sem.at[c, f])
-                for f, (src, dst) in enumerate(((su, un_hbm), (sv, vn_hbm)))]
-
-    def stores_t(c):
-        return [pltpu.make_async_copy(src.at[pl.ds(c * CHUNK, CHUNK)], dst.at[pl.ds(c * CHUNK, CHUNK)], st_sem.at[c, 2 + f])
                 for f, (src, dst) in enumerate(((tt, tn_hbm), (ts, sn_hbm)))]
 
     edges = [pltpu.make_async_copy(src, dst, ed_sem.at[i])
              for i, (src, dst) in enumerate(((col_in, cols), (rows_in, rows), (corr_in, corr), (kmask_in, kmask)))]
     for copy in edges:
         copy.start()
-    for c in range(NCH):
+    for c in range(AHEAD):
         for copy in loads(c):
             copy.start()
     small_in = [pltpu.make_async_copy(sources[i], small.at[i], in_sem.at[i]) for i in range(3)]
@@ -791,8 +776,7 @@
     BR = 128
     SB = 16
 
-    def level(c, kk):
-        k = c * CHUNK + kk
+    def level(k, c, kk):
         level_no = k.astype(F32)
         before = table[0, k]
 
@@ -833,27 +817,34 @@
         lax.fori_loop(0, ROWS // BR, block, 0)
 
     def chunk_step(c, carry):
+        @pl.when(c + AHEAD < LEVELS // TC)
+        def _():
+            for copy in loads(c + AHEAD):
+                copy.start()
+
         for copy in loads(c):
             copy.wait()
-        for kk in range(CHUNK):
-            k = c * CHUNK + kk
+        packet = c // (CHUNK // TC)
+        first = lax.rem(c, CHUNK // TC) * TC
+        for kk in range(TC):
+            k = c * TC + kk
             for m in range(2):
-                jj = kk * 2 + m
+                jj = (first + kk) * 2 + m
                 for f in (1, 2, 3):
                     for t in range(2):
-                        buf[f, k, m, t, 7:8, :] = rows[0, c, t, f, jj:jj + 1, :]
+                        buf[f, k, m, t, 7:8, :] = rows[0, packet, t, f, pl.ds(jj, 1), :]
                 for f in (2, 3):
                     for t in range(2):
-                        buf[f, k, m, t, 8 + ROWS:9 + ROWS, :] = rows[1, c, t, f, jj:jj + 1, :]
+                        buf[f, k, m, t, 8 + ROWS:9 + ROWS, :] = rows[1, packet, t, f, pl.ds(jj, 1), :]
 
         def one_level(kk, carry2):
-            level(c, kk)
+            level(c * TC + kk, packet, first + kk)
             return carry2
-        lax.fori_loop(0, CHUNK, one_level, 0)
+        lax.fori_loop(0, TC, one_level, 0)
         for copy in stores_v(c):
             copy.start()
         return carry
-    lax.fori_loop(0, NCH, chunk_step, 0)
+    lax.fori_loop(0, LEVELS // TC, chunk_step, 0)
 
     for copy in small_in:
         copy.wait()
@@ -888,10 +879,16 @@
         copy.wait()
 
     def drain(c, carry):
-        for copy in stores_v(c) + stores_t(c):
+        for copy in stores_t(c):
             copy.wait()
         return carry
     lax.fori_loop(0, NCH, drain, 0)
+
+    def drain_v(c, carry):
+        for copy in stores_v(c):
+            copy.wait()
+        return carry
+    lax.fori_loop(0, LEVELS // TC, drain_v, 0)
 
 
 def solution(mesh):
@@ -938,7 +935,7 @@
             vm(4, LEVELS, 2, 2, PR, LN), vm(LEVELS + 1, 2, ROWS, 2 * LN), vm(LEVELS + 1, 2, ROWS, 2 * LN), vm(2, 2, 2, ROWS, LN),
             vm(*full), vm(*full), vm(3, 2, ROWS, 2 * LN), vm(2, 2, 2, ROWS, LN), vm(3, 2, ROWS, LN),
             vm(NCH, PR, LN), vm(2, NCH, 2, 4, PAIRS, LN),
-            dma(NCH, 10), dma(4), dma(NCH, 4), dma(3), dma(3),
+            dma(LEVELS // TC, 10), dma(4), dma(NCH, 2), dma(LEVELS // TC, 2), dma(3), dma(3),
         ],
         compiler_params=pltpu.CompilerParams(vmem_limit_bytes=67043328),
     )

time: 64 us -> 62.9 us (0.983)
  Pallas kernels: 63.2 us -> 62.1 us
    pallas_call x1, Pallas kernels: 41.5 us -> 40.3 us  [local_step(): momentum(vel_x, vel_y, pot_temp, salinity, surf_eta, trans_x, trans_y, co...]
where the time goes in v6:
time: 62.9 us; the launch traced here: 62.7 us
  Pallas kernels  62.1 us (99%)
  between operations  0.64 us (1%)
    pallas_call x1, Pallas kernels, local_step(): momentum(vel_x, vel_y, pot_temp, salinity, surf_eta, trans_x, trans_y, co...  40.3 us
    pallas_call x1, Pallas kernels, local_step(): tracers(vel_x, vel_y, pot_temp, salinity, star_x, star_y, eta, tx, ty, co...  21.8 us

profile of v6, /device:TPU:0, one launch (start us, length us, event | category | flops | bytes accessed | tf_op | source)
XLA Modules:
  0.0 62.7 jit_solution(3091613643647350565)
XLA Ops:
  0.6 40.3 %momentum.1 = (f32[20,2,128,256]{3,2,1,0:T(8,128)}, f32[20,2,128,256]{3,2,1,0:T(8,128)}, f32[2,128,256]{2,1,0:T(8,128)}, f32[2,128,256]{2,1,0:T(8,128)}, f32[2,1...) custom-call(f32[20,2,128,256]{3,2,1,0:T(8,128)} %u_hbm.3, ...), custom_call_target="tpu_custom_call" | custom-call | tf_op jit(solution)/shard_map/momentum/pallas_call | solution.py:944
  40.9 21.8 %tracers.1 = (f32[2,128,256]{2,1,0:T(8,128)}, f32[2,128,256]{2,1,0:T(8,128)}, f32[2,128,256]{2,1,0:T(8,128)}, f32[20,2,128,256]{3,2,1,0:T(8,128)}, f32[20,2,128,...) custom-call(f32[20,2,128,256]{3,2,1,0:T(8,128)} %u_hbm.3, f32[20,2,128,256]{3,2,1,0:T(8,128)} %v_hbm.3, ...), custom_call_target="tpu_custom_call" | custom-call | tf_op jit(solution)/shard_map/tracers/pallas_call | solution.py:946

commit v7 on v6

--- a/solution.py
+++ b/solution.py
@@ -44,6 +44,13 @@
     return np.stack([before, ratio, 1.0 / inner, 1.0 / last]).astype(np.float32)
 
 
+def write_table(table, strength):
+    values = solve_table(strength)
+    for i in range(values.shape[0]):
+        for k in range(LEVELS):
+            table[i, k] = values[i, k]
+
+
 def lanes(rows):
     return lax.broadcasted_iota(jnp.int32, (rows, LN), 1)
 
@@ -76,12 +83,13 @@
     return jnp.where(origin, edge, a), jnp.where(origin, a, b)
 
 
-def momentum_kernel(u_hbm, v_hbm, t_hbm, s_hbm, eta_hbm, tx_hbm, ty_hbm, h_hbm, kmt_hbm, weights, table,
+def momentum_kernel(u_hbm, v_hbm, t_hbm, s_hbm, eta_hbm, tx_hbm, ty_hbm, h_hbm, kmt_hbm, weights_hbm,
                     us_hbm, vs_hbm, eta_out, tx_out, ty_out, corr_out, kmask_out, col_out, rows_out,
                     buf, tu, tv, cu, cv, pbufa, pbufb, pacc, phal, rhoc, gsum, xsum, kmask, kmt, vep, uwp, dup, txb, tyb, corr,
                     send_col, recv_col, send_row, recv_row,
                     xb, sp, rp, xf, sf, rf, hux, huy, ae, aw, an, as_, cc, ebufa, ebufb, dbuf, gbuf, eacc, bacc,
-                    ld_sem, xl_sem, cs_sem, cr_sem, xs_sem, xr_sem, fs_sem, fr_sem, st_sem, ot_sem, av_sem):
+                    ld_sem, xl_sem, cs_sem, cr_sem, xs_sem, xr_sem, fs_sem, fr_sem, st_sem, ot_sem, av_sem, weights, table, w_sem):
+    weights_load = pltpu.make_async_copy(weights_hbm, weights, w_sem)
     ku, kv = kmask.at[1], kmask.at[2]
     me_c = lax.axis_index("col")
     me_r = lax.axis_index("row")
@@ -107,7 +115,8 @@
         return [pltpu.make_async_copy(ref.at[:, :, pl.ds(t * LN, LN)], xb.at[pl.ds(2 + 2 * i, 2), t, pl.ds(32, ROWS), :], xl_sem.at[2 + 2 * i + t])
                 for t in range(2) for i, ref in enumerate((eta_hbm, tx_hbm, ty_hbm))]
 
-    for copy in map_loads() + loads(0) + loads(1) + loads(2) + flow_loads() + loads(3) + loads(4):
+    write_table(table, VISC_NUMBER)
+    for copy in map_loads() + loads(0) + loads(1) + loads(2) + flow_loads() + loads(3) + loads(4) + [weights_load]:
         copy.start()
 
     barrier = pltpu.get_barrier_semaphore()
@@ -196,14 +205,6 @@
             xb[0, t, 32 + r:96 + r, :] = level_count
             kmask[0, t, r:r + 64, :] = level_count
 
-    @pl.when((me_r == 0) | (me_r == 3))
-    def _():
-        pl.semaphore_wait(barrier, 3)
-
-    @pl.when((me_r != 0) & (me_r != 3))
-    def _():
-        pl.semaphore_wait(barrier, 5)
-
     def remote(src, dst, ssem, rsem, col, row):
         return pltpu.make_async_remote_copy(src_ref=src, dst_ref=dst, send_sem=ssem, recv_sem=rsem,
                                             device_id={"col": col, "row": row}, device_id_type=MESH_ID)
@@ -285,7 +286,14 @@
             for copy in down:
                 copy.wait_send()
 
-    start_all(map_copies())
+    def all_entered():
+        @pl.when((me_r == 0) | (me_r == 3))
+        def _():
+            pl.semaphore_wait(barrier, 3)
+
+        @pl.when((me_r != 0) & (me_r != 3))
+        def _():
+            pl.semaphore_wait(barrier, 5)
 
     def pack_and_send(c, with_maps=False):
         for copy in loads(c):
@@ -316,6 +324,9 @@
                         for t in range(2):
                             send_row[side, c, t, f, jj:jj + 1, :] = buf[f, k, m, t, row:row + 1, :]
         lax.fori_loop(0, ROWS // PK, block, 0)
+        if with_maps:
+            all_entered()
+            start_all(map_copies())
         start_all(edge_copies(c))
 
     pack_and_send(0, with_maps=True)
@@ -336,8 +347,7 @@
     def pack_rest(c, carry):
         pack_and_send(c)
         return carry
-    lax.fori_loop(1, NCH, pack_rest, 0)
-    pack_wide()
+    lax.fori_loop(1, NCH - 1, pack_rest, 0)
 
     RHO_T = np.float32(-THERM_EXP * PRESS_SCALE / LEVELS / 2)
     RHO_S = np.float32(HALINE_CON * PRESS_SCALE / LEVELS / 2)
@@ -424,6 +434,14 @@
     lax.fori_loop(0, 2, first_pressure, 0)
 
     def chunk_step(c, carry):
+        @pl.when(c == 1)
+        def _():
+            pack_and_send(NCH - 1)
+
+        @pl.when(c == 2)
+        def _():
+            pack_wide()
+
         wait_recv_all(edge_copies(c))
 
         @pl.when(c == 0)
@@ -588,6 +606,7 @@
         return carry
     lax.fori_loop(0, 2, first_block, 0)
 
+    weights_load.wait()
     whole = weights[SUBS - 1]
     moment = weights[SUBS - 1]
     for n in range(SUBS - 2, -1, -1):
@@ -720,9 +739,9 @@
     lax.fori_loop(0, NCH, drain, 0)
 
 
-def tracer_kernel(u_hbm, v_hbm, t_hbm, s_hbm, us_hbm, vs_hbm, eta_in, tx_in, ty_in, corr_in, kmask_in, col_in, rows_in, table,
+def tracer_kernel(u_hbm, v_hbm, t_hbm, s_hbm, us_hbm, vs_hbm, eta_in, tx_in, ty_in, corr_in, kmask_in, col_in, rows_in,
                   eta_hbm, tx_hbm, ty_hbm, un_hbm, vn_hbm, tn_hbm, sn_hbm,
-                  buf, tt, ts, ct, su, sv, small, corr, kmask, cols, rows, ld_sem, ed_sem, st_sem, sv_sem, in_sem, out_sem):
+                  buf, tt, ts, ct, su, sv, small, corr, kmask, cols, rows, ld_sem, ed_sem, st_sem, sv_sem, in_sem, out_sem, table):
     hbm = (u_hbm, v_hbm, t_hbm, s_hbm)
     sources = (eta_in, tx_in, ty_in)
     sinks = (eta_hbm, tx_hbm, ty_hbm)
@@ -753,6 +772,7 @@
     for c in range(AHEAD):
         for copy in loads(c):
             copy.start()
+    write_table(table, DIFF_NUMBER)
     small_in = [pltpu.make_async_copy(sources[i], small.at[i], in_sem.at[i]) for i in range(3)]
     small_out = [pltpu.make_async_copy(small.at[i], sinks[i], out_sem.at[i]) for i in range(3)]
     for copy in small_in:
@@ -894,13 +914,9 @@
 def solution(mesh):
     assert mesh.shape["col"] == 2 and mesh.shape["row"] == 4
     any_spec = pl.BlockSpec(memory_space=pl.ANY)
-    vmem_spec = pl.BlockSpec(memory_space=pltpu.VMEM)
-    smem_spec = pl.BlockSpec(memory_space=pltpu.SMEM)
     shape = lambda *dims: jax.ShapeDtypeStruct(dims, F32)
     dma = lambda *dims: pltpu.SemaphoreType.DMA(dims)
     vm = lambda *dims: pltpu.VMEM(dims, F32)
-    visc = solve_table(VISC_NUMBER)
-    diff = solve_table(DIFF_NUMBER)
     full = (LEVELS, 2, ROWS, 2 * LN)
     flat = (2, ROWS, 2 * LN)
 
@@ -909,7 +925,7 @@
         name="momentum",
         out_shape=(shape(*full), shape(*full), shape(*flat), shape(*flat), shape(*flat), shape(2, 2, 2, ROWS, LN),
                    shape(3, 2, ROWS, LN), shape(NCH, PR, LN), shape(2, NCH, 2, 4, PAIRS, LN)),
-        in_specs=[any_spec] * 9 + [smem_spec, smem_spec],
+        in_specs=[any_spec] * 10,
         out_specs=(any_spec,) * 9,
         scratch_shapes=[
             vm(4, LEVELS, 2, 2, PR, LN), vm(LEVELS + 1, 2, 2, ROWS, LN), vm(LEVELS + 1, 2, 2, ROWS, LN),
@@ -921,6 +937,7 @@
             vm(3, EXT, LN), vm(3, EXT, LN), vm(3, EXT, LN), vm(3, EXT, LN), vm(3, EXT, LN), vm(3, EXT, LN), vm(3, EXT, LN),
             vm(2, 3, EXT, LN), vm(2, 3, EXT, LN), vm(2, 3, EXT, LN), vm(2, 3, EXT, LN), vm(2, 2, ROWS + 8, LN), vm(2, 3, ROWS + 8, LN),
             dma(NCH, 8), dma(9), dma(NCH, 5), dma(NCH, 5), dma(7), dma(7), dma(5), dma(5), dma(NCH, 4), dma(6), dma(2, 3),
+            pltpu.SMEM((SUBS,), F32), pltpu.SMEM((4, LEVELS), F32), pltpu.SemaphoreType.DMA,
         ],
         compiler_params=pltpu.CompilerParams(collective_id=0, has_side_effects=True, vmem_limit_bytes=67043328),
     )
@@ -929,21 +946,21 @@
         tracer_kernel,
         name="tracers",
         out_shape=(shape(*flat), shape(*flat), shape(*flat), shape(*full), shape(*full), shape(*full), shape(*full)),
-        in_specs=[any_spec] * 13 + [smem_spec],
+        in_specs=[any_spec] * 13,
         out_specs=(any_spec,) * 7,
         scratch_shapes=[
             vm(4, LEVELS, 2, 2, PR, LN), vm(LEVELS + 1, 2, ROWS, 2 * LN), vm(LEVELS + 1, 2, ROWS, 2 * LN), vm(2, 2, 2, ROWS, LN),
             vm(*full), vm(*full), vm(3, 2, ROWS, 2 * LN), vm(2, 2, 2, ROWS, LN), vm(3, 2, ROWS, LN),
             vm(NCH, PR, LN), vm(2, NCH, 2, 4, PAIRS, LN),
-            dma(LEVELS // TC, 10), dma(4), dma(NCH, 2), dma(LEVELS // TC, 2), dma(3), dma(3),
+            dma(LEVELS // TC, 10), dma(4), dma(NCH, 2), dma(LEVELS // TC, 2), dma(3), dma(3), pltpu.SMEM((4, LEVELS), F32),
         ],
         compiler_params=pltpu.CompilerParams(vmem_limit_bytes=67043328),
     )
 
     def local_step(vel_x, vel_y, pot_temp, salinity, surf_eta, trans_x, trans_y, col_depth, wet_levels, avg_weights):
         star_x, star_y, eta, tx, ty, corr, kmask, cols, rows = momentum(
-            vel_x, vel_y, pot_temp, salinity, surf_eta, trans_x, trans_y, col_depth, wet_levels, avg_weights, jnp.asarray(visc))
-        return tracers(vel_x, vel_y, pot_temp, salinity, star_x, star_y, eta, tx, ty, corr, kmask, cols, rows, jnp.asarray(diff))
+            vel_x, vel_y, pot_temp, salinity, surf_eta, trans_x, trans_y, col_depth, wet_levels, avg_weights)
+        return tracers(vel_x, vel_y, pot_temp, salinity, star_x, star_y, eta, tx, ty, corr, kmask, cols, rows)
 
     spec_3d = P(None, None, "row", "col")
     spec_2d = P(None, "row", "col")

time: 62.9 us -> 61.1 us (0.971)
  Pallas kernels: 62.1 us -> 60.4 us
    pallas_call x1, Pallas kernels: 40.3 us -> 39.3 us  [local_step(): momentum(vel_x, vel_y, pot_temp, salinity, surf_eta, trans_x, trans_y, co...]
    pallas_call x1, Pallas kernels: 21.8 us -> 21.1 us  [local_step(): tracers(vel_x, vel_y, pot_temp, salinity, star_x, star_y, eta, tx, ty, co...]
where the time goes in v7:
time: 61.1 us; the launch traced here: 61 us
  Pallas kernels  60.4 us (99%)
  between operations  0.64 us (1%)
    pallas_call x1, Pallas kernels, local_step(): momentum(vel_x, vel_y, pot_temp, salinity, surf_eta, trans_x, trans_y, co...  39.3 us
    pallas_call x1, Pallas kernels, local_step(): tracers(vel_x, vel_y, pot_temp, salinity, star_x, star_y, eta, tx, ty, co...  21.1 us

profile of v7, /device:TPU:0, one launch (start us, length us, event | category | flops | bytes accessed | tf_op | source)
XLA Modules:
  0.0 61.0 jit_solution(14327265251196104954)
XLA Ops:
  0.6 39.3 %momentum.1 = (f32[20,2,128,256]{3,2,1,0:T(8,128)}, f32[20,2,128,256]{3,2,1,0:T(8,128)}, f32[2,128,256]{2,1,0:T(8,128)}, f32[2,128,256]{2,1,0:T(8,128)}, f32[2,1...) custom-call(f32[20,2,128,256]{3,2,1,0:T(8,128)} %u_hbm.3, ...), custom_call_target="tpu_custom_call" | custom-call | tf_op jit(solution)/shard_map/momentum/pallas_call | solution.py:961
  39.9 21.1 %tracers.1 = (f32[2,128,256]{2,1,0:T(8,128)}, f32[2,128,256]{2,1,0:T(8,128)}, f32[2,128,256]{2,1,0:T(8,128)}, f32[20,2,128,256]{3,2,1,0:T(8,128)}, f32[20,2,128,...) custom-call(f32[20,2,128,256]{3,2,1,0:T(8,128)} %u_hbm.3, f32[20,2,128,256]{3,2,1,0:T(8,128)} %v_hbm.3, ...), custom_call_target="tpu_custom_call" | custom-call | tf_op jit(solution)/shard_map/tracers/pallas_call | solution.py:963

commit v8 on v7

--- a/solution.py
+++ b/solution.py
@@ -25,7 +25,7 @@
 EXT = 192
 F32 = jnp.float32
 TC = 2
-AHEAD = 4
+AHEAD = 6
 PK = 64
 UP = 32
 MESH_ID = pl.DeviceIdType.MESH
@@ -762,7 +762,7 @@
                 for f, (src, dst) in enumerate(((su, un_hbm), (sv, vn_hbm)))]
 
     def stores_t(c):
-        return [pltpu.make_async_copy(src.at[pl.ds(c * CHUNK, CHUNK)], dst.at[pl.ds(c * CHUNK, CHUNK)], st_sem.at[c, f])
+        return [pltpu.make_async_copy(src.at[pl.ds(c * TC, TC)], dst.at[pl.ds(c * TC, TC)], st_sem.at[c, f])
                 for f, (src, dst) in enumerate(((tt, tn_hbm), (ts, sn_hbm)))]
 
     edges = [pltpu.make_async_copy(src, dst, ed_sem.at[i])
@@ -872,16 +872,16 @@
         copy.start()
 
     def upward(step, carry):
-        c = NCH - 1 - step
+        c = LEVELS // TC - 1 - step
 
         def block(i, carry2):
             r = pl.multiple_of(i * UP, UP)
             for t in range(2):
                 lane = slice(t * LN, (t + 1) * LN)
                 depth = kmask[0, t, pl.ds(r, UP), :]
-                below = [[ref[c * CHUNK + CHUNK, m, pl.ds(r, UP), lane] for m in range(2)] for ref in (tt, ts)]
-                for kk in range(CHUNK - 1, -1, -1):
-                    k = c * CHUNK + kk
+                below = [[ref[c * TC + TC, m, pl.ds(r, UP), lane] for m in range(2)] for ref in (tt, ts)]
+                for kk in range(TC - 1, -1, -1):
+                    k = c * TC + kk
                     level_no = k.astype(F32)
                     inv = jnp.where(depth > level_no + 1.0, table[2, k], jnp.where(depth > level_no, table[3, k], 0.0))
                     for f, ref in enumerate((tt, ts)):
@@ -893,22 +893,16 @@
         for copy in stores_t(c):
             copy.start()
         return carry
-    lax.fori_loop(0, NCH, upward, 0)
+    lax.fori_loop(0, LEVELS // TC, upward, 0)
 
     for copy in small_out:
         copy.wait()
 
     def drain(c, carry):
-        for copy in stores_t(c):
+        for copy in stores_v(c) + stores_t(c):
             copy.wait()
         return carry
-    lax.fori_loop(0, NCH, drain, 0)
-
-    def drain_v(c, carry):
-        for copy in stores_v(c):
-            copy.wait()
-        return carry
-    lax.fori_loop(0, LEVELS // TC, drain_v, 0)
+    lax.fori_loop(0, LEVELS // TC, drain, 0)
 
 
 def solution(mesh):
@@ -952,7 +946,7 @@
             vm(4, LEVELS, 2, 2, PR, LN), vm(LEVELS + 1, 2, ROWS, 2 * LN), vm(LEVELS + 1, 2, ROWS, 2 * LN), vm(2, 2, 2, ROWS, LN),
             vm(*full), vm(*full), vm(3, 2, ROWS, 2 * LN), vm(2, 2, 2, ROWS, LN), vm(3, 2, ROWS, LN),
             vm(NCH, PR, LN), vm(2, NCH, 2, 4, PAIRS, LN),
-            dma(LEVELS // TC, 10), dma(4), dma(NCH, 2), dma(LEVELS // TC, 2), dma(3), dma(3), pltpu.SMEM((4, LEVELS), F32),
+            dma(LEVELS // TC, 10), dma(4), dma(LEVELS // TC, 2), dma(LEVELS // TC, 2), dma(3), dma(3), pltpu.SMEM((4, LEVELS), F32),
         ],
         compiler_params=pltpu.CompilerParams(vmem_limit_bytes=67043328),
     )

time: 61.1 us -> 60.8 us (level)
  no operation moved by 1% of the time
where the time goes in v8:
time: 60.8 us; the launch traced here: 60.7 us
  Pallas kernels  60.1 us (99%)
  between operations  0.64 us (1%)
    pallas_call x1, Pallas kernels, local_step(): momentum(vel_x, vel_y, pot_temp, salinity, surf_eta, trans_x, trans_y, co...  39.3 us
    pallas_call x1, Pallas kernels, local_step(): tracers(vel_x, vel_y, pot_temp, salinity, star_x, star_y, eta, tx, ty, co...  20.8 us

profile of v8, /device:TPU:0, one launch (start us, length us, event | category | flops | bytes accessed | tf_op | source)
XLA Modules:
  0.0 60.7 jit_solution(16855316762839304375)
XLA Ops:
  0.6 39.3 %momentum.1 = (f32[20,2,128,256]{3,2,1,0:T(8,128)}, f32[20,2,128,256]{3,2,1,0:T(8,128)}, f32[2,128,256]{2,1,0:T(8,128)}, f32[2,128,256]{2,1,0:T(8,128)}, f32[2,1...) custom-call(f32[20,2,128,256]{3,2,1,0:T(8,128)} %u_hbm.3, ...), custom_call_target="tpu_custom_call" | custom-call | tf_op jit(solution)/shard_map/momentum/pallas_call | solution.py:955
  39.9 20.8 %tracers.1 = (f32[2,128,256]{2,1,0:T(8,128)}, f32[2,128,256]{2,1,0:T(8,128)}, f32[2,128,256]{2,1,0:T(8,128)}, f32[20,2,128,256]{3,2,1,0:T(8,128)}, f32[20,2,128,...) custom-call(f32[20,2,128,256]{3,2,1,0:T(8,128)} %u_hbm.3, f32[20,2,128,256]{3,2,1,0:T(8,128)} %v_hbm.3, ...), custom_call_target="tpu_custom_call" | custom-call | tf_op jit(solution)/shard_map/tracers/pallas_call | solution.py:957

commit v9 on v8

--- a/solution.py
+++ b/solution.py
@@ -347,7 +347,9 @@
     def pack_rest(c, carry):
         pack_and_send(c)
         return carry
-    lax.fori_loop(1, NCH - 1, pack_rest, 0)
+    lax.fori_loop(1, NCH - 2, pack_rest, 0)
+    pack_wide()
+    lax.fori_loop(NCH - 2, NCH - 1, pack_rest, 0)
 
     RHO_T = np.float32(-THERM_EXP * PRESS_SCALE / LEVELS / 2)
     RHO_S = np.float32(HALINE_CON * PRESS_SCALE / LEVELS / 2)
@@ -438,10 +440,6 @@
         def _():
             pack_and_send(NCH - 1)
 
-        @pl.when(c == 2)
-        def _():
-            pack_wide()
-
         wait_recv_all(edge_copies(c))
 
         @pl.when(c == 0)

time: 60.8 us -> 62.3 us (1.025)
  Pallas kernels: 60.1 us -> 61.5 us
    pallas_call x1, Pallas kernels: 39.3 us -> 40.7 us  [local_step(): momentum(vel_x, vel_y, pot_temp, salinity, surf_eta, trans_x, trans_y, co...]
where the time goes in v9:
time: 62.3 us; the launch traced here: 62.2 us
  Pallas kernels  61.5 us (99%)
  between operations  0.64 us (1%)
    pallas_call x1, Pallas kernels, local_step(): momentum(vel_x, vel_y, pot_temp, salinity, surf_eta, trans_x, trans_y, co...  40.7 us
    pallas_call x1, Pallas kernels, local_step(): tracers(vel_x, vel_y, pot_temp, salinity, star_x, star_y, eta, tx, ty, co...  20.8 us

profile of v9, /device:TPU:0, one launch (start us, length us, event | category | flops | bytes accessed | tf_op | source)
XLA Modules:
  0.0 62.2 jit_solution(1240374812705492194)
XLA Ops:
  0.6 40.7 %momentum.1 = (f32[20,2,128,256]{3,2,1,0:T(8,128)}, f32[20,2,128,256]{3,2,1,0:T(8,128)}, f32[2,128,256]{2,1,0:T(8,128)}, f32[2,128,256]{2,1,0:T(8,128)}, f32[2,1...) custom-call(f32[20,2,128,256]{3,2,1,0:T(8,128)} %u_hbm.3, ...), custom_call_target="tpu_custom_call" | custom-call | tf_op jit(solution)/shard_map/momentum/pallas_call | solution.py:953
  41.4 20.8 %tracers.1 = (f32[2,128,256]{2,1,0:T(8,128)}, f32[2,128,256]{2,1,0:T(8,128)}, f32[2,128,256]{2,1,0:T(8,128)}, f32[20,2,128,256]{3,2,1,0:T(8,128)}, f32[20,2,128,...) custom-call(f32[20,2,128,256]{3,2,1,0:T(8,128)} %u_hbm.3, f32[20,2,128,256]{3,2,1,0:T(8,128)} %v_hbm.3, ...), custom_call_target="tpu_custom_call" | custom-call | tf_op jit(solution)/shard_map/tracers/pallas_call | solution.py:955

commit v10 on v9

--- a/solution.py
+++ b/solution.py
@@ -342,7 +342,6 @@
         for copy in flow_loads():
             copy.wait()
         pack_pairs(xb, (0, 2, 4, 6), (1, 3, 5, 7), sp)
-        start_all(flow_copies())
 
     def pack_rest(c, carry):
         pack_and_send(c)
@@ -439,6 +438,7 @@
         @pl.when(c == 1)
         def _():
             pack_and_send(NCH - 1)
+            start_all(flow_copies())
 
         wait_recv_all(edge_copies(c))
 

time: 62.3 us -> 60.7 us (0.974)
  Pallas kernels: 61.5 us -> 59.9 us
    pallas_call x1, Pallas kernels: 40.7 us -> 39.1 us  [local_step(): momentum(vel_x, vel_y, pot_temp, salinity, surf_eta, trans_x, trans_y, co...]
where the time goes in v10:
time: 60.7 us; the launch traced here: 60.6 us
  Pallas kernels  59.9 us (99%)
  between operations  0.64 us (1%)
    pallas_call x1, Pallas kernels, local_step(): momentum(vel_x, vel_y, pot_temp, salinity, surf_eta, trans_x, trans_y, co...  39.1 us
    pallas_call x1, Pallas kernels, local_step(): tracers(vel_x, vel_y, pot_temp, salinity, star_x, star_y, eta, tx, ty, co...  20.8 us

profile of v10, /device:TPU:0, one launch (start us, length us, event | category | flops | bytes accessed | tf_op | source)
XLA Modules:
  0.0 60.6 jit_solution(9265129857903780943)
XLA Ops:
  0.6 39.1 %momentum.1 = (f32[20,2,128,256]{3,2,1,0:T(8,128)}, f32[20,2,128,256]{3,2,1,0:T(8,128)}, f32[2,128,256]{2,1,0:T(8,128)}, f32[2,128,256]{2,1,0:T(8,128)}, f32[2,1...) custom-call(f32[20,2,128,256]{3,2,1,0:T(8,128)} %u_hbm.3, ...), custom_call_target="tpu_custom_call" | custom-call | tf_op jit(solution)/shard_map/momentum/pallas_call | solution.py:953
  39.8 20.8 %tracers.1 = (f32[2,128,256]{2,1,0:T(8,128)}, f32[2,128,256]{2,1,0:T(8,128)}, f32[2,128,256]{2,1,0:T(8,128)}, f32[20,2,128,256]{3,2,1,0:T(8,128)}, f32[20,2,128,...) custom-call(f32[20,2,128,256]{3,2,1,0:T(8,128)} %u_hbm.3, f32[20,2,128,256]{3,2,1,0:T(8,128)} %v_hbm.3, ...), custom_call_target="tpu_custom_call" | custom-call | tf_op jit(solution)/shard_map/tracers/pallas_call | solution.py:955
